TPU v7x, 1024 devices: a whole 4x8x16 slice. The times are simulated.
1024 devices in a mesh: gx: 8 (over x, core), gy: 16 (over z), gz: 8 (over y).
Axes of the slice: x: 4, y: 8, z: 16, core: 2. Of those that a mesh axis runs over, the one named last changes fastest.
Arguments:
- density: float32 [64, 256, 1024], P('gx', 'gy', 'gz'), may hold values from 0.1 to 10
- x_faces: float32 [2, 256, 1024], P(None, 'gy', 'gz'), may hold values from -6 to 6
- y_faces: float32 [2, 64, 1024], P(None, 'gx', 'gz'), may hold values from -6 to 6
- z_faces: float32 [2, 64, 256], P(None, 'gx', 'gy'), may hold values from -6 to 6
Outputs:
- solution_field: float32 [64, 256, 1024], P('gx', 'gy', 'gz')
- residual: float32 [64, 256, 1024], P('gx', 'gy', 'gz')
All inputs are finite; a program needn't handle non-finite values.
Results may differ from a plain program's by a relative error of at most 0.0003.
Values sent between devices are 32-bit elements; how exact they have to be, the bound alone decides.
No kernel may reach another device: no remote copies, remote signals or barrier semaphores. Data moves between devices by JAX's collectives and lax.ppermute only.
A program may use at most 32 MiB of HBM per device.

v0:
```python
import functools

import jax
import jax.numpy as jnp
from jax import lax
from jax.sharding import Mesh
from jax.sharding import PartitionSpec as P

ITERS = 2
LEVELS = 3
COARSE_SWEEPS = 3
GX_GY_GZ = ("gx_0", "gx_1", "gy", "gz")
GX = ("gx_0", "gx_1")


relax_rate = 1.0 / 9.0
coupling = 0.5


def extended_2(x, sides, width):
    edges = {}
    for axis, dim in sides:
        size, length = (lax.axis_size(axis), x.shape[dim])
        up = [(i, (i + 1) % size) for i in range(size - 1)]
        last = lax.slice_in_dim(x, length - width, length, axis=dim)
        first = lax.slice_in_dim(x, 0, width, axis=dim)
        edges[dim] = (
            lax.ppermute(last, axis, up),
            lax.ppermute(first, axis, [(b, a) for a, b in up]),
        )
    done = []
    for _, dim in sides:
        low, high = edges[dim]
        around = [(width, width) if d in done else (0, 0) for d in range(x.ndim)]
        x = jnp.concatenate([jnp.pad(low, around), x, jnp.pad(high, around)], axis=dim)
        done.append(dim)
    return x


def padded_2(cells, sides, width):
    for axis, dim in sides:
        count = lax.axis_size(axis)
        ends = count - 1
        head = lax.slice_in_dim(cells, 0, width, axis=dim)
        tail = lax.slice_in_dim(cells, cells.shape[dim] - width, cells.shape[dim], axis=dim)
        cells = jnp.concatenate(
            [
                lax.ppermute(tail, axis, [(i, (i + 1) % count) for i in range(ends)]),
                cells,
                lax.ppermute(head, axis, [((i + 1) % count, i) for i in range(ends)]),
            ],
            axis=dim,
        )
    return cells


def by_axis(x, axes):
    return functools.reduce(lax.psum, axes, x)


def beside_sum(padded):
    beside = padded[2:, 1:-1, 1:-1] + padded[:-2, 1:-1, 1:-1]
    beside = beside + padded[1:-1, 2:, 1:-1] + padded[1:-1, :-2, 1:-1]
    beside = beside + padded[1:-1, 1:-1, 2:] + padded[1:-1, 1:-1, :-2]
    return beside


def operate(field):
    padded = extended_2(field, ((GX, 0), ("gy", 1), ("gz", 2)), 1)
    return 6.0 * field - beside_sum(padded)


def restrict(field):
    sx, sy, sz = field.shape
    return 0.5 * jnp.sum(field.reshape(sx // 2, 2, sy // 2, 2, sz // 2, 2), axis=(1, 3, 5))


def prolong(field):
    sx, sy, sz = field.shape
    spread = jnp.broadcast_to(field[:, None, :, None, :, None], (sx, 2, sy, 2, sz, 2))
    return spread.reshape(2 * sx, 2 * sy, 2 * sz)


def inside(cells, block_index, block_count, depth):
    position = block_index * cells - depth + jnp.arange(cells + 2 * depth, dtype=jnp.int32)
    valid = (position >= 0) & (position < cells * block_count)
    return valid.astype(jnp.float32)


def cover_mask(shape, depth):
    sx, sy, sz = shape
    cover_x = inside(sx, lax.axis_index(GX), lax.axis_size(GX), depth)
    cover_y = inside(sy, lax.axis_index("gy"), lax.axis_size("gy"), depth)
    cover_z = inside(sz, lax.axis_index("gz"), lax.axis_size("gz"), depth)
    return cover_x[:, None, None] * cover_y[None, :, None] * cover_z[None, None, :]


def coarse_solve(right_side):
    reach = COARSE_SWEEPS - 1
    extended = padded_2(right_side, ((GX, 0), ("gy", 1), ("gz", 2)), reach)
    approx_ext = relax_rate * extended
    for sweep_idx in range(reach):
        depth = reach - sweep_idx - 1
        center = approx_ext[1:-1, 1:-1, 1:-1]
        source = extended[
            sweep_idx + 1 : extended.shape[0] - sweep_idx - 1,
            sweep_idx + 1 : extended.shape[1] - sweep_idx - 1,
            sweep_idx + 1 : extended.shape[2] - sweep_idx - 1,
        ]
        approx_ext = center + relax_rate * (source - (6.0 * center - beside_sum(approx_ext)))
        if depth > 0:
            approx_ext = approx_ext * cover_mask(right_side.shape, depth)
    return approx_ext


def cycle(right_side, level_idx):
    if level_idx == LEVELS - 1:
        return coarse_solve(right_side)
    approx = relax_rate * right_side
    defect = right_side - operate(approx)
    approx = approx + prolong(cycle(restrict(defect), level_idx + 1))
    return approx + relax_rate * (right_side - operate(approx))


def precondition_image(residual):
    approx = relax_rate * residual
    defect = residual - operate(approx)
    approx = approx + prolong(cycle(restrict(defect), 1))
    precond = approx + relax_rate * (residual - operate(approx))
    return (precond, operate(precond))


def joint_sums(residual, precond, precond_image):
    return (
        by_axis(jnp.sum(residual * precond), GX_GY_GZ),
        by_axis(jnp.sum(precond * precond_image), GX_GY_GZ),
    )


def local(density, x_faces, y_faces, z_faces):
    right_side = -coupling * density
    right_side = right_side.at[0].add(jnp.where(lax.axis_index(GX) == 0, x_faces[0], 0.0))
    right_side = right_side.at[-1].add(
        jnp.where(lax.axis_index(GX) == lax.axis_size(GX) - 1, x_faces[1], 0.0)
    )
    right_side = right_side.at[:, 0].add(jnp.where(lax.axis_index("gy") == 0, y_faces[0], 0.0))
    right_side = right_side.at[:, -1].add(
        jnp.where(lax.axis_index("gy") == lax.axis_size("gy") - 1, y_faces[1], 0.0)
    )
    right_side = right_side.at[:, :, 0].add(jnp.where(lax.axis_index("gz") == 0, z_faces[0], 0.0))
    right_side = right_side.at[:, :, -1].add(
        jnp.where(lax.axis_index("gz") == lax.axis_size("gz") - 1, z_faces[1], 0.0)
    )
    solution_field = jnp.zeros_like(right_side)
    residual = right_side
    precond, pimage = precondition_image(residual)
    gamma_now, delta_now = joint_sums(residual, precond, pimage)
    step_size = gamma_now / delta_now
    direction = precond
    image = pimage
    for iteration in range(ITERS):
        solution_field = solution_field + step_size * direction
        residual = residual - step_size * image
        if iteration + 1 < ITERS:
            precond, pimage = precondition_image(residual)
            gamma_next, delta_now = joint_sums(residual, precond, pimage)
            growth = gamma_next / gamma_now
            step_size = gamma_next / (delta_now - growth * gamma_next / step_size)
            direction = precond + growth * direction
            image = pimage + growth * image
            gamma_now = gamma_next
    return (solution_field, residual)


def solution(mesh):
    torus = Mesh(
        mesh.devices.reshape(4, 2, mesh.shape["gy"], mesh.shape["gz"]), ("gx_0", "gx_1", "gy", "gz")
    )
    in_specs = (P(GX, "gy", "gz"), P(None, "gy", "gz"), P(None, GX, "gz"), P(None, GX, "gy"))
    out_specs = (P(GX, "gy", "gz"), P(GX, "gy", "gz"))
    return jax.shard_map(local, mesh=torus, in_specs=in_specs, out_specs=out_specs, check_vma=False)
```

profile of v0, /device:TPU:64, one launch (start us, length us, event | category | flops | bytes accessed | tf_op | source)
XLA Modules:
  0.0 448.0 jit_solution(9917282230100738439)
XLA Ops:
  5.6 4.3 collective-permute-start.3
  9.9 11.2 %collective-permute-start.2 = (f32[8,1,128]{2,1,0:T(1,128)S(1)}, f32[8,1,128]{2,1,0:T(1,128)S(1)}, u32[]{:S(2)}, u32[]{:S(2)}) collective-permute-start(f32[8,1,128]{2,1,0:T(1,128)S(1)} %get-tuple-element.141), channel_id=1, source_target_pairs={{8,0},{16,8},{24,16},{32,24},{40,32},{48,40},{56,48},{64,56},{72,6... | collective-permute-start | bytes 12296 | tf_op jit(solution)/shard_map/ppermute | solution.py:29
  25.1 4.5 %collective-permute-start.5 = (f32[8,16,1]{2,1,0:T(8,128)S(1)}, f32[8,16,1]{2,1,0:T(8,128)S(1)}, u32[]{:S(2)}, u32[]{:S(2)}) collective-permute-start(f32[8,16,1]{2,1,0:T(8,128)S(1)} %get-tuple-element.137), channel_id=1, source_target_pairs={{0,1},{1,2},{2,3},{3,4},{4,5},{5,6},{6,7},{8,9},{9,10},{10,11},{11... | collective-permute-start | bytes 1544 | tf_op jit(solution)/shard_map/ppermute | solution.py:28
  32.1 5.5 %reshape.296 = f32[4,2,8,2,64,2]{5,4,3,2,1,0:T(8,128)} reshape(f32[8,16,128]{2,1,0:T(8,128)S(1)} %fusion.50) | data formatting | bytes 131072 | tf_op jit(solution)/shard_map/reshape | solution.py:75
  37.7 2.5 reduce_sum.72
  40.3 1.9 collective-permute-start.9
  42.2 3.9 collective-permute-start.8
  50.1 5.0 %collective-permute-start.11 = (f32[4,8,1]{2,1,0:T(8,128)S(1)}, f32[4,8,1]{2,1,0:T(8,128)S(1)}, u32[]{:S(2)}, u32[]{:S(2)}) collective-permute-start(f32[4,8,1]{2,1,0:T(8,128)S(1)} %get-tuple-element.165), channel_id=1, source_target_pairs={{0,1},{1,2},{2,3},{3,4},{4,5},{5,6},{6,7},{8,9},{9,10},{10,11},{11... | collective-permute-start | bytes 392 | tf_op jit(solution)/shard_map/ppermute | solution.py:28
  58.7 3.0 collective-permute-start.12
  62.5 2.2 collective-permute-start.14
  64.7 3.6 collective-permute-start.15
  68.5 1.8 collective-permute-done.15
  70.4 4.2 collective-permute-start.16
  76.1 4.3 collective-permute-done.17
  81.1 4.2 collective-permute-start.21
  85.3 1.9 collective-permute-start.20
  87.2 2.1 collective-permute-start.19
  92.1 5.4 %collective-permute-start.23 = (f32[4,8,1]{2,1,0:T(8,128)S(1)}, f32[4,8,1]{2,1,0:T(8,128)S(1)}, u32[]{:S(2)}, u32[]{:S(2)}) collective-permute-start(f32[4,8,1]{2,1,0:T(8,128)S(1)} %get-tuple-element.159), channel_id=1, source_target_pairs={{0,1},{1,2},{2,3},{3,4},{4,5},{5,6},{6,7},{8,9},{9,10},{10,11},{11... | collective-permute-start | bytes 392 | tf_op jit(solution)/shard_map/ppermute | solution.py:28
  99.0 2.6 broadcast_in_dim.27
  101.6 4.0 reshape.299
  105.6 5.2 %collective-permute-start.27 = (f32[8,1,128]{2,1,0:T(1,128)S(1)}, f32[8,1,128]{2,1,0:T(1,128)S(1)}, u32[]{:S(2)}, u32[]{:S(2)}) collective-permute-start(f32[8,1,128]{2,1,0:T(1,128)S(1)} %get-tuple-element.134), channel_id=1, source_target_pairs={{0,8},{8,16},{16,24},{24,32},{32,40},{40,48},{48,56},{56,64},{64,7... | collective-permute-start | bytes 12296 | tf_op jit(solution)/shard_map/ppermute | solution.py:28
  110.8 1.9 collective-permute-start.26
  112.7 6.2 %collective-permute-start.25 = (f32[1,16,128]{2,1,0:T(8,128)S(1)}, f32[1,16,128]{2,1,0:T(8,128)S(1)}, u32[]{:S(2)}, u32[]{:S(2)}) collective-permute-start(f32[1,16,128]{2,1,0:T(8,128)S(1)} %get-tuple-element.132), channel_id=1, source_target_pairs={{0,128},{128,256},{256,384},{384,512},{512,640},{640,768},{768,896... | collective-permute-start | bytes 24584 | tf_op jit(solution)/shard_map/ppermute | solution.py:28
  121.6 6.0 %collective-permute-start.29 = (f32[8,16,1]{2,1,0:T(8,128)S(1)}, f32[8,16,1]{2,1,0:T(8,128)S(1)}, u32[]{:S(2)}, u32[]{:S(2)}) collective-permute-start(f32[8,16,1]{2,1,0:T(8,128)S(1)} %get-tuple-element.131), channel_id=1, source_target_pairs={{0,1},{1,2},{2,3},{3,4},{4,5},{5,6},{6,7},{8,9},{9,10},{10,11},{11... | collective-permute-start | bytes 1544 | tf_op jit(solution)/shard_map/ppermute | solution.py:28
  129.8 3.9 collective-permute-start.33
  133.7 1.9 collective-permute-start.32
  135.6 4.3 collective-permute-start.31
  142.6 5.8 %collective-permute-start.35 = (f32[8,16,1]{2,1,0:T(8,128)S(1)}, f32[8,16,1]{2,1,0:T(8,128)S(1)}, u32[]{:S(2)}, u32[]{:S(2)}) collective-permute-start(f32[8,16,1]{2,1,0:T(8,128)S(1)} %get-tuple-element.125), channel_id=1, source_target_pairs={{0,1},{1,2},{2,3},{3,4},{4,5},{5,6},{6,7},{8,9},{9,10},{10,11},{11... | collective-permute-start | bytes 1544 | tf_op jit(solution)/shard_map/ppermute | solution.py:28
  151.0 14.7 %all-reduce.45 = (f32[]{:T(128)}, f32[]{:T(128)}) all-reduce(f32[]{:T(128)} %get-tuple-element.81, f32[]{:T(128)} %get-tuple-element.80), channel_id=1, replica_groups=mesh['gx_0'=4,'gx_1'=2,'gy'=16,'gz'=8] {'gx_0'}, use_global_device_ids=true, to_apply=%region_3.4 | all-reduce | flops 2 | bytes 16 | tf_op jit(solution)/shard_map/psum | solution.py:58
  165.7 3.1 all-reduce.47
  168.8 38.1 %all-reduce.41 = (f32[]{:T(128)}, f32[]{:T(128)}) all-reduce(f32[]{:T(128)} %get-tuple-element.96, f32[]{:T(128)} %get-tuple-element.97), channel_id=1, replica_groups=mesh['gx_0'=4,'gx_1'=2,'gy'=16,'gz'=8] {'gy'}, use_global_device_ids=true, to_apply=%region_5.6 | all-reduce | flops 2 | bytes 16 | tf_op jit(solution)/shard_map/psum | solution.py:58
  206.9 24.2 %all-reduce.43 = (f32[]{:T(128)}, f32[]{:T(128)}) all-reduce(f32[]{:T(128)} %get-tuple-element.84, f32[]{:T(128)} %get-tuple-element.85), channel_id=1, replica_groups=mesh['gx_0'=4,'gx_1'=2,'gy'=16,'gz'=8] {'gz'}, use_global_device_ids=true, to_apply=%region_6.7 | all-reduce | flops 2 | bytes 16 | tf_op jit(solution)/shard_map/psum | solution.py:58
  232.5 1.9 collective-permute-start.39
  234.4 3.9 collective-permute-start.38
  242.3 4.5 %collective-permute-start.41 = (f32[8,16,1]{2,1,0:T(8,128)S(1)}, f32[8,16,1]{2,1,0:T(8,128)S(1)}, u32[]{:S(2)}, u32[]{:S(2)}) collective-permute-start(f32[8,16,1]{2,1,0:T(8,128)S(1)} %get-tuple-element.119), channel_id=1, source_target_pairs={{0,1},{1,2},{2,3},{3,4},{4,5},{5,6},{6,7},{8,9},{9,10},{10,11},{11... | collective-permute-start | bytes 1544 | tf_op jit(solution)/shard_map/ppermute | solution.py:28
  249.4 5.5 %reshape.300 = f32[4,2,8,2,64,2]{5,4,3,2,1,0:T(8,128)} reshape(f32[8,16,128]{2,1,0:T(8,128)S(1)} %fusion.22) | data formatting | bytes 131072 | tf_op jit(solution)/shard_map/reshape | solution.py:75
  254.9 2.5 reduce_sum.76
  257.5 1.9 collective-permute-start.45
  259.4 3.9 collective-permute-start.44
  267.4 5.0 %collective-permute-start.47 = (f32[4,8,1]{2,1,0:T(8,128)S(1)}, f32[4,8,1]{2,1,0:T(8,128)S(1)}, u32[]{:S(2)}, u32[]{:S(2)}) collective-permute-start(f32[4,8,1]{2,1,0:T(8,128)S(1)} %get-tuple-element.153), channel_id=1, source_target_pairs={{0,1},{1,2},{2,3},{3,4},{4,5},{5,6},{6,7},{8,9},{9,10},{10,11},{11... | collective-permute-start | bytes 392 | tf_op jit(solution)/shard_map/ppermute | solution.py:28
  275.9 5.0 %collective-permute-start.48 = (f32[2,4,32]{2,1,0:T(4,128)S(1)}, f32[2,4,32]{2,1,0:T(4,128)S(1)}, u32[]{:S(2)}, u32[]{:S(2)}) collective-permute-start(f32[2,4,32]{2,1,0:T(4,128)S(1)} %broadcast_multiply_fusion.7), channel_id=1, source_target_pairs={{0,128},{128,256},{256,384},{384,512},{512,640},{640,768},{768,896... | collective-permute-start | bytes 3080 | tf_op jit(solution)/shard_map/ppermute | solution.py:48
  281.8 1.9 collective-permute-start.50
  283.7 3.9 collective-permute-start.51
  287.6 1.6 collective-permute-done.51
  289.3 3.9 collective-permute-start.52
  294.7 4.2 collective-permute-done.53
  299.7 3.7 collective-permute-start.57
  303.4 2.1 collective-permute-start.56
  305.5 2.0 collective-permute-start.55
  310.2 4.5 %collective-permute-start.59 = (f32[4,8,1]{2,1,0:T(8,128)S(1)}, f32[4,8,1]{2,1,0:T(8,128)S(1)}, u32[]{:S(2)}, u32[]{:S(2)}) collective-permute-start(f32[4,8,1]{2,1,0:T(8,128)S(1)} %get-tuple-element.147), channel_id=1, source_target_pairs={{0,1},{1,2},{2,3},{3,4},{4,5},{5,6},{6,7},{8,9},{9,10},{10,11},{11... | collective-permute-start | bytes 392 | tf_op jit(solution)/shard_map/ppermute | solution.py:28
  316.2 2.6 broadcast_in_dim.51
  318.8 4.0 reshape.303
  322.9 4.9 %collective-permute-start.63 = (f32[8,1,128]{2,1,0:T(1,128)S(1)}, f32[8,1,128]{2,1,0:T(1,128)S(1)}, u32[]{:S(2)}, u32[]{:S(2)}) collective-permute-start(f32[8,1,128]{2,1,0:T(1,128)S(1)} %get-tuple-element.116), channel_id=1, source_target_pairs={{0,8},{8,16},{16,24},{24,32},{32,40},{40,48},{48,56},{56,64},{64,7... | collective-permute-start | bytes 12296 | tf_op jit(solution)/shard_map/ppermute | solution.py:28
  327.7 1.9 collective-permute-start.62
  329.7 6.5 %collective-permute-start.61 = (f32[1,16,128]{2,1,0:T(8,128)S(1)}, f32[1,16,128]{2,1,0:T(8,128)S(1)}, u32[]{:S(2)}, u32[]{:S(2)}) collective-permute-start(f32[1,16,128]{2,1,0:T(8,128)S(1)} %get-tuple-element.114), channel_id=1, source_target_pairs={{0,128},{128,256},{256,384},{384,512},{512,640},{640,768},{768,896... | collective-permute-start | bytes 24584 | tf_op jit(solution)/shard_map/ppermute | solution.py:28
  338.9 5.4 %collective-permute-start.65 = (f32[8,16,1]{2,1,0:T(8,128)S(1)}, f32[8,16,1]{2,1,0:T(8,128)S(1)}, u32[]{:S(2)}, u32[]{:S(2)}) collective-permute-start(f32[8,16,1]{2,1,0:T(8,128)S(1)} %get-tuple-element.113), channel_id=1, source_target_pairs={{0,1},{1,2},{2,3},{3,4},{4,5},{5,6},{6,7},{8,9},{9,10},{10,11},{11... | collective-permute-start | bytes 1544 | tf_op jit(solution)/shard_map/ppermute | solution.py:28
  346.4 3.9 collective-permute-start.69
  350.3 1.9 collective-permute-start.68
  352.2 4.3 collective-permute-start.67
  359.2 5.8 %collective-permute-start.71 = (f32[8,16,1]{2,1,0:T(8,128)S(1)}, f32[8,16,1]{2,1,0:T(8,128)S(1)}, u32[]{:S(2)}, u32[]{:S(2)}) collective-permute-start(f32[8,16,1]{2,1,0:T(8,128)S(1)} %get-tuple-element.107), channel_id=1, source_target_pairs={{0,1},{1,2},{2,3},{3,4},{4,5},{5,6},{6,7},{8,9},{9,10},{10,11},{11... | collective-permute-start | bytes 1544 | tf_op jit(solution)/shard_map/ppermute | solution.py:28
  367.7 13.6 %all-reduce.44 = (f32[]{:T(128)}, f32[]{:T(128)}) all-reduce(f32[]{:T(128)} %get-tuple-element.79, f32[]{:T(128)} %get-tuple-element.78), channel_id=1, replica_groups=mesh['gx_0'=4,'gx_1'=2,'gy'=16,'gz'=8] {'gx_0'}, use_global_device_ids=true, to_apply=%region_15.16 | all-reduce | flops 2 | bytes 16 | tf_op jit(solution)/shard_map/psum | solution.py:58
  381.3 3.2 all-reduce.46
  384.5 33.9 %all-reduce.40 = (f32[]{:T(128)}, f32[]{:T(128)}) all-reduce(f32[]{:T(128)} %get-tuple-element.94, f32[]{:T(128)} %get-tuple-element.95), channel_id=1, replica_groups=mesh['gx_0'=4,'gx_1'=2,'gy'=16,'gz'=8] {'gy'}, use_global_device_ids=true, to_apply=%region_17.18 | all-reduce | flops 2 | bytes 16 | tf_op jit(solution)/shard_map/psum | solution.py:58
  418.4 24.2 %all-reduce.42 = (f32[]{:T(128)}, f32[]{:T(128)}) all-reduce(f32[]{:T(128)} %get-tuple-element.82, f32[]{:T(128)} %get-tuple-element.83), channel_id=1, replica_groups=mesh['gx_0'=4,'gx_1'=2,'gy'=16,'gz'=8] {'gz'}, use_global_device_ids=true, to_apply=%region_18.19 | all-reduce | flops 2 | bytes 16 | tf_op jit(solution)/shard_map/psum | solution.py:58
  (208 shorter events, 67.9 us)
Async XLA Ops:
  5.6 19.5 %collective-permute-start.3 = (f32[8,1,128]{2,1,0:T(1,128)S(1)}, f32[8,1,128]{2,1,0:T(1,128)S(1)}, u32[]{:S(2)}, u32[]{:S(2)}) collective-permute-start(f32[8,1,128]{2,1,0:T(1,128)S(1)} %get-tuple-element.140), channel_id=1, source_target_pairs={{0,8},{8,16},{16,24},{24,32},{32,40},{40,48},{48,56},{56,64},{64,7... | collective-permute-start | bytes 12296 | tf_op jit(solution)/shard_map/ppermute | solution.py:28
  9.9 19.8 %collective-permute-start.2 = (f32[8,1,128]{2,1,0:T(1,128)S(1)}, f32[8,1,128]{2,1,0:T(1,128)S(1)}, u32[]{:S(2)}, u32[]{:S(2)}) collective-permute-start(f32[8,1,128]{2,1,0:T(1,128)S(1)} %get-tuple-element.141), channel_id=1, source_target_pairs={{8,0},{16,8},{24,16},{32,24},{40,32},{48,40},{56,48},{64,56},{72,6... | collective-permute-start | bytes 12296 | tf_op jit(solution)/shard_map/ppermute | solution.py:29
  21.1 10.9 %collective-permute-start.1 = (f32[1,16,128]{2,1,0:T(8,128)S(1)}, f32[1,16,128]{2,1,0:T(8,128)S(1)}, u32[]{:S(2)}, u32[]{:S(2)}) collective-permute-start(f32[1,16,128]{2,1,0:T(8,128)S(1)} %get-tuple-element.138), channel_id=1, source_target_pairs={{0,128},{128,256},{256,384},{384,512},{512,640},{640,768},{768,896... | collective-permute-start | bytes 24584 | tf_op jit(solution)/shard_map/ppermute | solution.py:28
  22.4 9.6 %collective-permute-start = (f32[1,16,128]{2,1,0:T(8,128)S(1)}, f32[1,16,128]{2,1,0:T(8,128)S(1)}, u32[]{:S(2)}, u32[]{:S(2)}) collective-permute-start(f32[1,16,128]{2,1,0:T(8,128)S(1)} %get-tuple-element.139), channel_id=1, source_target_pairs={{128,0},{256,128},{384,256},{512,384},{640,512},{768,640},{896,768... | collective-permute-start | bytes 24584 | tf_op jit(solution)/shard_map/ppermute | solution.py:29
  23.8 6.7 %collective-permute-start.4 = (f32[8,16,1]{2,1,0:T(8,128)S(1)}, f32[8,16,1]{2,1,0:T(8,128)S(1)}, u32[]{:S(2)}, u32[]{:S(2)}) collective-permute-start(f32[8,16,1]{2,1,0:T(8,128)S(1)} %get-tuple-element.136), channel_id=1, source_target_pairs={{1,0},{2,1},{3,2},{4,3},{5,4},{6,5},{7,6},{9,8},{10,9},{11,10},{12... | collective-permute-start | bytes 1544 | tf_op jit(solution)/shard_map/ppermute | solution.py:29
  25.1 6.9 %collective-permute-start.5 = (f32[8,16,1]{2,1,0:T(8,128)S(1)}, f32[8,16,1]{2,1,0:T(8,128)S(1)}, u32[]{:S(2)}, u32[]{:S(2)}) collective-permute-start(f32[8,16,1]{2,1,0:T(8,128)S(1)} %get-tuple-element.137), channel_id=1, source_target_pairs={{0,1},{1,2},{2,3},{3,4},{4,5},{5,6},{6,7},{8,9},{9,10},{10,11},{11... | collective-permute-start | bytes 1544 | tf_op jit(solution)/shard_map/ppermute | solution.py:28
  40.3 9.9 %collective-permute-start.9 = (f32[4,1,64]{2,1,0:T(1,128)S(1)}, f32[4,1,64]{2,1,0:T(1,128)S(1)}, u32[]{:S(2)}, u32[]{:S(2)}) collective-permute-start(f32[4,1,64]{2,1,0:T(1,128)S(1)} %get-tuple-element.168), channel_id=1, source_target_pairs={{0,8},{8,16},{16,24},{24,32},{32,40},{40,48},{48,56},{56,64},{64,7... | collective-permute-start | bytes 3080 | tf_op jit(solution)/shard_map/ppermute | solution.py:28
  42.2 13.0 %collective-permute-start.8 = (f32[4,1,64]{2,1,0:T(1,128)S(1)}, f32[4,1,64]{2,1,0:T(1,128)S(1)}, u32[]{:S(2)}, u32[]{:S(2)}) collective-permute-start(f32[4,1,64]{2,1,0:T(1,128)S(1)} %get-tuple-element.169), channel_id=1, source_target_pairs={{8,0},{16,8},{24,16},{32,24},{40,32},{48,40},{56,48},{64,56},{72,6... | collective-permute-start | bytes 3080 | tf_op jit(solution)/shard_map/ppermute | solution.py:29
  46.1 10.5 %collective-permute-start.7 = (f32[1,8,64]{2,1,0:T(8,128)S(1)}, f32[1,8,64]{2,1,0:T(8,128)S(1)}, u32[]{:S(2)}, u32[]{:S(2)}) collective-permute-start(f32[1,8,64]{2,1,0:T(8,128)S(1)} %get-tuple-element.166), channel_id=1, source_target_pairs={{0,128},{128,256},{256,384},{384,512},{512,640},{640,768},{768,896... | collective-permute-start | bytes 6152 | tf_op jit(solution)/shard_map/ppermute | solution.py:28
  47.5 9.1 %collective-permute-start.6 = (f32[1,8,64]{2,1,0:T(8,128)S(1)}, f32[1,8,64]{2,1,0:T(8,128)S(1)}, u32[]{:S(2)}, u32[]{:S(2)}) collective-permute-start(f32[1,8,64]{2,1,0:T(8,128)S(1)} %get-tuple-element.167), channel_id=1, source_target_pairs={{128,0},{256,128},{384,256},{512,384},{640,512},{768,640},{896,768... | collective-permute-start | bytes 6152 | tf_op jit(solution)/shard_map/ppermute | solution.py:29
  48.8 6.4 %collective-permute-start.10 = (f32[4,8,1]{2,1,0:T(8,128)S(1)}, f32[4,8,1]{2,1,0:T(8,128)S(1)}, u32[]{:S(2)}, u32[]{:S(2)}) collective-permute-start(f32[4,8,1]{2,1,0:T(8,128)S(1)} %get-tuple-element.164), channel_id=1, source_target_pairs={{1,0},{2,1},{3,2},{4,3},{5,4},{6,5},{7,6},{9,8},{10,9},{11,10},{12... | collective-permute-start | bytes 392 | tf_op jit(solution)/shard_map/ppermute | solution.py:29
  50.1 6.4 %collective-permute-start.11 = (f32[4,8,1]{2,1,0:T(8,128)S(1)}, f32[4,8,1]{2,1,0:T(8,128)S(1)}, u32[]{:S(2)}, u32[]{:S(2)}) collective-permute-start(f32[4,8,1]{2,1,0:T(8,128)S(1)} %get-tuple-element.165), channel_id=1, source_target_pairs={{0,1},{1,2},{2,3},{3,4},{4,5},{5,6},{6,7},{8,9},{9,10},{10,11},{11... | collective-permute-start | bytes 392 | tf_op jit(solution)/shard_map/ppermute | solution.py:28
  62.5 5.9 %collective-permute-start.14 = (f32[6,2,32]{2,1,0:T(2,128)S(1)}, f32[6,2,32]{2,1,0:T(2,128)S(1)}, u32[]{:S(2)}, u32[]{:S(2)}) collective-permute-start(f32[6,2,32]{2,1,0:T(2,128)S(1)} %get-tuple-element.172), channel_id=1, source_target_pairs={{0,8},{8,16},{16,24},{24,32},{32,40},{40,48},{48,56},{56,64},{64,7... | collective-permute-start | bytes 4616 | tf_op jit(solution)/shard_map/ppermute | solution.py:48
  81.1 10.9 %collective-permute-start.21 = (f32[4,1,64]{2,1,0:T(1,128)S(1)}, f32[4,1,64]{2,1,0:T(1,128)S(1)}, u32[]{:S(2)}, u32[]{:S(2)}) collective-permute-start(f32[4,1,64]{2,1,0:T(1,128)S(1)} %get-tuple-element.162), channel_id=1, source_target_pairs={{0,8},{8,16},{16,24},{24,32},{32,40},{40,48},{48,56},{56,64},{64,7... | collective-permute-start | bytes 3080 | tf_op jit(solution)/shard_map/ppermute | solution.py:28
  85.3 12.2 %collective-permute-start.20 = (f32[4,1,64]{2,1,0:T(1,128)S(1)}, f32[4,1,64]{2,1,0:T(1,128)S(1)}, u32[]{:S(2)}, u32[]{:S(2)}) collective-permute-start(f32[4,1,64]{2,1,0:T(1,128)S(1)} %get-tuple-element.163), channel_id=1, source_target_pairs={{8,0},{16,8},{24,16},{32,24},{40,32},{48,40},{56,48},{64,56},{72,6... | collective-permute-start | bytes 3080 | tf_op jit(solution)/shard_map/ppermute | solution.py:29
  87.2 11.6 %collective-permute-start.19 = (f32[1,8,64]{2,1,0:T(8,128)S(1)}, f32[1,8,64]{2,1,0:T(8,128)S(1)}, u32[]{:S(2)}, u32[]{:S(2)}) collective-permute-start(f32[1,8,64]{2,1,0:T(8,128)S(1)} %get-tuple-element.160), channel_id=1, source_target_pairs={{0,128},{128,256},{256,384},{384,512},{512,640},{640,768},{768,896... | collective-permute-start | bytes 6152 | tf_op jit(solution)/shard_map/ppermute | solution.py:28
  89.4 9.5 %collective-permute-start.18 = (f32[1,8,64]{2,1,0:T(8,128)S(1)}, f32[1,8,64]{2,1,0:T(8,128)S(1)}, u32[]{:S(2)}, u32[]{:S(2)}) collective-permute-start(f32[1,8,64]{2,1,0:T(8,128)S(1)} %get-tuple-element.161), channel_id=1, source_target_pairs={{128,0},{256,128},{384,256},{512,384},{640,512},{768,640},{896,768... | collective-permute-start | bytes 6152 | tf_op jit(solution)/shard_map/ppermute | solution.py:29
  90.8 6.7 %collective-permute-start.22 = (f32[4,8,1]{2,1,0:T(8,128)S(1)}, f32[4,8,1]{2,1,0:T(8,128)S(1)}, u32[]{:S(2)}, u32[]{:S(2)}) collective-permute-start(f32[4,8,1]{2,1,0:T(8,128)S(1)} %get-tuple-element.158), channel_id=1, source_target_pairs={{1,0},{2,1},{3,2},{4,3},{5,4},{6,5},{7,6},{9,8},{10,9},{11,10},{12... | collective-permute-start | bytes 392 | tf_op jit(solution)/shard_map/ppermute | solution.py:29
  92.1 6.8 %collective-permute-start.23 = (f32[4,8,1]{2,1,0:T(8,128)S(1)}, f32[4,8,1]{2,1,0:T(8,128)S(1)}, u32[]{:S(2)}, u32[]{:S(2)}) collective-permute-start(f32[4,8,1]{2,1,0:T(8,128)S(1)} %get-tuple-element.159), channel_id=1, source_target_pairs={{0,1},{1,2},{2,3},{3,4},{4,5},{5,6},{6,7},{8,9},{9,10},{10,11},{11... | collective-permute-start | bytes 392 | tf_op jit(solution)/shard_map/ppermute | solution.py:28
  105.6 16.0 %collective-permute-start.27 = (f32[8,1,128]{2,1,0:T(1,128)S(1)}, f32[8,1,128]{2,1,0:T(1,128)S(1)}, u32[]{:S(2)}, u32[]{:S(2)}) collective-permute-start(f32[8,1,128]{2,1,0:T(1,128)S(1)} %get-tuple-element.134), channel_id=1, source_target_pairs={{0,8},{8,16},{16,24},{24,32},{32,40},{40,48},{48,56},{56,64},{64,7... | collective-permute-start | bytes 12296 | tf_op jit(solution)/shard_map/ppermute | solution.py:28
  110.8 16.9 %collective-permute-start.26 = (f32[8,1,128]{2,1,0:T(1,128)S(1)}, f32[8,1,128]{2,1,0:T(1,128)S(1)}, u32[]{:S(2)}, u32[]{:S(2)}) collective-permute-start(f32[8,1,128]{2,1,0:T(1,128)S(1)} %get-tuple-element.135), channel_id=1, source_target_pairs={{8,0},{16,8},{24,16},{32,24},{40,32},{48,40},{56,48},{64,56},{72,6... | collective-permute-start | bytes 12296 | tf_op jit(solution)/shard_map/ppermute | solution.py:29
  112.7 16.9 %collective-permute-start.25 = (f32[1,16,128]{2,1,0:T(8,128)S(1)}, f32[1,16,128]{2,1,0:T(8,128)S(1)}, u32[]{:S(2)}, u32[]{:S(2)}) collective-permute-start(f32[1,16,128]{2,1,0:T(8,128)S(1)} %get-tuple-element.132), channel_id=1, source_target_pairs={{0,128},{128,256},{256,384},{384,512},{512,640},{640,768},{768,896... | collective-permute-start | bytes 24584 | tf_op jit(solution)/shard_map/ppermute | solution.py:28
  119.0 10.6 %collective-permute-start.24 = (f32[1,16,128]{2,1,0:T(8,128)S(1)}, f32[1,16,128]{2,1,0:T(8,128)S(1)}, u32[]{:S(2)}, u32[]{:S(2)}) collective-permute-start(f32[1,16,128]{2,1,0:T(8,128)S(1)} %get-tuple-element.133), channel_id=1, source_target_pairs={{128,0},{256,128},{384,256},{512,384},{640,512},{768,640},{896,768... | collective-permute-start | bytes 24584 | tf_op jit(solution)/shard_map/ppermute | solution.py:29
  120.3 7.6 %collective-permute-start.28 = (f32[8,16,1]{2,1,0:T(8,128)S(1)}, f32[8,16,1]{2,1,0:T(8,128)S(1)}, u32[]{:S(2)}, u32[]{:S(2)}) collective-permute-start(f32[8,16,1]{2,1,0:T(8,128)S(1)} %get-tuple-element.130), channel_id=1, source_target_pairs={{1,0},{2,1},{3,2},{4,3},{5,4},{6,5},{7,6},{9,8},{10,9},{11,10},{12... | collective-permute-start | bytes 1544 | tf_op jit(solution)/shard_map/ppermute | solution.py:29
  121.6 7.9 %collective-permute-start.29 = (f32[8,16,1]{2,1,0:T(8,128)S(1)}, f32[8,16,1]{2,1,0:T(8,128)S(1)}, u32[]{:S(2)}, u32[]{:S(2)}) collective-permute-start(f32[8,16,1]{2,1,0:T(8,128)S(1)} %get-tuple-element.131), channel_id=1, source_target_pairs={{0,1},{1,2},{2,3},{3,4},{4,5},{5,6},{6,7},{8,9},{9,10},{10,11},{11... | collective-permute-start | bytes 1544 | tf_op jit(solution)/shard_map/ppermute | solution.py:28
  129.8 12.8 %collective-permute-start.33 = (f32[8,1,128]{2,1,0:T(1,128)S(1)}, f32[8,1,128]{2,1,0:T(1,128)S(1)}, u32[]{:S(2)}, u32[]{:S(2)}) collective-permute-start(f32[8,1,128]{2,1,0:T(1,128)S(1)} %get-tuple-element.126), channel_id=1, source_target_pairs={{0,8},{8,16},{16,24},{24,32},{32,40},{40,48},{48,56},{56,64},{64,7... | collective-permute-start | bytes 12296 | tf_op jit(solution)/shard_map/ppermute | solution.py:28
  133.7 14.7 %collective-permute-start.32 = (f32[8,1,128]{2,1,0:T(1,128)S(1)}, f32[8,1,128]{2,1,0:T(1,128)S(1)}, u32[]{:S(2)}, u32[]{:S(2)}) collective-permute-start(f32[8,1,128]{2,1,0:T(1,128)S(1)} %get-tuple-element.127), channel_id=1, source_target_pairs={{8,0},{16,8},{24,16},{32,24},{40,32},{48,40},{56,48},{64,56},{72,6... | collective-permute-start | bytes 12296 | tf_op jit(solution)/shard_map/ppermute | solution.py:29
  135.6 14.6 %collective-permute-start.31 = (f32[1,16,128]{2,1,0:T(8,128)S(1)}, f32[1,16,128]{2,1,0:T(8,128)S(1)}, u32[]{:S(2)}, u32[]{:S(2)}) collective-permute-start(f32[1,16,128]{2,1,0:T(8,128)S(1)} %get-tuple-element.128), channel_id=1, source_target_pairs={{0,128},{128,256},{256,384},{384,512},{512,640},{640,768},{768,896... | collective-permute-start | bytes 24584 | tf_op jit(solution)/shard_map/ppermute | solution.py:28
  139.9 10.3 %collective-permute-start.30 = (f32[1,16,128]{2,1,0:T(8,128)S(1)}, f32[1,16,128]{2,1,0:T(8,128)S(1)}, u32[]{:S(2)}, u32[]{:S(2)}) collective-permute-start(f32[1,16,128]{2,1,0:T(8,128)S(1)} %get-tuple-element.129), channel_id=1, source_target_pairs={{128,0},{256,128},{384,256},{512,384},{640,512},{768,640},{896,768... | collective-permute-start | bytes 24584 | tf_op jit(solution)/shard_map/ppermute | solution.py:29
  141.3 7.4 %collective-permute-start.34 = (f32[8,16,1]{2,1,0:T(8,128)S(1)}, f32[8,16,1]{2,1,0:T(8,128)S(1)}, u32[]{:S(2)}, u32[]{:S(2)}) collective-permute-start(f32[8,16,1]{2,1,0:T(8,128)S(1)} %get-tuple-element.124), channel_id=1, source_target_pairs={{1,0},{2,1},{3,2},{4,3},{5,4},{6,5},{7,6},{9,8},{10,9},{11,10},{12... | collective-permute-start | bytes 1544 | tf_op jit(solution)/shard_map/ppermute | solution.py:29
  142.6 7.7 %collective-permute-start.35 = (f32[8,16,1]{2,1,0:T(8,128)S(1)}, f32[8,16,1]{2,1,0:T(8,128)S(1)}, u32[]{:S(2)}, u32[]{:S(2)}) collective-permute-start(f32[8,16,1]{2,1,0:T(8,128)S(1)} %get-tuple-element.125), channel_id=1, source_target_pairs={{0,1},{1,2},{2,3},{3,4},{4,5},{5,6},{6,7},{8,9},{9,10},{10,11},{11... | collective-permute-start | bytes 1544 | tf_op jit(solution)/shard_map/ppermute | solution.py:28
  232.5 9.8 %collective-permute-start.39 = (f32[8,1,128]{2,1,0:T(1,128)S(1)}, f32[8,1,128]{2,1,0:T(1,128)S(1)}, u32[]{:S(2)}, u32[]{:S(2)}) collective-permute-start(f32[8,1,128]{2,1,0:T(1,128)S(1)} %get-tuple-element.122), channel_id=1, source_target_pairs={{0,8},{8,16},{16,24},{24,32},{32,40},{40,48},{48,56},{56,64},{64,7... | collective-permute-start | bytes 12296 | tf_op jit(solution)/shard_map/ppermute | solution.py:28
  234.4 12.5 %collective-permute-start.38 = (f32[8,1,128]{2,1,0:T(1,128)S(1)}, f32[8,1,128]{2,1,0:T(1,128)S(1)}, u32[]{:S(2)}, u32[]{:S(2)}) collective-permute-start(f32[8,1,128]{2,1,0:T(1,128)S(1)} %get-tuple-element.123), channel_id=1, source_target_pairs={{8,0},{16,8},{24,16},{32,24},{40,32},{48,40},{56,48},{64,56},{72,6... | collective-permute-start | bytes 12296 | tf_op jit(solution)/shard_map/ppermute | solution.py:29
  238.3 10.9 %collective-permute-start.37 = (f32[1,16,128]{2,1,0:T(8,128)S(1)}, f32[1,16,128]{2,1,0:T(8,128)S(1)}, u32[]{:S(2)}, u32[]{:S(2)}) collective-permute-start(f32[1,16,128]{2,1,0:T(8,128)S(1)} %get-tuple-element.120), channel_id=1, source_target_pairs={{0,128},{128,256},{256,384},{384,512},{512,640},{640,768},{768,896... | collective-permute-start | bytes 24584 | tf_op jit(solution)/shard_map/ppermute | solution.py:28
  239.6 9.6 %collective-permute-start.36 = (f32[1,16,128]{2,1,0:T(8,128)S(1)}, f32[1,16,128]{2,1,0:T(8,128)S(1)}, u32[]{:S(2)}, u32[]{:S(2)}) collective-permute-start(f32[1,16,128]{2,1,0:T(8,128)S(1)} %get-tuple-element.121), channel_id=1, source_target_pairs={{128,0},{256,128},{384,256},{512,384},{640,512},{768,640},{896,768... | collective-permute-start | bytes 24584 | tf_op jit(solution)/shard_map/ppermute | solution.py:29
  241.0 6.7 %collective-permute-start.40 = (f32[8,16,1]{2,1,0:T(8,128)S(1)}, f32[8,16,1]{2,1,0:T(8,128)S(1)}, u32[]{:S(2)}, u32[]{:S(2)}) collective-permute-start(f32[8,16,1]{2,1,0:T(8,128)S(1)} %get-tuple-element.118), channel_id=1, source_target_pairs={{1,0},{2,1},{3,2},{4,3},{5,4},{6,5},{7,6},{9,8},{10,9},{11,10},{12... | collective-permute-start | bytes 1544 | tf_op jit(solution)/shard_map/ppermute | solution.py:29
  242.3 6.9 %collective-permute-start.41 = (f32[8,16,1]{2,1,0:T(8,128)S(1)}, f32[8,16,1]{2,1,0:T(8,128)S(1)}, u32[]{:S(2)}, u32[]{:S(2)}) collective-permute-start(f32[8,16,1]{2,1,0:T(8,128)S(1)} %get-tuple-element.119), channel_id=1, source_target_pairs={{0,1},{1,2},{2,3},{3,4},{4,5},{5,6},{6,7},{8,9},{9,10},{10,11},{11... | collective-permute-start | bytes 1544 | tf_op jit(solution)/shard_map/ppermute | solution.py:28
  257.5 9.9 %collective-permute-start.45 = (f32[4,1,64]{2,1,0:T(1,128)S(1)}, f32[4,1,64]{2,1,0:T(1,128)S(1)}, u32[]{:S(2)}, u32[]{:S(2)}) collective-permute-start(f32[4,1,64]{2,1,0:T(1,128)S(1)} %get-tuple-element.156), channel_id=1, source_target_pairs={{0,8},{8,16},{16,24},{24,32},{32,40},{40,48},{48,56},{56,64},{64,7... | collective-permute-start | bytes 3080 | tf_op jit(solution)/shard_map/ppermute | solution.py:28
  259.4 13.0 %collective-permute-start.44 = (f32[4,1,64]{2,1,0:T(1,128)S(1)}, f32[4,1,64]{2,1,0:T(1,128)S(1)}, u32[]{:S(2)}, u32[]{:S(2)}) collective-permute-start(f32[4,1,64]{2,1,0:T(1,128)S(1)} %get-tuple-element.157), channel_id=1, source_target_pairs={{8,0},{16,8},{24,16},{32,24},{40,32},{48,40},{56,48},{64,56},{72,6... | collective-permute-start | bytes 3080 | tf_op jit(solution)/shard_map/ppermute | solution.py:29
  263.4 10.5 %collective-permute-start.43 = (f32[1,8,64]{2,1,0:T(8,128)S(1)}, f32[1,8,64]{2,1,0:T(8,128)S(1)}, u32[]{:S(2)}, u32[]{:S(2)}) collective-permute-start(f32[1,8,64]{2,1,0:T(8,128)S(1)} %get-tuple-element.154), channel_id=1, source_target_pairs={{0,128},{128,256},{256,384},{384,512},{512,640},{640,768},{768,896... | collective-permute-start | bytes 6152 | tf_op jit(solution)/shard_map/ppermute | solution.py:28
  264.7 9.1 %collective-permute-start.42 = (f32[1,8,64]{2,1,0:T(8,128)S(1)}, f32[1,8,64]{2,1,0:T(8,128)S(1)}, u32[]{:S(2)}, u32[]{:S(2)}) collective-permute-start(f32[1,8,64]{2,1,0:T(8,128)S(1)} %get-tuple-element.155), channel_id=1, source_target_pairs={{128,0},{256,128},{384,256},{512,384},{640,512},{768,640},{896,768... | collective-permute-start | bytes 6152 | tf_op jit(solution)/shard_map/ppermute | solution.py:29
  266.1 6.4 %collective-permute-start.46 = (f32[4,8,1]{2,1,0:T(8,128)S(1)}, f32[4,8,1]{2,1,0:T(8,128)S(1)}, u32[]{:S(2)}, u32[]{:S(2)}) collective-permute-start(f32[4,8,1]{2,1,0:T(8,128)S(1)} %get-tuple-element.152), channel_id=1, source_target_pairs={{1,0},{2,1},{3,2},{4,3},{5,4},{6,5},{7,6},{9,8},{10,9},{11,10},{12... | collective-permute-start | bytes 392 | tf_op jit(solution)/shard_map/ppermute | solution.py:29
  267.4 6.4 %collective-permute-start.47 = (f32[4,8,1]{2,1,0:T(8,128)S(1)}, f32[4,8,1]{2,1,0:T(8,128)S(1)}, u32[]{:S(2)}, u32[]{:S(2)}) collective-permute-start(f32[4,8,1]{2,1,0:T(8,128)S(1)} %get-tuple-element.153), channel_id=1, source_target_pairs={{0,1},{1,2},{2,3},{3,4},{4,5},{5,6},{6,7},{8,9},{9,10},{10,11},{11... | collective-permute-start | bytes 392 | tf_op jit(solution)/shard_map/ppermute | solution.py:28
  274.6 6.3 %collective-permute-start.49 = (f32[2,4,32]{2,1,0:T(4,128)S(1)}, f32[2,4,32]{2,1,0:T(4,128)S(1)}, u32[]{:S(2)}, u32[]{:S(2)}) collective-permute-start(f32[2,4,32]{2,1,0:T(4,128)S(1)} %broadcast_multiply_fusion.7), channel_id=1, source_target_pairs={{128,0},{256,128},{384,256},{512,384},{640,512},{768,640},{896,768... | collective-permute-start | bytes 3080 | tf_op jit(solution)/shard_map/ppermute | solution.py:50
  275.9 5.8 %collective-permute-start.48 = (f32[2,4,32]{2,1,0:T(4,128)S(1)}, f32[2,4,32]{2,1,0:T(4,128)S(1)}, u32[]{:S(2)}, u32[]{:S(2)}) collective-permute-start(f32[2,4,32]{2,1,0:T(4,128)S(1)} %broadcast_multiply_fusion.7), channel_id=1, source_target_pairs={{0,128},{128,256},{256,384},{384,512},{512,640},{640,768},{768,896... | collective-permute-start | bytes 3080 | tf_op jit(solution)/shard_map/ppermute | solution.py:48
  281.8 5.9 %collective-permute-start.50 = (f32[6,2,32]{2,1,0:T(2,128)S(1)}, f32[6,2,32]{2,1,0:T(2,128)S(1)}, u32[]{:S(2)}, u32[]{:S(2)}) collective-permute-start(f32[6,2,32]{2,1,0:T(2,128)S(1)} %get-tuple-element.170), channel_id=1, source_target_pairs={{0,8},{8,16},{16,24},{24,32},{32,40},{40,48},{48,56},{56,64},{64,7... | collective-permute-start | bytes 4616 | tf_op jit(solution)/shard_map/ppermute | solution.py:48
  299.7 10.5 %collective-permute-start.57 = (f32[4,1,64]{2,1,0:T(1,128)S(1)}, f32[4,1,64]{2,1,0:T(1,128)S(1)}, u32[]{:S(2)}, u32[]{:S(2)}) collective-permute-start(f32[4,1,64]{2,1,0:T(1,128)S(1)} %get-tuple-element.150), channel_id=1, source_target_pairs={{0,8},{8,16},{16,24},{24,32},{32,40},{40,48},{48,56},{56,64},{64,7... | collective-permute-start | bytes 3080 | tf_op jit(solution)/shard_map/ppermute | solution.py:28
  303.4 11.3 %collective-permute-start.56 = (f32[4,1,64]{2,1,0:T(1,128)S(1)}, f32[4,1,64]{2,1,0:T(1,128)S(1)}, u32[]{:S(2)}, u32[]{:S(2)}) collective-permute-start(f32[4,1,64]{2,1,0:T(1,128)S(1)} %get-tuple-element.151), channel_id=1, source_target_pairs={{8,0},{16,8},{24,16},{32,24},{40,32},{48,40},{56,48},{64,56},{72,6... | collective-permute-start | bytes 3080 | tf_op jit(solution)/shard_map/ppermute | solution.py:29
  305.5 10.6 %collective-permute-start.55 = (f32[1,8,64]{2,1,0:T(8,128)S(1)}, f32[1,8,64]{2,1,0:T(8,128)S(1)}, u32[]{:S(2)}, u32[]{:S(2)}) collective-permute-start(f32[1,8,64]{2,1,0:T(8,128)S(1)} %get-tuple-element.148), channel_id=1, source_target_pairs={{0,128},{128,256},{256,384},{384,512},{512,640},{640,768},{768,896... | collective-permute-start | bytes 6152 | tf_op jit(solution)/shard_map/ppermute | solution.py:28
  307.5 8.7 %collective-permute-start.54 = (f32[1,8,64]{2,1,0:T(8,128)S(1)}, f32[1,8,64]{2,1,0:T(8,128)S(1)}, u32[]{:S(2)}, u32[]{:S(2)}) collective-permute-start(f32[1,8,64]{2,1,0:T(8,128)S(1)} %get-tuple-element.149), channel_id=1, source_target_pairs={{128,0},{256,128},{384,256},{512,384},{640,512},{768,640},{896,768... | collective-permute-start | bytes 6152 | tf_op jit(solution)/shard_map/ppermute | solution.py:29
  308.9 5.9 %collective-permute-start.58 = (f32[4,8,1]{2,1,0:T(8,128)S(1)}, f32[4,8,1]{2,1,0:T(8,128)S(1)}, u32[]{:S(2)}, u32[]{:S(2)}) collective-permute-start(f32[4,8,1]{2,1,0:T(8,128)S(1)} %get-tuple-element.146), channel_id=1, source_target_pairs={{1,0},{2,1},{3,2},{4,3},{5,4},{6,5},{7,6},{9,8},{10,9},{11,10},{12... | collective-permute-start | bytes 392 | tf_op jit(solution)/shard_map/ppermute | solution.py:29
  310.2 6.0 %collective-permute-start.59 = (f32[4,8,1]{2,1,0:T(8,128)S(1)}, f32[4,8,1]{2,1,0:T(8,128)S(1)}, u32[]{:S(2)}, u32[]{:S(2)}) collective-permute-start(f32[4,8,1]{2,1,0:T(8,128)S(1)} %get-tuple-element.147), channel_id=1, source_target_pairs={{0,1},{1,2},{2,3},{3,4},{4,5},{5,6},{6,7},{8,9},{9,10},{10,11},{11... | collective-permute-start | bytes 392 | tf_op jit(solution)/shard_map/ppermute | solution.py:28
  322.9 16.0 %collective-permute-start.63 = (f32[8,1,128]{2,1,0:T(1,128)S(1)}, f32[8,1,128]{2,1,0:T(1,128)S(1)}, u32[]{:S(2)}, u32[]{:S(2)}) collective-permute-start(f32[8,1,128]{2,1,0:T(1,128)S(1)} %get-tuple-element.116), channel_id=1, source_target_pairs={{0,8},{8,16},{16,24},{24,32},{32,40},{40,48},{48,56},{56,64},{64,7... | collective-permute-start | bytes 12296 | tf_op jit(solution)/shard_map/ppermute | solution.py:28
  327.7 16.6 %collective-permute-start.62 = (f32[8,1,128]{2,1,0:T(1,128)S(1)}, f32[8,1,128]{2,1,0:T(1,128)S(1)}, u32[]{:S(2)}, u32[]{:S(2)}) collective-permute-start(f32[8,1,128]{2,1,0:T(1,128)S(1)} %get-tuple-element.117), channel_id=1, source_target_pairs={{8,0},{16,8},{24,16},{32,24},{40,32},{48,40},{56,48},{64,56},{72,6... | collective-permute-start | bytes 12296 | tf_op jit(solution)/shard_map/ppermute | solution.py:29
  329.7 16.5 %collective-permute-start.61 = (f32[1,16,128]{2,1,0:T(8,128)S(1)}, f32[1,16,128]{2,1,0:T(8,128)S(1)}, u32[]{:S(2)}, u32[]{:S(2)}) collective-permute-start(f32[1,16,128]{2,1,0:T(8,128)S(1)} %get-tuple-element.114), channel_id=1, source_target_pairs={{0,128},{128,256},{256,384},{384,512},{512,640},{640,768},{768,896... | collective-permute-start | bytes 24584 | tf_op jit(solution)/shard_map/ppermute | solution.py:28
  336.2 10.0 %collective-permute-start.60 = (f32[1,16,128]{2,1,0:T(8,128)S(1)}, f32[1,16,128]{2,1,0:T(8,128)S(1)}, u32[]{:S(2)}, u32[]{:S(2)}) collective-permute-start(f32[1,16,128]{2,1,0:T(8,128)S(1)} %get-tuple-element.115), channel_id=1, source_target_pairs={{128,0},{256,128},{384,256},{512,384},{640,512},{768,640},{896,768... | collective-permute-start | bytes 24584 | tf_op jit(solution)/shard_map/ppermute | solution.py:29
  337.6 7.0 %collective-permute-start.64 = (f32[8,16,1]{2,1,0:T(8,128)S(1)}, f32[8,16,1]{2,1,0:T(8,128)S(1)}, u32[]{:S(2)}, u32[]{:S(2)}) collective-permute-start(f32[8,16,1]{2,1,0:T(8,128)S(1)} %get-tuple-element.112), channel_id=1, source_target_pairs={{1,0},{2,1},{3,2},{4,3},{5,4},{6,5},{7,6},{9,8},{10,9},{11,10},{12... | collective-permute-start | bytes 1544 | tf_op jit(solution)/shard_map/ppermute | solution.py:29
  338.9 7.3 %collective-permute-start.65 = (f32[8,16,1]{2,1,0:T(8,128)S(1)}, f32[8,16,1]{2,1,0:T(8,128)S(1)}, u32[]{:S(2)}, u32[]{:S(2)}) collective-permute-start(f32[8,16,1]{2,1,0:T(8,128)S(1)} %get-tuple-element.113), channel_id=1, source_target_pairs={{0,1},{1,2},{2,3},{3,4},{4,5},{5,6},{6,7},{8,9},{9,10},{10,11},{11... | collective-permute-start | bytes 1544 | tf_op jit(solution)/shard_map/ppermute | solution.py:28
  346.4 12.8 %collective-permute-start.69 = (f32[8,1,128]{2,1,0:T(1,128)S(1)}, f32[8,1,128]{2,1,0:T(1,128)S(1)}, u32[]{:S(2)}, u32[]{:S(2)}) collective-permute-start(f32[8,1,128]{2,1,0:T(1,128)S(1)} %get-tuple-element.108), channel_id=1, source_target_pairs={{0,8},{8,16},{16,24},{24,32},{32,40},{40,48},{48,56},{56,64},{64,7... | collective-permute-start | bytes 12296 | tf_op jit(solution)/shard_map/ppermute | solution.py:28
  350.3 14.7 %collective-permute-start.68 = (f32[8,1,128]{2,1,0:T(1,128)S(1)}, f32[8,1,128]{2,1,0:T(1,128)S(1)}, u32[]{:S(2)}, u32[]{:S(2)}) collective-permute-start(f32[8,1,128]{2,1,0:T(1,128)S(1)} %get-tuple-element.109), channel_id=1, source_target_pairs={{8,0},{16,8},{24,16},{32,24},{40,32},{48,40},{56,48},{64,56},{72,6... | collective-permute-start | bytes 12296 | tf_op jit(solution)/shard_map/ppermute | solution.py:29
  352.2 14.6 %collective-permute-start.67 = (f32[1,16,128]{2,1,0:T(8,128)S(1)}, f32[1,16,128]{2,1,0:T(8,128)S(1)}, u32[]{:S(2)}, u32[]{:S(2)}) collective-permute-start(f32[1,16,128]{2,1,0:T(8,128)S(1)} %get-tuple-element.110), channel_id=1, source_target_pairs={{0,128},{128,256},{256,384},{384,512},{512,640},{640,768},{768,896... | collective-permute-start | bytes 24584 | tf_op jit(solution)/shard_map/ppermute | solution.py:28
  356.5 10.3 %collective-permute-start.66 = (f32[1,16,128]{2,1,0:T(8,128)S(1)}, f32[1,16,128]{2,1,0:T(8,128)S(1)}, u32[]{:S(2)}, u32[]{:S(2)}) collective-permute-start(f32[1,16,128]{2,1,0:T(8,128)S(1)} %get-tuple-element.111), channel_id=1, source_target_pairs={{128,0},{256,128},{384,256},{512,384},{640,512},{768,640},{896,768... | collective-permute-start | bytes 24584 | tf_op jit(solution)/shard_map/ppermute | solution.py:29
  357.9 7.4 %collective-permute-start.70 = (f32[8,16,1]{2,1,0:T(8,128)S(1)}, f32[8,16,1]{2,1,0:T(8,128)S(1)}, u32[]{:S(2)}, u32[]{:S(2)}) collective-permute-start(f32[8,16,1]{2,1,0:T(8,128)S(1)} %get-tuple-element.106), channel_id=1, source_target_pairs={{1,0},{2,1},{3,2},{4,3},{5,4},{6,5},{7,6},{9,8},{10,9},{11,10},{12... | collective-permute-start | bytes 1544 | tf_op jit(solution)/shard_map/ppermute | solution.py:29
  359.2 7.7 %collective-permute-start.71 = (f32[8,16,1]{2,1,0:T(8,128)S(1)}, f32[8,16,1]{2,1,0:T(8,128)S(1)}, u32[]{:S(2)}, u32[]{:S(2)}) collective-permute-start(f32[8,16,1]{2,1,0:T(8,128)S(1)} %get-tuple-element.107), channel_id=1, source_target_pairs={{0,1},{1,2},{2,3},{3,4},{4,5},{5,6},{6,7},{8,9},{9,10},{10,11},{11... | collective-permute-start | bytes 1544 | tf_op jit(solution)/shard_map/ppermute | solution.py:28
  (8 other events, 41.9 us)
where the time goes:
time: 451 us; the launch traced here: 448 us
  starting transfers between devices  212 us (47%)
  blocking collectives  155 us (34%)
  waiting for transfers between devices  31.3 us (7%)
  local copies, waits for them, and re-layouts  28.4 us (6%)
  other arithmetic  13 us (3%)
  between operations  8.09 us (2%)
    psum x8, blocking collectives, by_axis(): return functools.reduce(lax.psum, axes, x)  155 us
    ppermute x30, starting transfers between devices, extended_2(): lax.ppermute(last, axis, up)  118 us
    ppermute x30, starting transfers between devices, extended_2(): lax.ppermute(first, axis, [(b, a) for a, b in up])  60.4 us
    ppermute x6, starting transfers between devices, padded_2(): lax.ppermute(tail, axis, [(i, (i + 1) % count) for i in range(ends)])  20.3 us
    ppermute x30, waiting for transfers between devices, extended_2(): lax.ppermute(last, axis, up)  14.9 us
    ppermute x6, starting transfers between devices, padded_2(): lax.ppermute(head, axis, [((i + 1) % count, i) for i in range(ends)])  12.9 us
    reshape x4, local copies, waits for them, and re-layouts, restrict(): field.reshape(sx // 2, 2, sy // 2, 2, sz // 2, 2)  12.2 us
    ppermute x6, waiting for transfers between devices, padded_2(): lax.ppermute(head, axis, [((i + 1) % count, i) for i in range(ends)])  11.9 us
  transfers between devices with their start and end apart: 72, of which 23 were waited for; matrix products, arithmetic and copies ran while one was open for 0% of the time, Pallas kernels for 0%

commit v1 on v0

v1 whole, which is shorter than its diff:
```python
import functools

import jax
import jax.numpy as jnp
from jax import lax
from jax.experimental import pallas as pl
from jax.experimental.pallas import tpu as pltpu
from jax.sharding import Mesh
from jax.sharding import PartitionSpec as P

AXES = ("gx_0", "gx_1", "gy", "gz")
GX = ("gx_0", "gx_1")
NX, NY, NZ = 64, 256, 1024
BX, BY, BZ = 8, 16, 128
CZ = 32
HY, HZ = 32, 32
ROWS, LANES = BY + 2 * HY, 128
relax = 1.0 / 9.0
coupling = 0.5
VMEM = pl.BlockSpec(memory_space=pltpu.VMEM)
SMEM = pl.BlockSpec(memory_space=pltpu.SMEM)


def roll(x, shift, axis):
    return pltpu.roll(x, shift % x.shape[axis], axis)


def lane_index(shape):
    return lax.broadcasted_iota(jnp.int32, shape, 1)


def row_index(shape):
    return lax.broadcasted_iota(jnp.int32, shape, 0)


def rhs_kernel(where_ref, density, xf, yf, zf, rhs, packed):
    gx, gy, gz = where_ref[0], where_ref[1], where_ref[2]
    rows, lanes = row_index((BY, BZ)), lane_index((BY, BZ))
    eye = row_index((BY, BY)) == lane_index((BY, BY))
    low_y = (rows == 0) & (gy == 0)
    high_y = (rows == BY - 1) & (gy == NY // BY - 1)
    low_z = (lanes == 0) & (gz == 0)
    high_z = (lanes == BZ - 1) & (gz == NZ // BZ - 1)

    def column(row):
        return jnp.sum(jnp.where(eye, row, 0.0), axis=1, keepdims=True)

    layers = []
    for x in range(BX):
        value = -coupling * density[x]
        if x == 0:
            value = value + jnp.where(gx == 0, xf[0], 0.0)
        if x == BX - 1:
            value = value + jnp.where(gx == NX // BX - 1, xf[1], 0.0)
        value = value + jnp.where(low_y, yf[0, x : x + 1, :], 0.0)
        value = value + jnp.where(high_y, yf[1, x : x + 1, :], 0.0)
        value = value + jnp.where(low_z, column(zf[0, x : x + 1, :]), 0.0)
        value = value + jnp.where(high_z, column(zf[1, x : x + 1, :]), 0.0)
        rhs[x] = value
        layers.append(value)
    for chunk in range(4):
        for quad in range(2):
            out = None
            for k in range(4):
                part = roll(layers[4 * quad + k], 32 * (k - chunk), 1)
                out = part if k == 0 else jnp.where(lanes >= 32 * k, part, out)
            packed[2 * chunk, quad] = out
            packed[2 * chunk + 1, quad] = out


def make_rhs(where, density, xf, yf, zf):
    return pl.pallas_call(
        rhs_kernel,
        out_shape=(
            jax.ShapeDtypeStruct((BX, BY, BZ), jnp.float32),
            jax.ShapeDtypeStruct((8, 2, BY, BZ), jnp.float32),
        ),
        in_specs=[SMEM, VMEM, VMEM, VMEM, VMEM],
        out_specs=(VMEM, VMEM),
    )(where, density, xf, yf, zf)


def join_kernel(where_ref, own, near, far, near2, far2, out):
    core = where_ref[3]
    out[:, 2 * BY : 3 * BY] = own[...]

    @pl.when(core == 0)
    def _():
        out[:, 0:BY] = far[...]
        out[:, BY : 2 * BY] = near[...]
        out[:, 3 * BY : 4 * BY] = near2[...]
        out[:, 4 * BY : 5 * BY] = far2[...]

    @pl.when(core == 1)
    def _():
        out[:, 0:BY] = far2[...]
        out[:, BY : 2 * BY] = near2[...]
        out[:, 3 * BY : 4 * BY] = near[...]
        out[:, 4 * BY : 5 * BY] = far[...]


def join(where, own, near, far, near2, far2):
    return pl.pallas_call(
        join_kernel,
        out_shape=jax.ShapeDtypeStruct((16, ROWS, 128), jnp.float32),
        in_specs=[SMEM] + [VMEM] * 5,
        out_specs=VMEM,
    )(where, own, near, far, near2, far2)


def around(x, step):
    return (roll(x, step, 0) + roll(x, -step, 0)) + (roll(x, step, 1) + roll(x, -step, 1))


def fold(x, step):
    rows, lanes = row_index(x.shape), lane_index(x.shape)
    x = x + jnp.where(rows & step == 0, roll(x, -step, 0), roll(x, step, 0))
    return x + jnp.where(lanes & step == 0, roll(x, -step, 1), roll(x, step, 1))


def third(x):
    return x * (1.0 / 3.0)


def cycle_in(src, mask, f1, f2, t2, e2, e1, lo, hi, lo2, hi2, n0, n1, n2):
    rows = slice(lo, hi)
    inner = slice(lo2, hi2)

    def down0(i, _):
        a, b = src[2 * i + 1, rows], src[2 * i + 2, rows]
        t = a + b
        s = third(t) + relax * ((t + src[2 * i, rows] + src[2 * i + 3, rows]) + around(t, 1))
        f1[i + 1, rows] = 0.5 * fold(s, 1) * mask[rows]
        return 0

    lax.fori_loop(0, NX // 2, down0, 0)

    def down1(i, _):
        t = f1[2 * i + 1, rows] + f1[2 * i + 2, rows]
        s = third(t) + relax * ((t + f1[2 * i, rows] + f1[2 * i + 3, rows]) + around(t, 2))
        f2[i + 1, rows] = 0.5 * fold(s, 2) * mask[rows]
        return 0

    lax.fori_loop(0, NX // 4, down1, 0)

    def sweep0(i, _):
        r = f2[i + 1, rows]
        s = (4.0 / 3.0) * r + relax * ((f2[i, rows] + f2[i + 2, rows]) + around(r, 4))
        t2[i + 1, rows] = relax * s * mask[rows]
        return 0

    lax.fori_loop(0, NX // 4, sweep0, 0)

    def sweep1(i, _):
        v = t2[i + 1, rows]
        s = third(v) + relax * (f2[i + 1, rows] + ((t2[i, rows] + t2[i + 2, rows]) + around(v, 4)))
        e2[i + 1, rows] = s * mask[rows]
        return 0

    lax.fori_loop(0, NX // 4, sweep1, 0)

    def up1(i, _):
        e = e2[i + 1, rows]
        before = relax * f1[2 * i, rows] + e2[i, rows]
        ra, rb = f1[2 * i + 1, rows], f1[2 * i + 2, rows]
        va, vb = relax * ra + e, relax * rb + e
        after = relax * f1[2 * i + 3, rows] + e2[i + 2, rows]
        m = mask[rows]
        e1[2 * i + 1, rows] = (third(va) + relax * (ra + ((before + vb) + around(va, 2)))) * m
        e1[2 * i + 2, rows] = (third(vb) + relax * (rb + ((va + after) + around(vb, 2)))) * m
        return 0

    lax.fori_loop(0, NX // 4, up1, 0)


def cycle_out(src, mask, e1, out, lo, hi):
    rows = slice(lo, hi)

    def up0(i, _):
        e = e1[i + 1, rows]
        before = relax * src[2 * i, rows] + e1[i, rows]
        ra, rb = src[2 * i + 1, rows], src[2 * i + 2, rows]
        va, vb = relax * ra + e, relax * rb + e
        after = relax * src[2 * i + 3, rows] + e1[i + 2, rows]
        m = mask[rows]
        out[2 * i + 1, rows] = (third(va) + relax * (ra + ((before + vb) + around(va, 1)))) * m
        out[2 * i + 2, rows] = (third(vb) + relax * (rb + ((va + after) + around(vb, 1)))) * m
        return 0

    lax.fori_loop(0, NX // 2, up0, 0)


def operate_on(src, i, rows):
    v = src[i + 1, rows]
    return 6.0 * v - ((src[i, rows] + src[i + 2, rows]) + around(v, 1))


def cycles_kernel(where_ref, own, got, swapped, out, r0, z0, q0, w, f1, f2, t2, e2, e1, mask):
    gx0, core, gy, gz = where_ref[4], where_ref[3], where_ref[1], where_ref[2]
    shape = (ROWS, LANES)
    rows, lanes = row_index(shape), lane_index(shape)
    y = gy * BY - HY + rows
    z = (gz * 4 + gx0) * CZ - HZ + lanes
    valid = (y >= 0) & (y < NY) & (z >= 0) & (z < NZ) & (lanes < CZ + 2 * HZ)
    mask[...] = jnp.where(valid, 1.0, 0.0)
    zero = jnp.zeros(shape, jnp.float32)
    for ref, count in ((r0, NX), (z0, NX), (q0, NX), (w, NX), (f1, NX // 2), (e1, NX // 2), (f2, NX // 4), (t2, NX // 4), (e2, NX // 4)):
        ref[0] = zero
        ref[count + 1] = zero

    def unpack(i, _):
        a, c, b = got[i], own[i], swapped[i]
        first = core == 0
        left, right = jnp.where(first, a, b), jnp.where(first, b, a)
        for k in range(4):
            value = jnp.where(lanes < 32, roll(left, -32 * k, 1), jnp.where(lanes < 64, roll(c, 32 - 32 * k, 1), roll(right, 64 - 32 * k, 1)))
            r0[4 * i + k + 1] = jnp.where(lanes < 96, value, 0.0)
        return 0

    lax.fori_loop(0, NX // 4, unpack, 0)
    cycle_in(r0, mask, f1, f2, t2, e2, e1, 0, 80, 8, 72, 0, 0, 0)
    cycle_out(r0, mask, e1, z0, 8, 72)

    mid = slice(16, 64)

    def image(i, _):
        q0[i + 1, mid] = operate_on(z0, i, mid) * mask[mid]
        return 0

    lax.fori_loop(0, NX, image, 0)
    cycle_in(q0, mask, f1, f2, t2, e2, e1, 16, 64, 24, 56, 0, 0, 0)
    cycle_out(q0, mask, e1, w, 24, 56)

    home = slice(HY, HY + BY)
    wide = slice(24, 56)
    hlanes = lane_index((BY, LANES))
    inside = (hlanes >= HZ) & (hlanes < HZ + CZ)

    def sums(i, acc):
        s = operate_on(w, i, wide)[8:24]
        r, zz, q, ww = r0[i + 1, home], z0[i + 1, home], q0[i + 1, home], w[i + 1, home]
        a0, a1, a2, a3, a4 = acc
        value = jnp.where(hlanes < 32, roll(zz, -32, 1), jnp.where(hlanes < 64, q, jnp.where(hlanes < 96, roll(ww, 32, 1), roll(s, 64, 1))))
        slab = i // BX

        @pl.when(slab % 2 == core)
        def _():
            out[slab // 2, pl.ds(pl.multiple_of((i % BX) * BY, BY), BY)] = value

        return a0 + r * zz, a1 + zz * q, a2 + r * ww, a3 + q * ww, a4 + ww * s

    init = jnp.zeros((BY, LANES), jnp.float32)
    acc = lax.fori_loop(0, NX, sums, (init,) * 5)
    out_rows, out_lanes = row_index((8, LANES)), lane_index((8, LANES))
    row = jnp.zeros((8, LANES), jnp.float32)
    for k, a in enumerate(acc):
        total = jnp.sum(jnp.where(inside, a, 0.0))
        row = jnp.where(out_lanes == k, total, row)
    for t in range(4):
        out[t, BX * BY : BX * BY + 8] = row


def cycles(where, own, got, swapped):
    def field(n):
        return pltpu.VMEM((n + 2, ROWS, LANES), jnp.float32)

    return pl.pallas_call(
        cycles_kernel,
        out_shape=jax.ShapeDtypeStruct((4, BX * BY + 8, LANES), jnp.float32),
        in_specs=[SMEM] + [VMEM] * 3,
        out_specs=VMEM,
        scratch_shapes=[field(NX)] * 4 + [field(NX // 2), field(NX // 4), field(NX // 4), field(NX // 4), field(NX // 2), pltpu.VMEM((ROWS, LANES), jnp.float32)],
        compiler_params=pltpu.CompilerParams(vmem_limit_bytes=48 * 1024 * 1024),
    )(where, own, got, swapped)


def finish_kernel(rhs, fields, sums, solution, residual):
    total = jnp.sum(sums[...], axis=0, keepdims=True)
    lanes = lane_index(total.shape)

    def pick(k):
        return jnp.sum(jnp.where(lanes == k, total, 0.0), axis=1, keepdims=True)

    rz, zq, rw, qw, ws = (pick(k) for k in range(5))
    step0 = rz / zq
    rz1 = rz - step0 * (rw + zq) + step0 * step0 * qw
    growth = rz1 / rz
    image1 = (zq - 2.0 * step0 * qw + step0 * step0 * ws) + 2.0 * growth * (zq - step0 * qw) + growth * growth * zq
    step1 = rz1 / image1
    on_z = step0 + step1 * (1.0 + growth)
    on_w = -step1 * step0
    wide = lane_index((BY, LANES))
    for x in range(BX):
        parts = [fields[c, x * BY : (x + 1) * BY] for c in range(4)]

        def field(f):
            value = None
            for c in range(4):
                part = roll(parts[c], 32 * (c - f), 1)
                value = part if c == 0 else jnp.where(wide >= 32 * c, part, value)
            return value

        z0, q0, w, s = (field(f) for f in range(4))
        solution[x] = on_z * z0 + on_w * w
        residual[x] = rhs[x] - (on_z * q0 + on_w * s)


def finish(rhs, fields, sums):
    shape = jax.ShapeDtypeStruct((BX, BY, BZ), jnp.float32)
    return pl.pallas_call(finish_kernel, out_shape=(shape, shape), in_specs=[VMEM] * 3, out_specs=(VMEM, VMEM))(rhs, fields, sums)


def both_ways(count, step):
    pairs = [(i, i + step) for i in range(count - step)]
    return pairs + [(count + b, count + a) for a, b in pairs]


def z_pairs():
    def number(core, block):
        return ((block % 4) * 2 + core) * 8 + block // 4

    up = [(i, i + 1) for i in range(31)]
    return [(number(0, a), number(0, b)) for a, b in up] + [(number(1, b), number(1, a)) for a, b in up]


SWAP = [(0, 1), (1, 0)]


def local(density, x_faces, y_faces, z_faces):
    where = jnp.stack([lax.axis_index(GX), lax.axis_index("gy"), lax.axis_index("gz"), lax.axis_index("gx_1"), lax.axis_index("gx_0")]).astype(jnp.int32)
    rhs, packed = make_rhs(where, density, x_faces, y_faces, z_faces)
    own = lax.all_to_all(packed, GX, 0, 0, tiled=True).reshape(16, BY, 128)
    near = lax.ppermute(own, ("gx_1", "gy"), both_ways(16, 1))
    far = lax.ppermute(own, ("gx_1", "gy"), both_ways(16, 2))
    near2 = lax.ppermute(near, "gx_1", SWAP)
    far2 = lax.ppermute(far, "gx_1", SWAP)
    joined = join(where, own, near, far, near2, far2)
    got = lax.ppermute(joined, ("gx_0", "gx_1", "gz"), z_pairs())
    swapped = lax.ppermute(got, "gx_1", SWAP)
    packed = cycles(where, joined, got, swapped)
    fields = lax.all_to_all(packed, "gx_0", 0, 0, tiled=True)
    sums = jnp.sum(fields[:, BX * BY, :], axis=0)
    sums = lax.all_to_all(jnp.broadcast_to(sums, (128, 1, 128)), ("gy", "gz"), 0, 0, tiled=True)
    return finish(rhs, fields, sums.reshape(128, 128))


def solution(mesh):
    torus = Mesh(mesh.devices.reshape(4, 2, mesh.shape["gy"], mesh.shape["gz"]), AXES)
    in_specs = (P(GX, "gy", "gz"), P(None, "gy", "gz"), P(None, GX, "gz"), P(None, GX, "gy"))
    out_specs = (P(GX, "gy", "gz"), P(GX, "gy", "gz"))
    return jax.shard_map(local, mesh=torus, in_specs=in_specs, out_specs=out_specs, check_vma=False)
```

time: 451 us -> 159 us (0.35)
  the two profiles are of different devices: /device:TPU:64 before, /device:TPU:8 now
where the time goes in v1:
time: 159 us; the launch traced here: 158 us
  blocking collectives  58.7 us (37%)
  Pallas kernels  57.4 us (36%)
  waiting for transfers between devices  20.2 us (13%)
  starting transfers between devices  18.7 us (12%)
  local copies, waits for them, and re-layouts  2.46 us (2%)
    pallas_call x1, Pallas kernels, cycles(): pl.pallas_call(cycles_kernel, out_shape=jax.ShapeDtypeStruct((4, BX * BY...  51.7 us
    all_to_all x1, blocking collectives, local(): lax.all_to_all(jnp.broadcast_to(sums, (128, 1, 128)), ('gy', 'gz'), 0, 0,...  38.6 us
    ppermute x1, waiting for transfers between devices, local(): got = lax.ppermute(joined, ('gx_0', 'gx_1', 'gz'), z_pairs())  16.2 us
    all_to_all x1, blocking collectives, local(): own = lax.all_to_all(packed, GX, 0, 0, tiled=True).reshape(16, BY, 128)  10.4 us
    all_to_all x1, blocking collectives, local(): fields = lax.all_to_all(packed, 'gx_0', 0, 0, tiled=True)  9.78 us
    ppermute x1, starting transfers between devices, local(): far = lax.ppermute(own, ('gx_1', 'gy'), both_ways(16, 2))  6.21 us
    ppermute x1, starting transfers between devices, local(): near = lax.ppermute(own, ('gx_1', 'gy'), both_ways(16, 1))  4.28 us
  transfers between devices with their start and end apart: 6, of which 4 were waited for; matrix products, arithmetic and copies ran while one was open for 0% of the time, Pallas kernels for 0%

profile of v1, /device:TPU:8, one launch (start us, length us, event | category | flops | bytes accessed | tf_op | source)
XLA Modules:
  0.0 158.2 jit_solution(13358396952489030652)
XLA Ops:
  0.6 0.7 stack.23.where_ref
  1.3 1.7 %shard_map.59 = (f32[8,16,128]{2,1,0:T(8,128)}, f32[8,2,16,128]{3,2,1,0:T(8,128)}) custom-call(s32[5]{0:T(128)} %stack.23.where_ref, f32[8,16,128]{2,1,0:T(8,128)} %density.1, f32[2,16,128]{2,1,0:T(8,128)} %xf.1, f32[2,8,128]{2,1,0:T(8,128)} %yf.1, f32[2,8,16]{2,1,0:T(8,128)} %zf.1), custom_call_target="tpu_custom_call" | custom-call | tf_op jit(solution)/shard_map/pallas_call | solution.py:72
  3.0 10.4 %all_to_all.15 = f32[8,2,16,128]{3,2,1,0:T(8,128)S(1)} all-to-all(f32[8,2,16,128]{3,2,1,0:T(8,128)} %get-tuple-element.5), channel_id=1, replica_groups=mesh['gx_0'=4,'gx_1'=2,'gy'=16,'gz'=8] {'gx_0','gx_1'}, dimensions={0} | all-to-all | bytes 262144 | tf_op jit(solution)/shard_map/all_to_all | solution.py:332
  13.4 0.0 copy-start.3
  13.4 0.0 copy-start.1
  13.5 6.2 %collective-permute-start.1 = (f32[16,16,128]{2,1,0:T(8,128)S(1)}, f32[16,16,128]{2,1,0:T(8,128)S(1)}, u32[]{:S(2)}, u32[]{:S(2)}) collective-permute-start(f32[16,16,128]{2,1,0:T(8,128)S(1)} %bitcast.7), channel_id=1, source_target_pairs={{0,16},{8,24},{16,32},{24,40},{32,48},{40,56},{48,64},{56,72},{64,... | collective-permute-start | bytes 393224 | tf_op jit(solution)/shard_map/ppermute | solution.py:334
  19.7 4.3 %collective-permute-start = (f32[16,16,128]{2,1,0:T(8,128)S(1)}, f32[16,16,128]{2,1,0:T(8,128)S(1)}, u32[]{:S(2)}, u32[]{:S(2)}) collective-permute-start(f32[16,16,128]{2,1,0:T(8,128)S(1)} %bitcast.8), channel_id=1, source_target_pairs={{0,8},{8,16},{16,24},{24,32},{32,40},{40,48},{48,56},{56,64},{64,7... | collective-permute-start | bytes 393224 | tf_op jit(solution)/shard_map/ppermute | solution.py:333
  24.0 0.0 collective-permute-done.1.far
  24.0 0.0 copy-start.4
  24.0 1.9 %collective-permute-start.3 = (f32[16,16,128]{2,1,0:T(8,128)S(1)}, f32[16,16,128]{2,1,0:T(8,128)S(1)}, u32[]{:S(2)}, u32[]{:S(2)}) collective-permute-start(f32[16,16,128]{2,1,0:T(8,128)S(1)} %collective-permute-done.1.far), channel_id=1, source_target_pairs={{0,128},{128,0},{1,129},{129,1},{2,130},{130,2},{3,131},{131,3},{4... | collective-permute-start | bytes 393224 | tf_op jit(solution)/shard_map/ppermute | solution.py:336
  25.9 0.5 collective-permute-done.near
  26.5 0.0 copy-start.5
  26.5 1.9 %collective-permute-start.2 = (f32[16,16,128]{2,1,0:T(8,128)S(1)}, f32[16,16,128]{2,1,0:T(8,128)S(1)}, u32[]{:S(2)}, u32[]{:S(2)}) collective-permute-start(f32[16,16,128]{2,1,0:T(8,128)S(1)} %collective-permute-done.near), channel_id=1, source_target_pairs={{0,128},{128,0},{1,129},{129,1},{2,130},{130,2},{3,131},{131,3},{4... | collective-permute-start | bytes 393224 | tf_op jit(solution)/shard_map/ppermute | solution.py:335
  28.4 0.0 collective-permute-done.3.far2
  28.4 0.0 copy-start.6
  28.4 1.3 collective-permute-done.2.near2
  29.7 0.0 copy-done.3
  29.7 0.0 copy-done.4
  29.7 0.0 copy-done.5
  29.7 0.0 copy-done.6
  29.7 0.0 copy-start.7
  29.7 0.6 copy-done.7
  30.4 2.1 %shard_map.60.own = f32[16,80,128]{2,1,0:T(8,128)} custom-call(s32[5]{0:T(128)} %stack.23.where_ref, f32[16,16,128]{2,1,0:T(8,128)} %bitcast.9, f32[16,16,128]{2,1,0:T(8,128)} %copy-done.5, f32[16,16,128]{2,1,0:T(8,128)} %copy-done.4, f32[16,16,128]{2,1,0:T(8,128)} %copy-done.7, f32[16,16,128]{2,1,0:T(8,128)} %copy-done.6), custom_call_target="tpu_custom_call" | custom-call | tf_op jit(solution)/shard_map/pallas_call | solution.py:103
  32.4 2.5 %collective-permute-start.4 = (f32[16,80,128]{2,1,0:T(8,128)}, f32[16,80,128]{2,1,0:T(8,128)S(1)}, u32[]{:S(2)}, u32[]{:S(2)}) collective-permute-start(f32[16,80,128]{2,1,0:T(8,128)} %shard_map.60.own), channel_id=1, source_target_pairs={{0,256},{256,512},{512,768},{768,1},{1,257},{257,513},{513,769},{7... | collective-permute-start | bytes 1966088 | tf_op jit(solution)/shard_map/ppermute | solution.py:338
  34.9 16.2 %collective-permute-done.4.got = f32[16,80,128]{2,1,0:T(8,128)S(1)} collective-permute-done((f32[16,80,128]{2,1,0:T(8,128)}, f32[16,80,128]{2,1,0:T(8,128)S(1)}, u32[]{:S(2)}, u32[]{:S(2)}) %collective-permute-start.4) | collective-permute-done | bytes 655392 | tf_op jit(solution)/shard_map/ppermute | solution.py:338
  51.1 1.9 %collective-permute-start.5 = (f32[16,80,128]{2,1,0:T(8,128)S(1)}, f32[16,80,128]{2,1,0:T(8,128)S(1)}, u32[]{:S(2)}, u32[]{:S(2)}) collective-permute-start(f32[16,80,128]{2,1,0:T(8,128)S(1)} %collective-permute-done.4.got), channel_id=1, source_target_pairs={{0,128},{128,0},{1,129},{129,1},{2,130},{130,2},{3,131},{131,3},{4... | collective-permute-start | bytes 1966088 | tf_op jit(solution)/shard_map/ppermute | solution.py:339
  53.1 2.1 %collective-permute-done.5.swapped = f32[16,80,128]{2,1,0:T(8,128)S(1)} collective-permute-done((f32[16,80,128]{2,1,0:T(8,128)S(1)}, f32[16,80,128]{2,1,0:T(8,128)S(1)}, u32[]{:S(2)}, u32[]{:S(2)}) %collective-permute-start.5) | collective-permute-done | bytes 655392 | tf_op jit(solution)/shard_map/ppermute | solution.py:339
  55.1 0.0 copy-done.1
  55.1 0.0 copy-start
  55.1 1.1 copy-done
  56.2 51.7 %shard_map.61 = f32[4,136,128]{2,1,0:T(8,128)S(1)} custom-call(s32[5]{0:T(128)S(1)} %copy-done.1, f32[16,80,128]{2,1,0:T(8,128)S(1)} %copy-done, f32[16,80,128]{2,1,0:T(8,128)S(1)} %collective-permute-done.4.got, f32[16,80,128]{2,1,0:T(8,128)S(1)} %collective-permute-done.5.swapped), custom_call_target="tpu_custom_call" | custom-call | tf_op jit(solution)/shard_map/pallas_call | solution.py:267
  107.9 9.8 %all_to_all.16.fields = f32[4,136,128]{2,1,0:T(8,128)S(1)} all-to-all(f32[4,136,128]{2,1,0:T(8,128)S(1)} %shard_map.61), channel_id=1, replica_groups=mesh['gx_0'=4,'gx_1'=2,'gy'=16,'gz'=8] {'gx_0'}, dimensions={0} | all-to-all | bytes 557056 | tf_op jit(solution)/shard_map/all_to_all | solution.py:341
  117.7 0.0 copy-start.2
  117.7 38.6 %all_to_all.17 = f32[128,1,128]{2,1,0:T(1,128)} all-to-all(f32[128,1,128]{2,1,0:T(1,128)S(1)} %broadcast_in_dim.3), channel_id=1, replica_groups=mesh['gx_0'=4,'gx_1'=2,'gy'=16,'gz'=8] {'gy','gz'}, dimensions={0} | all-to-all | bytes 131072 | tf_op jit(solution)/shard_map/all_to_all | solution.py:343
  156.3 0.0 copy-done.2
  156.3 1.9 %shard_map.62 = (f32[8,16,128]{2,1,0:T(8,128)}, f32[8,16,128]{2,1,0:T(8,128)}) custom-call(f32[8,16,128]{2,1,0:T(8,128)} %get-tuple-element.4.rhs, f32[4,136,128]{2,1,0:T(8,128)} %copy-done.2, f32[128,128]{1,0:T(8,128)} %bitcast.10), custom_call_target="tpu_custom_call" | custom-call | tf_op jit(solution)/shard_map/pallas_call | solution.py:310
  (2 shorter events, 0.1 us)
Async XLA Ops:
  13.4 16.2 %copy-start.3 = (f32[8,2,16,128]{3,2,1,0:T(8,128)}, f32[8,2,16,128]{3,2,1,0:T(8,128)S(1)}, u32[]{:S(2)}) copy-start(f32[8,2,16,128]{3,2,1,0:T(8,128)S(1)} %all_to_all.15) | copy-start | bytes 393220
  13.4 41.7 %copy-start.1 = (s32[5]{0:T(128)S(1)}, s32[5]{0:T(128)}, u32[]{:S(2)}) copy-start(s32[5]{0:T(128)} %stack.23.where_ref) | copy-start | bytes 64
  13.5 10.5 %collective-permute-start.1 = (f32[16,16,128]{2,1,0:T(8,128)S(1)}, f32[16,16,128]{2,1,0:T(8,128)S(1)}, u32[]{:S(2)}, u32[]{:S(2)}) collective-permute-start(f32[16,16,128]{2,1,0:T(8,128)S(1)} %bitcast.7), channel_id=1, source_target_pairs={{0,16},{8,24},{16,32},{24,40},{32,48},{40,56},{48,64},{56,72},{64,... | collective-permute-start | bytes 393224 | tf_op jit(solution)/shard_map/ppermute | solution.py:334
  19.7 6.8 %collective-permute-start = (f32[16,16,128]{2,1,0:T(8,128)S(1)}, f32[16,16,128]{2,1,0:T(8,128)S(1)}, u32[]{:S(2)}, u32[]{:S(2)}) collective-permute-start(f32[16,16,128]{2,1,0:T(8,128)S(1)} %bitcast.8), channel_id=1, source_target_pairs={{0,8},{8,16},{16,24},{24,32},{32,40},{40,48},{48,56},{56,64},{64,7... | collective-permute-start | bytes 393224 | tf_op jit(solution)/shard_map/ppermute | solution.py:333
  24.0 5.7 %copy-start.4 = (f32[16,16,128]{2,1,0:T(8,128)}, f32[16,16,128]{2,1,0:T(8,128)S(1)}, u32[]{:S(2)}) copy-start(f32[16,16,128]{2,1,0:T(8,128)S(1)} %collective-permute-done.1.far) | copy-start | bytes 393220
  24.0 4.4 %collective-permute-start.3 = (f32[16,16,128]{2,1,0:T(8,128)S(1)}, f32[16,16,128]{2,1,0:T(8,128)S(1)}, u32[]{:S(2)}, u32[]{:S(2)}) collective-permute-start(f32[16,16,128]{2,1,0:T(8,128)S(1)} %collective-permute-done.1.far), channel_id=1, source_target_pairs={{0,128},{128,0},{1,129},{129,1},{2,130},{130,2},{3,131},{131,3},{4... | collective-permute-start | bytes 393224 | tf_op jit(solution)/shard_map/ppermute | solution.py:336
  26.5 3.2 %copy-start.5 = (f32[16,16,128]{2,1,0:T(8,128)}, f32[16,16,128]{2,1,0:T(8,128)S(1)}, u32[]{:S(2)}) copy-start(f32[16,16,128]{2,1,0:T(8,128)S(1)} %collective-permute-done.near) | copy-start | bytes 393220
  26.5 3.2 %collective-permute-start.2 = (f32[16,16,128]{2,1,0:T(8,128)S(1)}, f32[16,16,128]{2,1,0:T(8,128)S(1)}, u32[]{:S(2)}, u32[]{:S(2)}) collective-permute-start(f32[16,16,128]{2,1,0:T(8,128)S(1)} %collective-permute-done.near), channel_id=1, source_target_pairs={{0,128},{128,0},{1,129},{129,1},{2,130},{130,2},{3,131},{131,3},{4... | collective-permute-start | bytes 393224 | tf_op jit(solution)/shard_map/ppermute | solution.py:335
  28.4 1.3 copy-start.6
  29.7 0.6 copy-start.7
  32.4 18.7 %collective-permute-start.4 = (f32[16,80,128]{2,1,0:T(8,128)}, f32[16,80,128]{2,1,0:T(8,128)S(1)}, u32[]{:S(2)}, u32[]{:S(2)}) collective-permute-start(f32[16,80,128]{2,1,0:T(8,128)} %shard_map.60.own), channel_id=1, source_target_pairs={{0,256},{256,512},{512,768},{768,1},{1,257},{257,513},{513,769},{7... | collective-permute-start | bytes 1966088 | tf_op jit(solution)/shard_map/ppermute | solution.py:338
  51.1 4.0 %collective-permute-start.5 = (f32[16,80,128]{2,1,0:T(8,128)S(1)}, f32[16,80,128]{2,1,0:T(8,128)S(1)}, u32[]{:S(2)}, u32[]{:S(2)}) collective-permute-start(f32[16,80,128]{2,1,0:T(8,128)S(1)} %collective-permute-done.4.got), channel_id=1, source_target_pairs={{0,128},{128,0},{1,129},{129,1},{2,130},{130,2},{3,131},{131,3},{4... | collective-permute-start | bytes 1966088 | tf_op jit(solution)/shard_map/ppermute | solution.py:339
  55.1 1.1 copy-start
  117.7 38.6 %copy-start.2 = (f32[4,136,128]{2,1,0:T(8,128)}, f32[4,136,128]{2,1,0:T(8,128)S(1)}, u32[]{:S(2)}) copy-start(f32[4,136,128]{2,1,0:T(8,128)S(1)} %all_to_all.16.fields) | copy-start | bytes 835588

commit v2 on v1

v2 whole, which is shorter than its diff:
```python
import functools

import jax
import jax.numpy as jnp
from jax import lax
from jax.experimental import pallas as pl
from jax.experimental.pallas import tpu as pltpu
from jax.sharding import Mesh
from jax.sharding import PartitionSpec as P

AXES = ("gx_0", "gx_1", "gy", "gz")
GX = ("gx_0", "gx_1")
NX, NY, NZ = 64, 256, 1024
BX, BY, BZ = 8, 16, 128
CZ = 32
HY, HZ = 32, 32
ROWS, LANES = BY + 2 * HY, 128
relax = 1.0 / 9.0
coupling = 0.5
VMEM = pl.BlockSpec(memory_space=pltpu.VMEM)
SMEM = pl.BlockSpec(memory_space=pltpu.SMEM)


def roll(x, shift, axis):
    return pltpu.roll(x, shift % x.shape[axis], axis)


def lane_index(shape):
    return lax.broadcasted_iota(jnp.int32, shape, 1)


def row_index(shape):
    return lax.broadcasted_iota(jnp.int32, shape, 0)


PLANES = (0, 2, 1, 3)


def rhs_kernel(where_ref, density, xf, yf, zf, rhs, packed, scratch):
    gx, gy, gz = where_ref[0], where_ref[1], where_ref[2]
    rows, lanes = row_index((BY, BZ)), lane_index((BY, BZ))
    eye = row_index((BY, BY)) == lane_index((BY, BY))
    low_y = (rows == 0) & (gy == 0)
    high_y = (rows == BY - 1) & (gy == NY // BY - 1)
    low_z = (lanes == 0) & (gz == 0)
    high_z = (lanes == BZ - 1) & (gz == NZ // BZ - 1)

    def column(row):
        return jnp.sum(jnp.where(eye, row, 0.0), axis=1, keepdims=True)

    layers = []
    for x in range(BX):
        value = -coupling * density[x]
        if x == 0:
            value = value + jnp.where(gx == 0, xf[0], 0.0)
        if x == BX - 1:
            value = value + jnp.where(gx == NX // BX - 1, xf[1], 0.0)
        value = value + jnp.where(low_y, yf[0, x : x + 1, :], 0.0)
        value = value + jnp.where(high_y, yf[1, x : x + 1, :], 0.0)
        value = value + jnp.where(low_z, column(zf[0, x : x + 1, :]), 0.0)
        value = value + jnp.where(high_z, column(zf[1, x : x + 1, :]), 0.0)
        rhs[x] = value
        layers.append(value)
    for chunk in range(4):
        for quad in range(2):
            out = None
            for k in range(4):
                part = roll(layers[4 * quad + k], 32 * (k - chunk), 1)
                out = part if k == 0 else jnp.where(lanes >= 32 * k, part, out)
            scratch[chunk, quad] = out
    for chunk in range(4):
        for quad in range(2):
            for at, plane in enumerate(PLANES):
                part = scratch[chunk, quad, pl.ds(plane, 4, stride=4), :]
                packed[2 * chunk, quad, 4 * at : 4 * at + 4] = part
                packed[2 * chunk + 1, quad, 4 * at : 4 * at + 4] = part


def make_rhs(where, density, xf, yf, zf):
    return pl.pallas_call(
        rhs_kernel,
        out_shape=(
            jax.ShapeDtypeStruct((BX, BY, BZ), jnp.float32),
            jax.ShapeDtypeStruct((8, 2, BY, BZ), jnp.float32),
        ),
        in_specs=[SMEM, VMEM, VMEM, VMEM, VMEM],
        out_specs=(VMEM, VMEM),
        scratch_shapes=[pltpu.VMEM((4, 2, BY, BZ), jnp.float32)],
    )(where, density, xf, yf, zf)


def join_kernel(where_ref, own, near, far, near2, far2, out):
    core = where_ref[3]

    def place(blocks):
        def layer(i, _):
            for at in range(4):
                for b, block in enumerate(blocks):
                    out[i, 20 * at + 4 * b : 20 * at + 4 * b + 4] = block[i, 4 * at : 4 * at + 4]
            return 0

        lax.fori_loop(0, NX // 4, layer, 0, unroll=4)

    @pl.when(core == 0)
    def _():
        place((far, near, own, near2, far2))

    @pl.when(core == 1)
    def _():
        place((far2, near2, own, near, far))


def join(where, own, near, far, near2, far2):
    return pl.pallas_call(
        join_kernel,
        out_shape=jax.ShapeDtypeStruct((16, ROWS, 128), jnp.float32),
        in_specs=[SMEM] + [VMEM] * 5,
        out_specs=VMEM,
    )(where, own, near, far, near2, far2)


WHOLE = (0, 8, 12)
MIDDLE = (4, 12)
HOME = (6,)


def sides(x, step):
    return roll(x, step, 1) + roll(x, -step, 1)


def third(x):
    return x * (1.0 / 3.0)


def even(ref, x, half, j):
    return ref[x, 0, pl.ds(20 * half + j, 8)]


def odd(ref, x, half, j):
    return ref[x, 1, pl.ds(20 + 20 * half + j, 8)]


def below(ref, x, half, j):
    return ref[x, 1, pl.ds(20 * half + j, 8)]


def above(ref, x, half, j):
    return ref[x, 0, pl.ds(20 + 20 * half + j, 8)]


def put0(ref, x, parity, half, j, value):
    if parity == 0:
        if half == 0:
            ref[x, 0, pl.ds(39 + j, 8)] = value
        ref[x, 0, pl.ds(20 * half + j, 8)] = value
    else:
        if half == 1:
            if j == 12:
                ref[x, 1, pl.ds(13, 7)] = value[0:7]
            else:
                ref[x, 1, pl.ds(1 + j, 8)] = value
        ref[x, 1, pl.ds(20 + 20 * half + j, 8)] = value


def put1(ref, x, half, j, value):
    if half == 0:
        ref[x, pl.ds(59 + j, 8)] = value
    elif j == 12:
        ref[x, pl.ds(13, 7)] = value[0:7]
    else:
        ref[x, pl.ds(1 + j, 8)] = value
    ref[x, pl.ds(20 + 20 * half + j, 8)] = value


def chunks(count, size, body):
    lax.fori_loop(0, count // size, lambda i, _: body(i * size) or 0, 0)


def cycle_down(src, mask, fold, f1, f2, tiles):
    def level1(first):
        for j in tiles:
            m = mask[pl.ds(j, 8)]
            for half in range(2):
                cells = [even(src, 2 * first + k, half, j) + odd(src, 2 * first + k, half, j) for k in range(10)]
                for i in range(4):
                    before, a, b, after = cells[2 * i : 2 * i + 4]
                    u = a + b
                    y = [below(src, 2 * first + 2 * i + k, half, j) + above(src, 2 * first + 2 * i + k, half, j) for k in (1, 2)]
                    s = third(u) + relax * (((u + u) + (before + after)) + ((y[0] + y[1]) + sides(u, 1)))
                    put1(f1, first + i + 1, half, j, fold(s, 1) * m)

    chunks(NX // 2, 4, level1)

    def level2(first):
        for j in tiles:
            m = mask[pl.ds(j, 8)]
            cells = [f1[2 * first + k, pl.ds(20 + j, 8)] + f1[2 * first + k, pl.ds(40 + j, 8)] for k in range(10)]
            for i in range(4):
                before, a, b, after = cells[2 * i : 2 * i + 4]
                u = a + b
                y = [f1[2 * first + 2 * i + k, pl.ds(j, 8)] + f1[2 * first + 2 * i + k, pl.ds(60 + j, 8)] for k in (1, 2)]
                s = third(u) + relax * (((u + u) + (before + after)) + ((y[0] + y[1]) + sides(u, 2)))
                f2[first + i + 1, pl.ds(8 + j, 8)] = fold(s, 2) * m

    chunks(NX // 4, 4, level2)


def cycle_coarse(mask, f2, t2, e2, tiles, last):
    def around(ref, x, j):
        return (ref[x - 1, pl.ds(8 + j, 8)] + ref[x + 1, pl.ds(8 + j, 8)]) + (ref[x, pl.ds(7 + j, 8)] + ref[x, pl.ds(9 + j, 8)])

    def sweep1(first):
        for j in tiles:
            m = mask[pl.ds(j, 8)]
            for i in range(1, 9):
                r = f2[first + i, pl.ds(8 + j, 8)]
                s = (4.0 / 3.0) * r + relax * (around(f2, first + i, j) + sides(r, 4))
                t2[first + i, pl.ds(8 + j, 8)] = (relax * s) * m

    chunks(NX // 4, 8, sweep1)

    def sweep2(first):
        for j in last:
            m = mask[pl.ds(j, 8)]
            for i in range(1, 9):
                v = t2[first + i, pl.ds(8 + j, 8)]
                s = third(v) + relax * (f2[first + i, pl.ds(8 + j, 8)] + (around(t2, first + i, j) + sides(v, 4)))
                e2[first + i, pl.ds(8 + j, 8)] = s * m

    chunks(NX // 4, 8, sweep2)


def cycle_up(src, mask, f1, e2, v1, e1, v0, out, tiles, last):
    def correct1(first):
        for j in tiles:
            for i in range(4):
                e = e2[first + i + 1, pl.ds(8 + j, 8)]
                for half in range(2):
                    for k in (1, 2):
                        x = 2 * first + 2 * i + k
                        put1(v1, x, half, j, relax * f1[x, pl.ds(20 + 20 * half + j, 8)] + e)

    chunks(NX // 4, 4, correct1)

    def smooth1(first):
        for j in tiles:
            m = mask[pl.ds(j, 8)]
            for half in range(2):
                at = pl.ds(20 + 20 * half + j, 8)
                for i in range(1, 9):
                    x = first + i
                    v = v1[x, at]
                    y = v1[x, pl.ds(20 * half + j, 8)] + v1[x, pl.ds(40 + 20 * half + j, 8)]
                    s = third(v) + relax * ((f1[x, at] + (v1[x - 1, at] + v1[x + 1, at])) + (y + sides(v, 2)))
                    e1[x, pl.ds(20 * half + j, 8)] = s * m

    chunks(NX // 2, 8, smooth1)

    def correct0(first):
        for j in tiles:
            for i in range(1, 5):
                for half in range(2):
                    e = e1[first + i, pl.ds(20 * half + j, 8)]
                    for k in (-1, 0):
                        x = 2 * first + 2 * i + k
                        put0(v0, x, 0, half, j, relax * even(src, x, half, j) + e)
                        put0(v0, x, 1, half, j, relax * odd(src, x, half, j) + e)

    chunks(NX // 2, 4, correct0)

    def smooth0(first):
        for j in last:
            m = mask[pl.ds(j, 8)]
            for half in range(2):
                evens = [even(v0, first + k, half, j) for k in range(10)]
                odds = [odd(v0, first + k, half, j) for k in range(10)]
                for i in range(1, 9):
                    x = first + i
                    v, o = evens[i], odds[i]
                    s = third(v) + relax * ((even(src, x, half, j) + (evens[i - 1] + evens[i + 1])) + ((below(v0, x, half, j) + o) + sides(v, 1)))
                    put0(out, x, 0, half, j, s * m)
                    s = third(o) + relax * ((odd(src, x, half, j) + (odds[i - 1] + odds[i + 1])) + ((above(v0, x, half, j) + v) + sides(o, 1)))
                    put0(out, x, 1, half, j, s * m)

    chunks(NX, 8, smooth0)


def images(src, first, half, j, count):
    evens = [even(src, first + k, half, j) for k in range(count + 2)]
    odds = [odd(src, first + k, half, j) for k in range(count + 2)]
    result = []
    for i in range(1, count + 1):
        v, o = evens[i], odds[i]
        e = 6.0 * v - ((evens[i - 1] + evens[i + 1]) + ((below(src, first + i, half, j) + o) + sides(v, 1)))
        d = 6.0 * o - ((odds[i - 1] + odds[i + 1]) + ((above(src, first + i, half, j) + v) + sides(o, 1)))
        result.append((v, o, e, d))
    return result


def cycles_kernel(where_ref, own, got, swapped, out, r0, z0, q0, w, v0, f1, v1, e1, f2, t2, e2, mask):
    gx0, core, gy, gz = where_ref[4], where_ref[3], where_ref[1], where_ref[2]
    rows, lanes = row_index((24, LANES)), lane_index((24, LANES))
    y = gy * BY - HY + 4 * rows
    z = (gz * 4 + gx0) * CZ - HZ + lanes
    mask[...] = jnp.where((y >= 0) & (y < NY) & (z >= 0) & (z < NZ), 1.0, 0.0)
    for ref, count in ((r0, NX), (z0, NX), (q0, NX), (w, NX), (v0, NX), (f1, NX // 2), (v1, NX // 2), (f2, NX // 4), (t2, NX // 4)):
        ref[0] = jnp.zeros(ref.shape[1:], jnp.float32)
        ref[count + 1] = jnp.zeros(ref.shape[1:], jnp.float32)
    nothing = jnp.zeros((1, LANES), jnp.float32)

    def edges(i, _):
        for ref in (r0, v0):
            ref[i, 0, 59:60] = nothing
            ref[i, 1, 0:1] = nothing
        return 0

    lax.fori_loop(1, NX + 1, edges, 0, unroll=8)

    def edges1(i, _):
        for ref in (f1, v1):
            ref[i, 79:80] = nothing
            ref[i, 0:1] = nothing
        return 0

    lax.fori_loop(1, NX // 2 + 1, edges1, 0, unroll=8)

    def edges2(i, _):
        for ref in (f2, t2):
            ref[i, 7:8] = nothing
            ref[i, 28:29] = nothing
        return 0

    lax.fori_loop(1, NX // 4 + 1, edges2, 0, unroll=8)
    lanes = lane_index((8, LANES))

    def unpack(left, right):
        def body(first):
            for i in range(2):
                for parity in range(2):
                    for half in range(2):
                        for j in WHOLE:
                            at = pl.ds(20 * (2 * parity + half) + j, 8)
                            a, c, b = left[first + i, at], own[first + i, at], right[first + i, at]
                            for k in range(4):
                                value = jnp.where(lanes < 32, roll(a, -32 * k, 1), jnp.where(lanes < 64, roll(c, 32 - 32 * k, 1), roll(b, 64 - 32 * k, 1)))
                                put0(r0, 4 * (first + i) + k + 1, parity, half, j, value)

        chunks(NX // 4, 2, body)

    @pl.when(core == 0)
    def _():
        unpack(got, swapped)

    @pl.when(core == 1)
    def _():
        unpack(swapped, got)

    low = {step: lanes & step == 0 for step in (1, 2)}

    def fold(x, step):
        return 0.5 * (x + jnp.where(low[step], roll(x, -step, 1), roll(x, step, 1)))

    cycle_down(r0, mask, fold, f1, f2, WHOLE)
    cycle_coarse(mask, f2, t2, e2, WHOLE, WHOLE)
    cycle_up(r0, mask, f1, e2, v1, e1, v0, z0, WHOLE, MIDDLE)

    def image(first):
        for j in MIDDLE:
            m = mask[pl.ds(j, 8)]
            for half in range(2):
                for i, (_, _, e, d) in enumerate(images(z0, first, half, j, 8)):
                    put0(q0, first + i + 1, 0, half, j, e * m)
                    put0(q0, first + i + 1, 1, half, j, d * m)

    chunks(NX, 8, image)
    cycle_down(q0, mask, fold, f1, f2, MIDDLE)
    cycle_coarse(mask, f2, t2, e2, MIDDLE, HOME)
    cycle_up(q0, mask, f1, e2, v1, e1, v0, w, HOME, HOME)

    inside = (lanes >= HZ) & (lanes < HZ + CZ) & (row_index((8, LANES)) < 4)

    def sums(i, acc):
        acc = list(acc)
        for half in range(2):
            for k, (we, wo, se, so) in enumerate(images(w, 8 * i, half, 8, 8)):
                x = 8 * i + k + 1
                for get, ww, s in ((even, we, se), (odd, wo, so)):
                    r, zz, q = get(r0, x, half, 8), get(z0, x, half, 8), get(q0, x, half, 8)
                    for n, term in enumerate((r * zz, zz * q, r * ww, q * ww, ww * s)):
                        acc[n] = acc[n] + term
                at = 20 * half + 8
                v0[x, 0, pl.ds(at, 8)] = se
                v0[x, 1, pl.ds(20 + at, 8)] = so
        return tuple(acc)

    acc = lax.fori_loop(0, NX // 8, sums, (jnp.zeros((8, LANES), jnp.float32),) * 5)

    def send(t, _):
        for k in range(BX):
            x = BX * (2 * t + core) + k + 1
            for at in range(4):
                parity, half = at // 2, at % 2
                rows = pl.ds(20 * parity + 20 * half + 8, 4)
                zz, q, ww, s = (ref[x, parity, rows] for ref in (z0, q0, w, v0))
                wide = lanes[0:4]
                out[t, pl.ds(k * BY + 4 * at, 4)] = jnp.where(
                    wide < 32, roll(zz, -32, 1), jnp.where(wide < 64, q, jnp.where(wide < 96, roll(ww, 32, 1), roll(s, 64, 1)))
                )
        return 0

    lax.fori_loop(0, 4, send, 0)
    row = jnp.zeros((8, LANES), jnp.float32)
    for k, a in enumerate(acc):
        row = jnp.where(lanes == k, jnp.sum(jnp.where(inside, a, 0.0)), row)
    for t in range(4):
        out[t, BX * BY : BX * BY + 8] = row


def cycles(where, own, got, swapped):
    fine = pltpu.VMEM((NX + 2, 2, 64, LANES), jnp.float32)
    level1 = pltpu.VMEM((NX // 2 + 2, 80, LANES), jnp.float32)
    level2 = pltpu.VMEM((NX // 4 + 2, 40, LANES), jnp.float32)
    return pl.pallas_call(
        cycles_kernel,
        out_shape=jax.ShapeDtypeStruct((4, BX * BY + 8, LANES), jnp.float32),
        in_specs=[SMEM] + [VMEM] * 3,
        out_specs=VMEM,
        scratch_shapes=[fine] * 5 + [level1, level1, pltpu.VMEM((NX // 2 + 2, 40, LANES), jnp.float32)] + [level2] * 3 + [pltpu.VMEM((24, LANES), jnp.float32)],
        compiler_params=pltpu.CompilerParams(vmem_limit_bytes=48 * 1024 * 1024),
    )(where, own, got, swapped)


def finish_kernel(rhs, fields, sums, solution, residual):
    total = jnp.sum(sums[...], axis=0, keepdims=True)
    lanes = lane_index(total.shape)

    def pick(k):
        return jnp.sum(jnp.where(lanes == k, total, 0.0), axis=1, keepdims=True)

    rz, zq, rw, qw, ws = (pick(k) for k in range(5))
    step0 = rz / zq
    rz1 = rz - step0 * (rw + zq) + step0 * step0 * qw
    growth = rz1 / rz
    image1 = (zq - 2.0 * step0 * qw + step0 * step0 * ws) + 2.0 * growth * (zq - step0 * qw) + growth * growth * zq
    step1 = rz1 / image1
    on_z = step0 + step1 * (1.0 + growth)
    on_w = -step1 * step0
    wide = lane_index((BY, LANES))
    for x in range(BX):
        parts = [fields[c, x * BY : (x + 1) * BY] for c in range(4)]

        def field(f):
            value = None
            for c in range(4):
                part = roll(parts[c], 32 * (c - f), 1)
                value = part if c == 0 else jnp.where(wide >= 32 * c, part, value)
            return value

        z0, q0, w, s = (field(f) for f in range(4))
        u = on_z * z0 + on_w * w
        v = on_z * q0 + on_w * s
        for at, plane in enumerate(PLANES):
            rows = pl.ds(plane, 4, stride=4)
            solution[x, rows, :] = u[4 * at : 4 * at + 4]
            residual[x, rows, :] = rhs[x, rows, :] - v[4 * at : 4 * at + 4]


def finish(rhs, fields, sums):
    shape = jax.ShapeDtypeStruct((BX, BY, BZ), jnp.float32)
    return pl.pallas_call(finish_kernel, out_shape=(shape, shape), in_specs=[VMEM] * 3, out_specs=(VMEM, VMEM))(rhs, fields, sums)


def both_ways(count, step):
    pairs = [(i, i + step) for i in range(count - step)]
    return pairs + [(count + b, count + a) for a, b in pairs]


def z_pairs():
    def number(core, block):
        return ((block % 4) * 2 + core) * 8 + block // 4

    up = [(i, i + 1) for i in range(31)]
    return [(number(0, a), number(0, b)) for a, b in up] + [(number(1, b), number(1, a)) for a, b in up]


SWAP = [(0, 1), (1, 0)]


def local(density, x_faces, y_faces, z_faces):
    where = jnp.stack([lax.axis_index(GX), lax.axis_index("gy"), lax.axis_index("gz"), lax.axis_index("gx_1"), lax.axis_index("gx_0")]).astype(jnp.int32)
    rhs, packed = make_rhs(where, density, x_faces, y_faces, z_faces)
    own = lax.all_to_all(packed, GX, 0, 0, tiled=True).reshape(16, BY, 128)
    near = lax.ppermute(own, ("gx_1", "gy"), both_ways(16, 1))
    far = lax.ppermute(own, ("gx_1", "gy"), both_ways(16, 2))
    near2 = lax.ppermute(near, "gx_1", SWAP)
    far2 = lax.ppermute(far, "gx_1", SWAP)
    joined = join(where, own, near, far, near2, far2)
    got = lax.ppermute(joined, ("gx_0", "gx_1", "gz"), z_pairs())
    swapped = lax.ppermute(got, "gx_1", SWAP)
    packed = cycles(where, joined, got, swapped)
    fields = lax.all_to_all(packed, "gx_0", 0, 0, tiled=True)
    sums = jnp.sum(fields[:, BX * BY, :], axis=0)
    sums = lax.all_to_all(jnp.broadcast_to(sums, (128, 1, 128)), ("gy", "gz"), 0, 0, tiled=True)
    return finish(rhs, fields, sums.reshape(128, 128))


def solution(mesh):
    torus = Mesh(mesh.devices.reshape(4, 2, mesh.shape["gy"], mesh.shape["gz"]), AXES)
    in_specs = (P(GX, "gy", "gz"), P(None, "gy", "gz"), P(None, GX, "gz"), P(None, GX, "gy"))
    out_specs = (P(GX, "gy", "gz"), P(GX, "gy", "gz"))
    return jax.shard_map(local, mesh=torus, in_specs=in_specs, out_specs=out_specs, check_vma=False)
```

time: 159 us -> 124 us (0.78)
  Pallas kernels: 57.4 us -> 22.5 us
    pallas_call x1, Pallas kernels: 51.7 us -> 16.7 us  [cycles(): pl.pallas_call(cycles_kernel, out_shape=jax.ShapeDtypeStruct((4, BX * BY...]
where the time goes in v2:
time: 124 us; the launch traced here: 123 us
  blocking collectives  58.7 us (47%)
  Pallas kernels  22.5 us (18%)
  waiting for transfers between devices  20.2 us (16%)
  starting transfers between devices  18.7 us (15%)
  local copies, waits for them, and re-layouts  2.46 us (2%)
    all_to_all x1, blocking collectives, local(): lax.all_to_all(jnp.broadcast_to(sums, (128, 1, 128)), ('gy', 'gz'), 0, 0,...  38.6 us
    pallas_call x1, Pallas kernels, cycles(): pl.pallas_call(cycles_kernel, out_shape=jax.ShapeDtypeStruct((4, BX * BY...  16.7 us
    ppermute x1, waiting for transfers between devices, local(): got = lax.ppermute(joined, ('gx_0', 'gx_1', 'gz'), z_pairs())  16.2 us
    all_to_all x1, blocking collectives, local(): own = lax.all_to_all(packed, GX, 0, 0, tiled=True).reshape(16, BY, 128)  10.4 us
    all_to_all x1, blocking collectives, local(): fields = lax.all_to_all(packed, 'gx_0', 0, 0, tiled=True)  9.78 us
    ppermute x1, starting transfers between devices, local(): far = lax.ppermute(own, ('gx_1', 'gy'), both_ways(16, 2))  6.21 us
    ppermute x1, starting transfers between devices, local(): near = lax.ppermute(own, ('gx_1', 'gy'), both_ways(16, 1))  4.28 us
  transfers between devices with their start and end apart: 6, of which 4 were waited for; matrix products, arithmetic and copies ran while one was open for 0% of the time, Pallas kernels for 0%

profile of v2, /device:TPU:8, one launch (start us, length us, event | category | flops | bytes accessed | tf_op | source)
XLA Modules:
  0.0 123.3 jit_solution(7657340766701975558)
XLA Ops:
  0.6 0.7 stack.23.where_ref
  1.3 1.8 %shard_map.59 = (f32[8,16,128]{2,1,0:T(8,128)}, f32[8,2,16,128]{3,2,1,0:T(8,128)}) custom-call(s32[5]{0:T(128)} %stack.23.where_ref, f32[8,16,128]{2,1,0:T(8,128)} %density.1, f32[2,16,128]{2,1,0:T(8,128)} %xf.1, f32[2,8,128]{2,1,0:T(8,128)} %yf.1, f32[2,8,16]{2,1,0:T(8,128)} %zf.1), custom_call_target="tpu_custom_call" | custom-call | tf_op jit(solution)/shard_map/pallas_call | solution.py:80
  3.1 10.4 %all_to_all.15 = f32[8,2,16,128]{3,2,1,0:T(8,128)S(1)} all-to-all(f32[8,2,16,128]{3,2,1,0:T(8,128)} %get-tuple-element.5), channel_id=1, replica_groups=mesh['gx_0'=4,'gx_1'=2,'gy'=16,'gz'=8] {'gx_0','gx_1'}, dimensions={0} | all-to-all | bytes 262144 | tf_op jit(solution)/shard_map/all_to_all | solution.py:492
  13.5 0.0 copy-start.3
  13.5 0.0 copy-start.1
  13.5 6.2 %collective-permute-start.1 = (f32[16,16,128]{2,1,0:T(8,128)S(1)}, f32[16,16,128]{2,1,0:T(8,128)S(1)}, u32[]{:S(2)}, u32[]{:S(2)}) collective-permute-start(f32[16,16,128]{2,1,0:T(8,128)S(1)} %bitcast.7), channel_id=1, source_target_pairs={{0,16},{8,24},{16,32},{24,40},{32,48},{40,56},{48,64},{56,72},{64,... | collective-permute-start | bytes 393224 | tf_op jit(solution)/shard_map/ppermute | solution.py:494
  19.7 4.3 %collective-permute-start = (f32[16,16,128]{2,1,0:T(8,128)S(1)}, f32[16,16,128]{2,1,0:T(8,128)S(1)}, u32[]{:S(2)}, u32[]{:S(2)}) collective-permute-start(f32[16,16,128]{2,1,0:T(8,128)S(1)} %bitcast.8), channel_id=1, source_target_pairs={{0,8},{8,16},{16,24},{24,32},{32,40},{40,48},{48,56},{56,64},{64,7... | collective-permute-start | bytes 393224 | tf_op jit(solution)/shard_map/ppermute | solution.py:493
  24.0 0.0 collective-permute-done.1.far
  24.0 0.0 copy-start.4
  24.0 1.9 %collective-permute-start.3 = (f32[16,16,128]{2,1,0:T(8,128)S(1)}, f32[16,16,128]{2,1,0:T(8,128)S(1)}, u32[]{:S(2)}, u32[]{:S(2)}) collective-permute-start(f32[16,16,128]{2,1,0:T(8,128)S(1)} %collective-permute-done.1.far), channel_id=1, source_target_pairs={{0,128},{128,0},{1,129},{129,1},{2,130},{130,2},{3,131},{131,3},{4... | collective-permute-start | bytes 393224 | tf_op jit(solution)/shard_map/ppermute | solution.py:496
  25.9 0.5 collective-permute-done.near
  26.5 0.0 copy-start.5
  26.5 1.9 %collective-permute-start.2 = (f32[16,16,128]{2,1,0:T(8,128)S(1)}, f32[16,16,128]{2,1,0:T(8,128)S(1)}, u32[]{:S(2)}, u32[]{:S(2)}) collective-permute-start(f32[16,16,128]{2,1,0:T(8,128)S(1)} %collective-permute-done.near), channel_id=1, source_target_pairs={{0,128},{128,0},{1,129},{129,1},{2,130},{130,2},{3,131},{131,3},{4... | collective-permute-start | bytes 393224 | tf_op jit(solution)/shard_map/ppermute | solution.py:495
  28.4 0.0 collective-permute-done.3.far2
  28.4 0.0 copy-start.6
  28.4 1.3 %collective-permute-done.2.near2 = f32[16,16,128]{2,1,0:T(8,128)S(1)} collective-permute-done((f32[16,16,128]{2,1,0:T(8,128)S(1)}, f32[16,16,128]{2,1,0:T(8,128)S(1)}, u32[]{:S(2)}, u32[]{:S(2)}) %collective-permute-start.2) | collective-permute-done | bytes 131104 | tf_op jit(solution)/shard_map/ppermute | solution.py:495
  29.7 0.0 copy-done.3
  29.7 0.0 copy-done.4
  29.7 0.0 copy-done.5
  29.7 0.0 copy-done.6
  29.7 0.0 copy-start.7
  29.7 0.6 copy-done.7
  30.4 2.2 %shard_map.60.own = f32[16,80,128]{2,1,0:T(8,128)} custom-call(s32[5]{0:T(128)} %stack.23.where_ref, f32[16,16,128]{2,1,0:T(8,128)} %bitcast.9, f32[16,16,128]{2,1,0:T(8,128)} %copy-done.5, f32[16,16,128]{2,1,0:T(8,128)} %copy-done.4, f32[16,16,128]{2,1,0:T(8,128)} %copy-done.7, f32[16,16,128]{2,1,0:T(8,128)} %copy-done.6), custom_call_target="tpu_custom_call" | custom-call | tf_op jit(solution)/shard_map/pallas_call | solution.py:114
  32.5 2.5 %collective-permute-start.4 = (f32[16,80,128]{2,1,0:T(8,128)}, f32[16,80,128]{2,1,0:T(8,128)S(1)}, u32[]{:S(2)}, u32[]{:S(2)}) collective-permute-start(f32[16,80,128]{2,1,0:T(8,128)} %shard_map.60.own), channel_id=1, source_target_pairs={{0,256},{256,512},{512,768},{768,1},{1,257},{257,513},{513,769},{7... | collective-permute-start | bytes 1966088 | tf_op jit(solution)/shard_map/ppermute | solution.py:498
  35.0 16.2 %collective-permute-done.4.got = f32[16,80,128]{2,1,0:T(8,128)S(1)} collective-permute-done((f32[16,80,128]{2,1,0:T(8,128)}, f32[16,80,128]{2,1,0:T(8,128)S(1)}, u32[]{:S(2)}, u32[]{:S(2)}) %collective-permute-start.4) | collective-permute-done | bytes 655392 | tf_op jit(solution)/shard_map/ppermute | solution.py:498
  51.2 1.9 %collective-permute-start.5 = (f32[16,80,128]{2,1,0:T(8,128)S(1)}, f32[16,80,128]{2,1,0:T(8,128)S(1)}, u32[]{:S(2)}, u32[]{:S(2)}) collective-permute-start(f32[16,80,128]{2,1,0:T(8,128)S(1)} %collective-permute-done.4.got), channel_id=1, source_target_pairs={{0,128},{128,0},{1,129},{129,1},{2,130},{130,2},{3,131},{131,3},{4... | collective-permute-start | bytes 1966088 | tf_op jit(solution)/shard_map/ppermute | solution.py:499
  53.2 2.1 %collective-permute-done.5.swapped = f32[16,80,128]{2,1,0:T(8,128)S(1)} collective-permute-done((f32[16,80,128]{2,1,0:T(8,128)S(1)}, f32[16,80,128]{2,1,0:T(8,128)S(1)}, u32[]{:S(2)}, u32[]{:S(2)}) %collective-permute-start.5) | collective-permute-done | bytes 655392 | tf_op jit(solution)/shard_map/ppermute | solution.py:499
  55.2 0.0 copy-done.1
  55.2 0.0 copy-start
  55.2 1.1 copy-done
  56.3 16.7 %shard_map.61 = f32[4,136,128]{2,1,0:T(8,128)S(1)} custom-call(s32[5]{0:T(128)S(1)} %copy-done.1, f32[16,80,128]{2,1,0:T(8,128)S(1)} %copy-done, f32[16,80,128]{2,1,0:T(8,128)S(1)} %collective-permute-done.4.got, f32[16,80,128]{2,1,0:T(8,128)S(1)} %collective-permute-done.5.swapped), custom_call_target="tpu_custom_call" | custom-call | tf_op jit(solution)/shard_map/pallas_call | solution.py:423
  73.0 9.8 %all_to_all.16.fields = f32[4,136,128]{2,1,0:T(8,128)S(1)} all-to-all(f32[4,136,128]{2,1,0:T(8,128)S(1)} %shard_map.61), channel_id=1, replica_groups=mesh['gx_0'=4,'gx_1'=2,'gy'=16,'gz'=8] {'gx_0'}, dimensions={0} | all-to-all | bytes 557056 | tf_op jit(solution)/shard_map/all_to_all | solution.py:501
  82.8 0.0 copy-start.2
  82.8 38.6 %all_to_all.17 = f32[128,1,128]{2,1,0:T(1,128)} all-to-all(f32[128,1,128]{2,1,0:T(1,128)S(1)} %broadcast_in_dim.3), channel_id=1, replica_groups=mesh['gx_0'=4,'gx_1'=2,'gy'=16,'gz'=8] {'gy','gz'}, dimensions={0} | all-to-all | bytes 131072 | tf_op jit(solution)/shard_map/all_to_all | solution.py:503
  121.4 0.0 copy-done.2
  121.4 1.9 %shard_map.62 = (f32[8,16,128]{2,1,0:T(8,128)}, f32[8,16,128]{2,1,0:T(8,128)}) custom-call(f32[8,16,128]{2,1,0:T(8,128)} %get-tuple-element.4.rhs, f32[4,136,128]{2,1,0:T(8,128)} %copy-done.2, f32[128,128]{1,0:T(8,128)} %bitcast.10), custom_call_target="tpu_custom_call" | custom-call | tf_op jit(solution)/shard_map/pallas_call | solution.py:470
  (2 shorter events, 0.1 us)
Async XLA Ops:
  13.5 16.2 %copy-start.3 = (f32[8,2,16,128]{3,2,1,0:T(8,128)}, f32[8,2,16,128]{3,2,1,0:T(8,128)S(1)}, u32[]{:S(2)}) copy-start(f32[8,2,16,128]{3,2,1,0:T(8,128)S(1)} %all_to_all.15) | copy-start | bytes 393220
  13.5 41.8 %copy-start.1 = (s32[5]{0:T(128)S(1)}, s32[5]{0:T(128)}, u32[]{:S(2)}) copy-start(s32[5]{0:T(128)} %stack.23.where_ref) | copy-start | bytes 64
  13.5 10.5 %collective-permute-start.1 = (f32[16,16,128]{2,1,0:T(8,128)S(1)}, f32[16,16,128]{2,1,0:T(8,128)S(1)}, u32[]{:S(2)}, u32[]{:S(2)}) collective-permute-start(f32[16,16,128]{2,1,0:T(8,128)S(1)} %bitcast.7), channel_id=1, source_target_pairs={{0,16},{8,24},{16,32},{24,40},{32,48},{40,56},{48,64},{56,72},{64,... | collective-permute-start | bytes 393224 | tf_op jit(solution)/shard_map/ppermute | solution.py:494
  19.7 6.8 %collective-permute-start = (f32[16,16,128]{2,1,0:T(8,128)S(1)}, f32[16,16,128]{2,1,0:T(8,128)S(1)}, u32[]{:S(2)}, u32[]{:S(2)}) collective-permute-start(f32[16,16,128]{2,1,0:T(8,128)S(1)} %bitcast.8), channel_id=1, source_target_pairs={{0,8},{8,16},{16,24},{24,32},{32,40},{40,48},{48,56},{56,64},{64,7... | collective-permute-start | bytes 393224 | tf_op jit(solution)/shard_map/ppermute | solution.py:493
  24.0 5.7 %copy-start.4 = (f32[16,16,128]{2,1,0:T(8,128)}, f32[16,16,128]{2,1,0:T(8,128)S(1)}, u32[]{:S(2)}) copy-start(f32[16,16,128]{2,1,0:T(8,128)S(1)} %collective-permute-done.1.far) | copy-start | bytes 393220
  24.0 4.4 %collective-permute-start.3 = (f32[16,16,128]{2,1,0:T(8,128)S(1)}, f32[16,16,128]{2,1,0:T(8,128)S(1)}, u32[]{:S(2)}, u32[]{:S(2)}) collective-permute-start(f32[16,16,128]{2,1,0:T(8,128)S(1)} %collective-permute-done.1.far), channel_id=1, source_target_pairs={{0,128},{128,0},{1,129},{129,1},{2,130},{130,2},{3,131},{131,3},{4... | collective-permute-start | bytes 393224 | tf_op jit(solution)/shard_map/ppermute | solution.py:496
  26.5 3.2 %copy-start.5 = (f32[16,16,128]{2,1,0:T(8,128)}, f32[16,16,128]{2,1,0:T(8,128)S(1)}, u32[]{:S(2)}) copy-start(f32[16,16,128]{2,1,0:T(8,128)S(1)} %collective-permute-done.near) | copy-start | bytes 393220
  26.5 3.2 %collective-permute-start.2 = (f32[16,16,128]{2,1,0:T(8,128)S(1)}, f32[16,16,128]{2,1,0:T(8,128)S(1)}, u32[]{:S(2)}, u32[]{:S(2)}) collective-permute-start(f32[16,16,128]{2,1,0:T(8,128)S(1)} %collective-permute-done.near), channel_id=1, source_target_pairs={{0,128},{128,0},{1,129},{129,1},{2,130},{130,2},{3,131},{131,3},{4... | collective-permute-start | bytes 393224 | tf_op jit(solution)/shard_map/ppermute | solution.py:495
  28.4 1.3 %copy-start.6 = (f32[16,16,128]{2,1,0:T(8,128)}, f32[16,16,128]{2,1,0:T(8,128)S(1)}, u32[]{:S(2)}) copy-start(f32[16,16,128]{2,1,0:T(8,128)S(1)} %collective-permute-done.3.far2) | copy-start | bytes 393220
  29.7 0.6 copy-start.7
  32.5 18.7 %collective-permute-start.4 = (f32[16,80,128]{2,1,0:T(8,128)}, f32[16,80,128]{2,1,0:T(8,128)S(1)}, u32[]{:S(2)}, u32[]{:S(2)}) collective-permute-start(f32[16,80,128]{2,1,0:T(8,128)} %shard_map.60.own), channel_id=1, source_target_pairs={{0,256},{256,512},{512,768},{768,1},{1,257},{257,513},{513,769},{7... | collective-permute-start | bytes 1966088 | tf_op jit(solution)/shard_map/ppermute | solution.py:498
  51.2 4.0 %collective-permute-start.5 = (f32[16,80,128]{2,1,0:T(8,128)S(1)}, f32[16,80,128]{2,1,0:T(8,128)S(1)}, u32[]{:S(2)}, u32[]{:S(2)}) collective-permute-start(f32[16,80,128]{2,1,0:T(8,128)S(1)} %collective-permute-done.4.got), channel_id=1, source_target_pairs={{0,128},{128,0},{1,129},{129,1},{2,130},{130,2},{3,131},{131,3},{4... | collective-permute-start | bytes 1966088 | tf_op jit(solution)/shard_map/ppermute | solution.py:499
  55.2 1.1 copy-start
  82.8 38.6 %copy-start.2 = (f32[4,136,128]{2,1,0:T(8,128)}, f32[4,136,128]{2,1,0:T(8,128)S(1)}, u32[]{:S(2)}) copy-start(f32[4,136,128]{2,1,0:T(8,128)S(1)} %all_to_all.16.fields) | copy-start | bytes 835588

commit v3 on v2

--- a/solution.py
+++ b/solution.py
@@ -18,13 +18,21 @@
 relax = 1.0 / 9.0
 coupling = 0.5
 VMEM = pl.BlockSpec(memory_space=pltpu.VMEM)
-SMEM = pl.BlockSpec(memory_space=pltpu.SMEM)
+HBM = pl.BlockSpec(memory_space=pltpu.MemorySpace.HBM)
 
 
 def roll(x, shift, axis):
     return pltpu.roll(x, shift % x.shape[axis], axis)
 
 
+def place():
+    return tuple(lax.axis_index(axis) for axis in AXES)
+
+
+def small(**more):
+    return pltpu.CompilerParams(vmem_limit_bytes=4 * 1024 * 1024, **more)
+
+
 def lane_index(shape):
     return lax.broadcasted_iota(jnp.int32, shape, 1)
 
@@ -36,8 +44,12 @@
 PLANES = (0, 2, 1, 3)
 
 
-def rhs_kernel(where_ref, density, xf, yf, zf, rhs, packed, scratch):
-    gx, gy, gz = where_ref[0], where_ref[1], where_ref[2]
+def rhs_kernel(density_in, xf_in, yf_in, zf_in, rhs, packed, scratch, density, xf, yf, zf, arrived):
+    copies = [pltpu.make_async_copy(a, b, arrived.at[i]) for i, (a, b) in enumerate(((density_in, density), (xf_in, xf), (yf_in, yf), (zf_in, zf)))]
+    for copy in copies:
+        copy.start()
+    gx0, core, gy, gz = place()
+    gx = 2 * gx0 + core
     rows, lanes = row_index((BY, BZ)), lane_index((BY, BZ))
     eye = row_index((BY, BY)) == lane_index((BY, BY))
     low_y = (rows == 0) & (gy == 0)
@@ -48,6 +60,8 @@
     def column(row):
         return jnp.sum(jnp.where(eye, row, 0.0), axis=1, keepdims=True)
 
+    for copy in copies:
+        copy.wait()
     layers = []
     for x in range(BX):
         value = -coupling * density[x]
@@ -76,47 +90,20 @@
                 packed[2 * chunk + 1, quad, 4 * at : 4 * at + 4] = part
 
 
-def make_rhs(where, density, xf, yf, zf):
+def make_rhs(density, xf, yf, zf):
     return pl.pallas_call(
         rhs_kernel,
         out_shape=(
             jax.ShapeDtypeStruct((BX, BY, BZ), jnp.float32),
             jax.ShapeDtypeStruct((8, 2, BY, BZ), jnp.float32),
         ),
-        in_specs=[SMEM, VMEM, VMEM, VMEM, VMEM],
+        in_specs=[HBM] * 4,
         out_specs=(VMEM, VMEM),
-        scratch_shapes=[pltpu.VMEM((4, 2, BY, BZ), jnp.float32)],
-    )(where, density, xf, yf, zf)
-
-
-def join_kernel(where_ref, own, near, far, near2, far2, out):
-    core = where_ref[3]
-
-    def place(blocks):
-        def layer(i, _):
-            for at in range(4):
-                for b, block in enumerate(blocks):
-                    out[i, 20 * at + 4 * b : 20 * at + 4 * b + 4] = block[i, 4 * at : 4 * at + 4]
-            return 0
-
-        lax.fori_loop(0, NX // 4, layer, 0, unroll=4)
-
-    @pl.when(core == 0)
-    def _():
-        place((far, near, own, near2, far2))
-
-    @pl.when(core == 1)
-    def _():
-        place((far2, near2, own, near, far))
-
-
-def join(where, own, near, far, near2, far2):
-    return pl.pallas_call(
-        join_kernel,
-        out_shape=jax.ShapeDtypeStruct((16, ROWS, 128), jnp.float32),
-        in_specs=[SMEM] + [VMEM] * 5,
-        out_specs=VMEM,
-    )(where, own, near, far, near2, far2)
+        scratch_shapes=[pltpu.VMEM((4, 2, BY, BZ), jnp.float32)]
+        + [pltpu.VMEM(a.shape, a.dtype) for a in (density, xf, yf, zf)]
+        + [pltpu.SemaphoreType.DMA((4,))],
+        compiler_params=small(),
+    )(density, xf, yf, zf)
 
 
 WHOLE = (0, 8, 12)
@@ -297,8 +284,8 @@
     return result
 
 
-def cycles_kernel(where_ref, own, got, swapped, out, r0, z0, q0, w, v0, f1, v1, e1, f2, t2, e2, mask):
-    gx0, core, gy, gz = where_ref[4], where_ref[3], where_ref[1], where_ref[2]
+def cycles_kernel(own, side, side2, rows_, rows2, up, up2, down, down2, out, r0, z0, q0, w, v0, f1, v1, e1, f2, t2, e2, mask):
+    gx0, core, gy, gz = place()
     rows, lanes = row_index((24, LANES)), lane_index((24, LANES))
     y = gy * BY - HY + 4 * rows
     z = (gz * 4 + gx0) * CZ - HZ + lanes
@@ -333,27 +320,48 @@
     lax.fori_loop(1, NX // 4 + 1, edges2, 0, unroll=8)
     lanes = lane_index((8, LANES))
 
-    def unpack(left, right):
-        def body(first):
-            for i in range(2):
+    def unpack(low_side, high_side, low_rows, high_rows, low_up, high_up, low_down, high_down):
+        blocks = (
+            (low_up, low_rows, low_down, 1),
+            (low_up, low_rows, low_down, 0),
+            (low_side, own, high_side, None),
+            (high_up, high_rows, high_down, 0),
+            (high_up, high_rows, high_down, 1),
+        )
+
+        def body(i, _):
+            for b, (left, middle, right, pair) in enumerate(blocks):
                 for parity in range(2):
-                    for half in range(2):
-                        for j in WHOLE:
-                            at = pl.ds(20 * (2 * parity + half) + j, 8)
-                            a, c, b = left[first + i, at], own[first + i, at], right[first + i, at]
-                            for k in range(4):
-                                value = jnp.where(lanes < 32, roll(a, -32 * k, 1), jnp.where(lanes < 64, roll(c, 32 - 32 * k, 1), roll(b, 64 - 32 * k, 1)))
-                                put0(r0, 4 * (first + i) + k + 1, parity, half, j, value)
-
-        chunks(NX // 4, 2, body)
+                    at = pl.ds(8 * parity, 8)
+                    a, c, d = ((ref[i, at] if pair is None else ref[pair, i, at]) for ref in (left, middle, right))
+                    for k in range(4):
+                        value = jnp.where(lanes < 32, roll(a, -32 * k, 1), jnp.where(lanes < 64, roll(c, 32 - 32 * k, 1), roll(d, 64 - 32 * k, 1)))
+                        x = 4 * i + k + 1
+                        if parity == 0:
+                            if b > 0:
+                                r0[x, 0, 39 + 4 * b : 43 + 4 * b] = value[0:4]
+                            else:
+                                r0[x, 0, 40:43] = value[1:4]
+                            r0[x, 0, 4 * b : 4 * b + 4] = value[0:4]
+                            r0[x, 0, 20 + 4 * b : 24 + 4 * b] = value[4:8]
+                        else:
+                            if b < 4:
+                                r0[x, 1, 1 + 4 * b : 5 + 4 * b] = value[4:8]
+                            else:
+                                r0[x, 1, 17:20] = value[4:7]
+                            r0[x, 1, 20 + 4 * b : 24 + 4 * b] = value[0:4]
+                            r0[x, 1, 40 + 4 * b : 44 + 4 * b] = value[4:8]
+            return 0
+
+        lax.fori_loop(0, NX // 4, body, 0)
 
     @pl.when(core == 0)
     def _():
-        unpack(got, swapped)
+        unpack(side, side2, rows_, rows2, up, up2, down, down2)
 
     @pl.when(core == 1)
     def _():
-        unpack(swapped, got)
+        unpack(side2, side, rows2, rows_, up2, up, down2, down)
 
     low = {step: lanes & step == 0 for step in (1, 2)}
 
@@ -416,18 +424,18 @@
         out[t, BX * BY : BX * BY + 8] = row
 
 
-def cycles(where, own, got, swapped):
+def cycles(*blocks):
     fine = pltpu.VMEM((NX + 2, 2, 64, LANES), jnp.float32)
     level1 = pltpu.VMEM((NX // 2 + 2, 80, LANES), jnp.float32)
     level2 = pltpu.VMEM((NX // 4 + 2, 40, LANES), jnp.float32)
     return pl.pallas_call(
         cycles_kernel,
         out_shape=jax.ShapeDtypeStruct((4, BX * BY + 8, LANES), jnp.float32),
-        in_specs=[SMEM] + [VMEM] * 3,
+        in_specs=[VMEM] * 9,
         out_specs=VMEM,
         scratch_shapes=[fine] * 5 + [level1, level1, pltpu.VMEM((NX // 2 + 2, 40, LANES), jnp.float32)] + [level2] * 3 + [pltpu.VMEM((24, LANES), jnp.float32)],
-        compiler_params=pltpu.CompilerParams(vmem_limit_bytes=48 * 1024 * 1024),
-    )(where, own, got, swapped)
+        compiler_params=pltpu.CompilerParams(vmem_limit_bytes=30 * 1024 * 1024),
+    )(*blocks)
 
 
 def finish_kernel(rhs, fields, sums, solution, residual):
@@ -467,7 +475,7 @@
 
 def finish(rhs, fields, sums):
     shape = jax.ShapeDtypeStruct((BX, BY, BZ), jnp.float32)
-    return pl.pallas_call(finish_kernel, out_shape=(shape, shape), in_specs=[VMEM] * 3, out_specs=(VMEM, VMEM))(rhs, fields, sums)
+    return pl.pallas_call(finish_kernel, out_shape=(shape, shape), in_specs=[VMEM] * 3, out_specs=(VMEM, VMEM), compiler_params=small())(rhs, fields, sums)
 
 
 def both_ways(count, step):
@@ -475,29 +483,28 @@
     return pairs + [(count + b, count + a) for a, b in pairs]
 
 
-def z_pairs():
+def z_pairs(steps):
     def number(core, block):
         return ((block % 4) * 2 + core) * 8 + block // 4
 
-    up = [(i, i + 1) for i in range(31)]
-    return [(number(0, a), number(0, b)) for a, b in up] + [(number(1, b), number(1, a)) for a, b in up]
+    return [(number(core, a), number(core, a + step)) for core, step in enumerate(steps) for a in range(32) if 0 <= a + step < 32]
 
 
 SWAP = [(0, 1), (1, 0)]
+Z_AXES = ("gx_0", "gx_1", "gz")
 
 
 def local(density, x_faces, y_faces, z_faces):
-    where = jnp.stack([lax.axis_index(GX), lax.axis_index("gy"), lax.axis_index("gz"), lax.axis_index("gx_1"), lax.axis_index("gx_0")]).astype(jnp.int32)
-    rhs, packed = make_rhs(where, density, x_faces, y_faces, z_faces)
+    rhs, packed = make_rhs(density, x_faces, y_faces, z_faces)
     own = lax.all_to_all(packed, GX, 0, 0, tiled=True).reshape(16, BY, 128)
     near = lax.ppermute(own, ("gx_1", "gy"), both_ways(16, 1))
     far = lax.ppermute(own, ("gx_1", "gy"), both_ways(16, 2))
-    near2 = lax.ppermute(near, "gx_1", SWAP)
-    far2 = lax.ppermute(far, "gx_1", SWAP)
-    joined = join(where, own, near, far, near2, far2)
-    got = lax.ppermute(joined, ("gx_0", "gx_1", "gz"), z_pairs())
-    swapped = lax.ppermute(got, "gx_1", SWAP)
-    packed = cycles(where, joined, got, swapped)
+    side = lax.ppermute(own, Z_AXES, z_pairs((1, -1)))
+    rows = jnp.stack([near, far])
+    up = lax.ppermute(rows, Z_AXES, z_pairs((1, 1)))
+    down = lax.ppermute(rows, Z_AXES, z_pairs((-1, -1)))
+    swapped = [lax.ppermute(each, "gx_1", SWAP) for each in (side, rows, up, down)]
+    packed = cycles(own, side, swapped[0], rows, swapped[1], up, swapped[2], down, swapped[3])
     fields = lax.all_to_all(packed, "gx_0", 0, 0, tiled=True)
     sums = jnp.sum(fields[:, BX * BY, :], axis=0)
     sums = lax.all_to_all(jnp.broadcast_to(sums, (128, 1, 128)), ("gy", "gz"), 0, 0, tiled=True)

time: 124 us -> 117 us (0.944)
  waiting for transfers between devices: 20.2 us -> 3.82 us
  starting transfers between devices: 18.7 us -> 34.8 us
  Pallas kernels: 22.5 us -> 17.7 us
  blocking collectives: 58.7 us -> 55.9 us
    ppermute x4 -> x7, waiting for transfers between devices: 19.6 us -> 1.33 us  [the longest x4 1.32 us: local(): lax.ppermute(each, 'gx_1', SWAP)]
    ppermute x4 -> x7, starting transfers between devices: 8.2 us -> 24.5 us  [the longest x4 14.5 us: local(): lax.ppermute(each, 'gx_1', SWAP)]
    all_to_all x1, blocking collectives: 38.6 us -> 35.9 us  [local(): lax.all_to_all(jnp.broadcast_to(sums, (128, 1, 128)), ('gy', 'gz'), 0, 0,...]
    pallas_call x1 -> x0, Pallas kernels: 2.15 us -> none  [join(): pl.pallas_call(join_kernel, out_shape=jax.ShapeDtypeStruct((16, ROWS, 128...]
    ppermute x1, waiting for transfers between devices: 0.55 us -> 2.49 us  [local(): near = lax.ppermute(own, ('gx_1', 'gy'), both_ways(16, 1))]
    pallas_call x1, Pallas kernels: 1.76 us -> 0.39 us  [make_rhs(): pl.pallas_call(rhs_kernel, out_shape=(jax.ShapeDtypeStruct((BX, BY, BZ),...]
    unnamed x16 -> x8, local copies, waits for them, and re-layouts: 1.75 us -> 2.94 us
  transfers between devices with their start and end apart: 6 -> 9, of which waited for: 4 -> 2; matrix products, arithmetic and copies ran while one was open for 0% -> 0% of each run, Pallas kernels for 0% -> 0%
where the time goes in v3:
time: 117 us; the launch traced here: 116 us
  blocking collectives  55.9 us (48%)
  starting transfers between devices  34.8 us (30%)
  Pallas kernels  17.7 us (15%)
  waiting for transfers between devices  3.82 us (3%)
  local copies, waits for them, and re-layouts  2.98 us (3%)
    all_to_all x1, blocking collectives, local(): lax.all_to_all(jnp.broadcast_to(sums, (128, 1, 128)), ('gy', 'gz'), 0, 0,...  35.9 us
    pallas_call x1, Pallas kernels, cycles(): pl.pallas_call(cycles_kernel, out_shape=jax.ShapeDtypeStruct((4, BX * BY...  16.3 us
    ppermute x4, starting transfers between devices, local(): lax.ppermute(each, 'gx_1', SWAP)  14.5 us
    all_to_all x1, blocking collectives, local(): own = lax.all_to_all(packed, GX, 0, 0, tiled=True).reshape(16, BY, 128)  10.2 us
    all_to_all x1, blocking collectives, local(): fields = lax.all_to_all(packed, 'gx_0', 0, 0, tiled=True)  9.8 us
    ppermute x1, starting transfers between devices, local(): down = lax.ppermute(rows, Z_AXES, z_pairs((-1, -1)))  6.15 us
    ppermute x1, starting transfers between devices, local(): far = lax.ppermute(own, ('gx_1', 'gy'), both_ways(16, 2))  6.08 us
    ppermute x1, starting transfers between devices, local(): near = lax.ppermute(own, ('gx_1', 'gy'), both_ways(16, 1))  4.28 us
  transfers between devices with their start and end apart: 9, of which 2 were waited for; matrix products, arithmetic and copies ran while one was open for 0% of the time, Pallas kernels for 0%

profile of v3, /device:TPU:8, one launch (start us, length us, event | category | flops | bytes accessed | tf_op | source)
XLA Modules:
  0.0 116.0 jit_solution(14441837787841843993)
XLA Ops:
  0.6 0.0 copy-start
  0.6 0.8 copy-done
  1.5 0.0 copy-start.1
  1.5 0.7 copy-done.1
  2.2 0.0 copy-start.2
  2.2 0.7 copy-done.2
  2.9 0.0 copy-start.3
  2.9 0.7 copy-done.3
  3.6 0.4 shard_map.59
  4.0 10.2 %all_to_all.15 = f32[8,2,16,128]{3,2,1,0:T(8,128)S(1)} all-to-all(f32[8,2,16,128]{3,2,1,0:T(8,128)S(1)} %get-tuple-element.5), channel_id=1, replica_groups=mesh['gx_0'=4,'gx_1'=2,'gy'=16,'gz'=8] {'gx_0','gx_1'}, dimensions={0} | all-to-all | bytes 262144 | tf_op jit(solution)/shard_map/all_to_all | solution.py:499
  14.2 6.1 %collective-permute-start.3 = (f32[16,16,128]{2,1,0:T(8,128)S(1)}, f32[16,16,128]{2,1,0:T(8,128)S(1)}, u32[]{:S(2)}, u32[]{:S(2)}) collective-permute-start(f32[16,16,128]{2,1,0:T(8,128)S(1)} %bitcast.4), channel_id=1, source_target_pairs={{0,16},{8,24},{16,32},{24,40},{32,48},{40,56},{48,64},{56,72},{64,... | collective-permute-start | bytes 393224 | tf_op jit(solution)/shard_map/ppermute | solution.py:501
  20.3 4.3 %collective-permute-start.2 = (f32[16,16,128]{2,1,0:T(8,128)S(1)}, f32[16,16,128]{2,1,0:T(8,128)S(1)}, u32[]{:S(2)}, u32[]{:S(2)}) collective-permute-start(f32[16,16,128]{2,1,0:T(8,128)S(1)} %bitcast.5), channel_id=1, source_target_pairs={{0,8},{8,16},{16,24},{24,32},{32,40},{40,48},{48,56},{56,64},{64,7... | collective-permute-start | bytes 393224 | tf_op jit(solution)/shard_map/ppermute | solution.py:500
  24.6 0.0 collective-permute-done.3
  24.6 2.5 %collective-permute-done.2 = f32[16,16,128]{2,1,0:T(8,128)S(1)} collective-permute-done((f32[16,16,128]{2,1,0:T(8,128)S(1)}, f32[16,16,128]{2,1,0:T(8,128)S(1)}, u32[]{:S(2)}, u32[]{:S(2)}) %collective-permute-start.2) | collective-permute-done | bytes 131104 | tf_op jit(solution)/shard_map/ppermute | solution.py:500
  27.1 6.2 %collective-permute-start.7 = (f32[2,16,16,128]{3,2,1,0:T(8,128)S(1)}, f32[2,16,16,128]{3,2,1,0:T(8,128)S(1)}, u32[]{:S(2)}, u32[]{:S(2)}) collective-permute-start(f32[2,16,16,128]{3,2,1,0:T(8,128)S(1)} %pad_maximum_fusion.rows_), channel_id=1, source_target_pairs={{256,0},{512,256},{768,512},{1,768},{257,1},{513,257},{769,513},{2... | collective-permute-start | bytes 786440 | tf_op jit(solution)/shard_map/ppermute | solution.py:505
  33.2 1.9 %collective-permute-start.5 = (f32[2,16,16,128]{3,2,1,0:T(8,128)S(1)}, f32[2,16,16,128]{3,2,1,0:T(8,128)S(1)}, u32[]{:S(2)}, u32[]{:S(2)}) collective-permute-start(f32[2,16,16,128]{3,2,1,0:T(8,128)S(1)} %pad_maximum_fusion.rows_), channel_id=1, source_target_pairs={{0,256},{256,512},{512,768},{768,1},{1,257},{257,513},{513,769},{7... | collective-permute-start | bytes 786440 | tf_op jit(solution)/shard_map/ppermute | solution.py:504
  35.2 1.9 %collective-permute-start = (f32[16,16,128]{2,1,0:T(8,128)S(1)}, f32[16,16,128]{2,1,0:T(8,128)S(1)}, u32[]{:S(2)}, u32[]{:S(2)}) collective-permute-start(f32[16,16,128]{2,1,0:T(8,128)S(1)} %bitcast.6), channel_id=1, source_target_pairs={{0,256},{256,512},{512,768},{768,1},{1,257},{257,513},{513,769},{7... | collective-permute-start | bytes 393224 | tf_op jit(solution)/shard_map/ppermute | solution.py:502
  37.1 7.7 %collective-permute-start.4 = (f32[2,16,16,128]{3,2,1,0:T(8,128)S(1)}, f32[2,16,16,128]{3,2,1,0:T(8,128)S(1)}, u32[]{:S(2)}, u32[]{:S(2)}) collective-permute-start(f32[2,16,16,128]{3,2,1,0:T(8,128)S(1)} %pad_maximum_fusion.rows_), channel_id=1, source_target_pairs={{0,128},{128,0},{1,129},{129,1},{2,130},{130,2},{3,131},{131,3},{4... | collective-permute-start | bytes 786440 | tf_op jit(solution)/shard_map/ppermute | solution.py:506
  44.8 0.0 collective-permute-done.7.down
  44.8 1.9 %collective-permute-start.8 = (f32[2,16,16,128]{3,2,1,0:T(8,128)S(1)}, f32[2,16,16,128]{3,2,1,0:T(8,128)S(1)}, u32[]{:S(2)}, u32[]{:S(2)}) collective-permute-start(f32[2,16,16,128]{3,2,1,0:T(8,128)S(1)} %collective-permute-done.7.down), channel_id=1, source_target_pairs={{0,128},{128,0},{1,129},{129,1},{2,130},{130,2},{3,131},{131,3},{4... | collective-permute-start | bytes 786440 | tf_op jit(solution)/shard_map/ppermute | solution.py:506
  46.7 0.0 collective-permute-done.5.up
  46.7 3.0 %collective-permute-start.6 = (f32[2,16,16,128]{3,2,1,0:T(8,128)S(1)}, f32[2,16,16,128]{3,2,1,0:T(8,128)S(1)}, u32[]{:S(2)}, u32[]{:S(2)}) collective-permute-start(f32[2,16,16,128]{3,2,1,0:T(8,128)S(1)} %collective-permute-done.5.up), channel_id=1, source_target_pairs={{0,128},{128,0},{1,129},{129,1},{2,130},{130,2},{3,131},{131,3},{4... | collective-permute-start | bytes 786440 | tf_op jit(solution)/shard_map/ppermute | solution.py:506
  49.7 0.0 collective-permute-done.side
  49.7 1.9 %collective-permute-start.1 = (f32[16,16,128]{2,1,0:T(8,128)S(1)}, f32[16,16,128]{2,1,0:T(8,128)S(1)}, u32[]{:S(2)}, u32[]{:S(2)}) collective-permute-start(f32[16,16,128]{2,1,0:T(8,128)S(1)} %collective-permute-done.side), channel_id=1, source_target_pairs={{0,128},{128,0},{1,129},{129,1},{2,130},{130,2},{3,131},{131,3},{4... | collective-permute-start | bytes 393224 | tf_op jit(solution)/shard_map/ppermute | solution.py:506
  51.6 1.3 %collective-permute-done.1.side2 = f32[16,16,128]{2,1,0:T(8,128)S(1)} collective-permute-done((f32[16,16,128]{2,1,0:T(8,128)S(1)}, f32[16,16,128]{2,1,0:T(8,128)S(1)}, u32[]{:S(2)}, u32[]{:S(2)}) %collective-permute-start.1) | collective-permute-done | bytes 131104 | tf_op jit(solution)/shard_map/ppermute | solution.py:506
  52.9 0.0 collective-permute-done.4.rows2
  52.9 0.0 collective-permute-done.8.down2
  52.9 0.0 collective-permute-done.6.up2
  52.9 16.3 %shard_map.60 = f32[4,136,128]{2,1,0:T(8,128)S(1)} custom-call(f32[16,16,128]{2,1,0:T(8,128)S(1)} %bitcast.7, f32[16,16,128]{2,1,0:T(8,128)S(1)} %collective-permute-done.side, f32[16,16,128]{2,1,0:T(8,128)S(1)} %collective-permute-done.1.side2, f32[2,16,16,128]{3,2,1,0:T(8,128)S(1)} %pad_maximum_fusion.rows_, ...), custom_call_target="tpu_custom_call" | custom-call | tf_op jit(solution)/shard_map/pallas_call | solution.py:431
  69.3 9.8 %all_to_all.16.fields = f32[4,136,128]{2,1,0:T(8,128)S(1)} all-to-all(f32[4,136,128]{2,1,0:T(8,128)S(1)} %shard_map.60), channel_id=1, replica_groups=mesh['gx_0'=4,'gx_1'=2,'gy'=16,'gz'=8] {'gx_0'}, dimensions={0} | all-to-all | bytes 557056 | tf_op jit(solution)/shard_map/all_to_all | solution.py:508
  79.2 35.9 %all_to_all.17 = f32[128,1,128]{2,1,0:T(1,128)S(1)} all-to-all(f32[128,1,128]{2,1,0:T(1,128)S(1)} %broadcast_in_dim.3), channel_id=1, replica_groups=mesh['gx_0'=4,'gx_1'=2,'gy'=16,'gz'=8] {'gy','gz'}, dimensions={0} | all-to-all | bytes 131072 | tf_op jit(solution)/shard_map/all_to_all | solution.py:510
  115.0 0.9 shard_map.61
  (3 shorter events, 0.1 us)
Async XLA Ops:
  0.6 0.8 copy-start
  1.5 0.7 copy-start.1
  2.2 0.7 copy-start.2
  2.9 0.7 copy-start.3
  14.2 10.4 %collective-permute-start.3 = (f32[16,16,128]{2,1,0:T(8,128)S(1)}, f32[16,16,128]{2,1,0:T(8,128)S(1)}, u32[]{:S(2)}, u32[]{:S(2)}) collective-permute-start(f32[16,16,128]{2,1,0:T(8,128)S(1)} %bitcast.4), channel_id=1, source_target_pairs={{0,16},{8,24},{16,32},{24,40},{32,48},{40,56},{48,64},{56,72},{64,... | collective-permute-start | bytes 393224 | tf_op jit(solution)/shard_map/ppermute | solution.py:501
  20.3 6.8 %collective-permute-start.2 = (f32[16,16,128]{2,1,0:T(8,128)S(1)}, f32[16,16,128]{2,1,0:T(8,128)S(1)}, u32[]{:S(2)}, u32[]{:S(2)}) collective-permute-start(f32[16,16,128]{2,1,0:T(8,128)S(1)} %bitcast.5), channel_id=1, source_target_pairs={{0,8},{8,16},{16,24},{24,32},{32,40},{40,48},{48,56},{56,64},{64,7... | collective-permute-start | bytes 393224 | tf_op jit(solution)/shard_map/ppermute | solution.py:500
  27.1 17.7 %collective-permute-start.7 = (f32[2,16,16,128]{3,2,1,0:T(8,128)S(1)}, f32[2,16,16,128]{3,2,1,0:T(8,128)S(1)}, u32[]{:S(2)}, u32[]{:S(2)}) collective-permute-start(f32[2,16,16,128]{3,2,1,0:T(8,128)S(1)} %pad_maximum_fusion.rows_), channel_id=1, source_target_pairs={{256,0},{512,256},{768,512},{1,768},{257,1},{513,257},{769,513},{2... | collective-permute-start | bytes 786440 | tf_op jit(solution)/shard_map/ppermute | solution.py:505
  33.2 13.5 %collective-permute-start.5 = (f32[2,16,16,128]{3,2,1,0:T(8,128)S(1)}, f32[2,16,16,128]{3,2,1,0:T(8,128)S(1)}, u32[]{:S(2)}, u32[]{:S(2)}) collective-permute-start(f32[2,16,16,128]{3,2,1,0:T(8,128)S(1)} %pad_maximum_fusion.rows_), channel_id=1, source_target_pairs={{0,256},{256,512},{512,768},{768,1},{1,257},{257,513},{513,769},{7... | collective-permute-start | bytes 786440 | tf_op jit(solution)/shard_map/ppermute | solution.py:504
  35.2 14.5 %collective-permute-start = (f32[16,16,128]{2,1,0:T(8,128)S(1)}, f32[16,16,128]{2,1,0:T(8,128)S(1)}, u32[]{:S(2)}, u32[]{:S(2)}) collective-permute-start(f32[16,16,128]{2,1,0:T(8,128)S(1)} %bitcast.6), channel_id=1, source_target_pairs={{0,256},{256,512},{512,768},{768,1},{1,257},{257,513},{513,769},{7... | collective-permute-start | bytes 393224 | tf_op jit(solution)/shard_map/ppermute | solution.py:502
  37.1 15.8 %collective-permute-start.4 = (f32[2,16,16,128]{3,2,1,0:T(8,128)S(1)}, f32[2,16,16,128]{3,2,1,0:T(8,128)S(1)}, u32[]{:S(2)}, u32[]{:S(2)}) collective-permute-start(f32[2,16,16,128]{3,2,1,0:T(8,128)S(1)} %pad_maximum_fusion.rows_), channel_id=1, source_target_pairs={{0,128},{128,0},{1,129},{129,1},{2,130},{130,2},{3,131},{131,3},{4... | collective-permute-start | bytes 786440 | tf_op jit(solution)/shard_map/ppermute | solution.py:506
  44.8 8.2 %collective-permute-start.8 = (f32[2,16,16,128]{3,2,1,0:T(8,128)S(1)}, f32[2,16,16,128]{3,2,1,0:T(8,128)S(1)}, u32[]{:S(2)}, u32[]{:S(2)}) collective-permute-start(f32[2,16,16,128]{3,2,1,0:T(8,128)S(1)} %collective-permute-done.7.down), channel_id=1, source_target_pairs={{0,128},{128,0},{1,129},{129,1},{2,130},{130,2},{3,131},{131,3},{4... | collective-permute-start | bytes 786440 | tf_op jit(solution)/shard_map/ppermute | solution.py:506
  46.7 6.2 %collective-permute-start.6 = (f32[2,16,16,128]{3,2,1,0:T(8,128)S(1)}, f32[2,16,16,128]{3,2,1,0:T(8,128)S(1)}, u32[]{:S(2)}, u32[]{:S(2)}) collective-permute-start(f32[2,16,16,128]{3,2,1,0:T(8,128)S(1)} %collective-permute-done.5.up), channel_id=1, source_target_pairs={{0,128},{128,0},{1,129},{129,1},{2,130},{130,2},{3,131},{131,3},{4... | collective-permute-start | bytes 786440 | tf_op jit(solution)/shard_map/ppermute | solution.py:506
  49.7 3.2 %collective-permute-start.1 = (f32[16,16,128]{2,1,0:T(8,128)S(1)}, f32[16,16,128]{2,1,0:T(8,128)S(1)}, u32[]{:S(2)}, u32[]{:S(2)}) collective-permute-start(f32[16,16,128]{2,1,0:T(8,128)S(1)} %collective-permute-done.side), channel_id=1, source_target_pairs={{0,128},{128,0},{1,129},{129,1},{2,130},{130,2},{3,131},{131,3},{4... | collective-permute-start | bytes 393224 | tf_op jit(solution)/shard_map/ppermute | solution.py:506

commit v4 on v3

--- a/solution.py
+++ b/solution.py
@@ -102,7 +102,7 @@
         scratch_shapes=[pltpu.VMEM((4, 2, BY, BZ), jnp.float32)]
         + [pltpu.VMEM(a.shape, a.dtype) for a in (density, xf, yf, zf)]
         + [pltpu.SemaphoreType.DMA((4,))],
-        compiler_params=small(),
+        compiler_params=pltpu.CompilerParams(vmem_limit_bytes=60 * 1024 * 1024),
     )(density, xf, yf, zf)
 
 
@@ -284,7 +284,7 @@
     return result
 
 
-def cycles_kernel(own, side, side2, rows_, rows2, up, up2, down, down2, out, r0, z0, q0, w, v0, f1, v1, e1, f2, t2, e2, mask):
+def cycles_kernel(own, beside, rows_, up, down, out, r0, z0, q0, w, v0, f1, v1, e1, f2, t2, e2, mask):
     gx0, core, gy, gz = place()
     rows, lanes = row_index((24, LANES)), lane_index((24, LANES))
     y = gy * BY - HY + 4 * rows
@@ -320,20 +320,17 @@
     lax.fori_loop(1, NX // 4 + 1, edges2, 0, unroll=8)
     lanes = lane_index((8, LANES))
 
-    def unpack(low_side, high_side, low_rows, high_rows, low_up, high_up, low_down, high_down):
-        blocks = (
-            (low_up, low_rows, low_down, 1),
-            (low_up, low_rows, low_down, 0),
-            (low_side, own, high_side, None),
-            (high_up, high_rows, high_down, 0),
-            (high_up, high_rows, high_down, 1),
-        )
+    def unpack():
+        blocks = [(up, rows_, down, at) for at in ((0, 1), (0, 0), None, (1, 0), (1, 1))]
 
         def body(i, _):
-            for b, (left, middle, right, pair) in enumerate(blocks):
+            for b, (left, middle, right, which) in enumerate(blocks):
                 for parity in range(2):
                     at = pl.ds(8 * parity, 8)
-                    a, c, d = ((ref[i, at] if pair is None else ref[pair, i, at]) for ref in (left, middle, right))
+                    if which is None:
+                        a, c, d = beside[0, i, at], own[i, at], beside[1, i, at]
+                    else:
+                        a, c, d = (ref[which + (i, at)] for ref in (left, middle, right))
                     for k in range(4):
                         value = jnp.where(lanes < 32, roll(a, -32 * k, 1), jnp.where(lanes < 64, roll(c, 32 - 32 * k, 1), roll(d, 64 - 32 * k, 1)))
                         x = 4 * i + k + 1
@@ -355,14 +352,7 @@
 
         lax.fori_loop(0, NX // 4, body, 0)
 
-    @pl.when(core == 0)
-    def _():
-        unpack(side, side2, rows_, rows2, up, up2, down, down2)
-
-    @pl.when(core == 1)
-    def _():
-        unpack(side2, side, rows2, rows_, up2, up, down2, down)
-
+    unpack()
     low = {step: lanes & step == 0 for step in (1, 2)}
 
     def fold(x, step):
@@ -431,7 +421,7 @@
     return pl.pallas_call(
         cycles_kernel,
         out_shape=jax.ShapeDtypeStruct((4, BX * BY + 8, LANES), jnp.float32),
-        in_specs=[VMEM] * 9,
+        in_specs=[VMEM] * 5,
         out_specs=VMEM,
         scratch_shapes=[fine] * 5 + [level1, level1, pltpu.VMEM((NX // 2 + 2, 40, LANES), jnp.float32)] + [level2] * 3 + [pltpu.VMEM((24, LANES), jnp.float32)],
         compiler_params=pltpu.CompilerParams(vmem_limit_bytes=30 * 1024 * 1024),
@@ -490,7 +480,6 @@
     return [(number(core, a), number(core, a + step)) for core, step in enumerate(steps) for a in range(32) if 0 <= a + step < 32]
 
 
-SWAP = [(0, 1), (1, 0)]
 Z_AXES = ("gx_0", "gx_1", "gz")
 
 
@@ -503,8 +492,7 @@
     rows = jnp.stack([near, far])
     up = lax.ppermute(rows, Z_AXES, z_pairs((1, 1)))
     down = lax.ppermute(rows, Z_AXES, z_pairs((-1, -1)))
-    swapped = [lax.ppermute(each, "gx_1", SWAP) for each in (side, rows, up, down)]
-    packed = cycles(own, side, swapped[0], rows, swapped[1], up, swapped[2], down, swapped[3])
+    packed = cycles(own, *(lax.all_gather(each, "gx_1") for each in (side, rows, up, down)))
     fields = lax.all_to_all(packed, "gx_0", 0, 0, tiled=True)
     sums = jnp.sum(fields[:, BX * BY, :], axis=0)
     sums = lax.all_to_all(jnp.broadcast_to(sums, (128, 1, 128)), ("gy", "gz"), 0, 0, tiled=True)

time: 117 us -> 113 us (0.966)
  starting transfers between devices: 34.8 us -> 21.6 us
  blocking collectives: 55.9 us -> 68.8 us
  local copies, waits for them, and re-layouts: 2.98 us -> 0.04 us
  waiting for transfers between devices: 3.82 us -> 1.92 us
  Pallas kernels: 17.7 us -> 19 us
    ppermute x4 -> x0, starting transfers between devices: 14.5 us -> none  [local(): lax.ppermute(each, 'gx_1', SWAP)]
    all_gather x0 -> x4, blocking collectives: none -> 11 us  [local(): lax.all_gather(each, 'gx_1')]
    unnamed x8 -> x2, local copies, waits for them, and re-layouts: 2.94 us -> 0.01 us
    ppermute x1, waiting for transfers between devices: 2.49 us -> 0.01 us  [local(): near = lax.ppermute(own, ('gx_1', 'gy'), both_ways(16, 1))]
    ppermute x1, waiting for transfers between devices: 0.01 us -> 1.9 us  [local(): up = lax.ppermute(rows, Z_AXES, z_pairs((1, 1)))]
    all_to_all x1, blocking collectives: 35.9 us -> 37.4 us  [local(): lax.all_to_all(jnp.broadcast_to(sums, (128, 1, 128)), ('gy', 'gz'), 0, 0,...]
    pallas_call x1, Pallas kernels: 0.39 us -> 1.77 us  [make_rhs(): pl.pallas_call(rhs_kernel, out_shape=(jax.ShapeDtypeStruct((BX, BY, BZ),...]
    ppermute x4 -> x0, waiting for transfers between devices: 1.32 us -> none  [local(): lax.ppermute(each, 'gx_1', SWAP)]
  transfers between devices with their start and end apart: 9 -> 5, of which waited for: 2 -> 1; matrix products, arithmetic and copies ran while one was open for 0% -> 0% of each run, Pallas kernels for 0% -> 0%
where the time goes in v4:
time: 113 us; the launch traced here: 112 us
  blocking collectives  68.8 us (61%)
  starting transfers between devices  21.6 us (19%)
  Pallas kernels  19 us (17%)
  waiting for transfers between devices  1.92 us (2%)
    all_to_all x1, blocking collectives, local(): lax.all_to_all(jnp.broadcast_to(sums, (128, 1, 128)), ('gy', 'gz'), 0, 0,...  37.4 us
    pallas_call x1, Pallas kernels, cycles(): pl.pallas_call(cycles_kernel, out_shape=jax.ShapeDtypeStruct((4, BX * BY...  16.3 us
    all_gather x4, blocking collectives, local(): lax.all_gather(each, 'gx_1')  11 us
    all_to_all x1, blocking collectives, local(): own = lax.all_to_all(packed, GX, 0, 0, tiled=True).reshape(16, BY, 128)  10.4 us
    all_to_all x1, blocking collectives, local(): fields = lax.all_to_all(packed, 'gx_0', 0, 0, tiled=True)  10 us
    ppermute x1, starting transfers between devices, local(): down = lax.ppermute(rows, Z_AXES, z_pairs((-1, -1)))  6.87 us
    ppermute x1, starting transfers between devices, local(): far = lax.ppermute(own, ('gx_1', 'gy'), both_ways(16, 2))  6.08 us
    ppermute x1, starting transfers between devices, local(): near = lax.ppermute(own, ('gx_1', 'gy'), both_ways(16, 1))  4.28 us
  transfers between devices with their start and end apart: 5, of which 1 were waited for; matrix products, arithmetic and copies ran while one was open for 0% of the time, Pallas kernels for 0%

profile of v4, /device:TPU:8, one launch (start us, length us, event | category | flops | bytes accessed | tf_op | source)
XLA Modules:
  0.0 112.2 jit_solution(15832221705454077703)
XLA Ops:
  0.6 1.8 %shard_map.59 = (f32[8,16,128]{2,1,0:T(8,128)}, f32[8,2,16,128]{3,2,1,0:T(8,128)}) custom-call(f32[8,16,128]{2,1,0:T(8,128)} %density_in.1, f32[2,16,128]{2,1,0:T(8,128)} %xf_in.1, f32[2,8,128]{2,1,0:T(8,128)} %yf_in.1, f32[2,8,16]{2,1,0:T(8,128)} %zf_in.1), custom_call_target="tpu_custom_call" | custom-call | tf_op jit(solution)/shard_map/pallas_call | solution.py:94
  2.4 10.4 %all_to_all.15 = f32[8,2,16,128]{3,2,1,0:T(8,128)S(1)} all-to-all(f32[8,2,16,128]{3,2,1,0:T(8,128)} %get-tuple-element.5), channel_id=1, replica_groups=mesh['gx_0'=4,'gx_1'=2,'gy'=16,'gz'=8] {'gx_0','gx_1'}, dimensions={0} | all-to-all | bytes 262144 | tf_op jit(solution)/shard_map/all_to_all | solution.py:488
  12.8 6.1 %collective-permute-start.2 = (f32[16,16,128]{2,1,0:T(8,128)S(1)}, f32[16,16,128]{2,1,0:T(8,128)S(1)}, u32[]{:S(2)}, u32[]{:S(2)}) collective-permute-start(f32[16,16,128]{2,1,0:T(8,128)S(1)} %bitcast.12), channel_id=1, source_target_pairs={{0,16},{8,24},{16,32},{24,40},{32,48},{40,56},{48,64},{56,72},{64,... | collective-permute-start | bytes 393224 | tf_op jit(solution)/shard_map/ppermute | solution.py:490
  18.9 4.3 %collective-permute-start.1 = (f32[16,16,128]{2,1,0:T(8,128)S(1)}, f32[16,16,128]{2,1,0:T(8,128)S(1)}, u32[]{:S(2)}, u32[]{:S(2)}) collective-permute-start(f32[16,16,128]{2,1,0:T(8,128)S(1)} %bitcast.13), channel_id=1, source_target_pairs={{0,8},{8,16},{16,24},{24,32},{32,40},{40,48},{48,56},{56,64},{64,7... | collective-permute-start | bytes 393224 | tf_op jit(solution)/shard_map/ppermute | solution.py:489
  23.2 2.5 %collective-permute-start = (f32[16,16,128]{2,1,0:T(8,128)S(1)}, f32[16,16,128]{2,1,0:T(8,128)S(1)}, u32[]{:S(2)}, u32[]{:S(2)}) collective-permute-start(f32[16,16,128]{2,1,0:T(8,128)S(1)} %bitcast.14), channel_id=1, source_target_pairs={{0,256},{256,512},{512,768},{768,1},{1,257},{257,513},{513,769},{7... | collective-permute-start | bytes 393224 | tf_op jit(solution)/shard_map/ppermute | solution.py:491
  25.7 0.0 collective-permute-done.2
  25.7 0.0 collective-permute-done.1
  25.7 6.9 %collective-permute-start.4 = (f32[2,16,16,128]{3,2,1,0:T(8,128)S(1)}, f32[2,16,16,128]{3,2,1,0:T(8,128)S(1)}, u32[]{:S(2)}, u32[]{:S(2)}) collective-permute-start(f32[2,16,16,128]{3,2,1,0:T(8,128)S(1)} %pad_maximum_fusion), channel_id=1, source_target_pairs={{256,0},{512,256},{768,512},{1,768},{257,1},{513,257},{769,513},{2... | collective-permute-start | bytes 786440 | tf_op jit(solution)/shard_map/ppermute | solution.py:494
  32.6 1.9 %collective-permute-start.3 = (f32[2,16,16,128]{3,2,1,0:T(8,128)S(1)}, f32[2,16,16,128]{3,2,1,0:T(8,128)S(1)}, u32[]{:S(2)}, u32[]{:S(2)}) collective-permute-start(f32[2,16,16,128]{3,2,1,0:T(8,128)S(1)} %pad_maximum_fusion), channel_id=1, source_target_pairs={{0,256},{256,512},{512,768},{768,1},{1,257},{257,513},{513,769},{7... | collective-permute-start | bytes 786440 | tf_op jit(solution)/shard_map/ppermute | solution.py:493
  34.5 0.0 collective-permute-done
  34.5 3.8 %all-gather = f32[32,16,128]{2,1,0:T(8,128)S(1)} all-gather(f32[16,16,128]{2,1,0:T(8,128)S(1)} %collective-permute-done), channel_id=2, replica_groups=mesh['gx_0'=4,'gx_1'=2,'gy'=16,'gz'=8] {'gx_1'}, dimensions={0}, use_global_device_ids=true | all-gather | bytes 393216 | tf_op jit(solution)/shard_map/all_gather | solution.py:495
  38.3 2.2 %all-gather.1 = f32[4,16,16,128]{3,2,1,0:T(8,128)S(1)} all-gather(f32[2,16,16,128]{3,2,1,0:T(8,128)S(1)} %pad_maximum_fusion), channel_id=3, replica_groups=mesh['gx_0'=4,'gx_1'=2,'gy'=16,'gz'=8] {'gx_1'}, dimensions={0}, use_global_device_ids=true | all-gather | bytes 786432 | tf_op jit(solution)/shard_map/all_gather | solution.py:495
  40.5 0.0 collective-permute-done.4
  40.5 2.2 %all-gather.3 = f32[4,16,16,128]{3,2,1,0:T(8,128)S(1)} all-gather(f32[2,16,16,128]{3,2,1,0:T(8,128)S(1)} %collective-permute-done.4), channel_id=5, replica_groups=mesh['gx_0'=4,'gx_1'=2,'gy'=16,'gz'=8] {'gx_1'}, dimensions={0}, use_global_device_ids=true | all-gather | bytes 786432 | tf_op jit(solution)/shard_map/all_gather | solution.py:495
  42.7 1.9 %collective-permute-done.3 = f32[2,16,16,128]{3,2,1,0:T(8,128)S(1)} collective-permute-done((f32[2,16,16,128]{3,2,1,0:T(8,128)S(1)}, f32[2,16,16,128]{3,2,1,0:T(8,128)S(1)}, u32[]{:S(2)}, u32[]{:S(2)}) %collective-permute-start.3) | collective-permute-done | bytes 262176 | tf_op jit(solution)/shard_map/ppermute | solution.py:493
  44.6 2.8 %all-gather.2 = f32[4,16,16,128]{3,2,1,0:T(8,128)S(1)} all-gather(f32[2,16,16,128]{3,2,1,0:T(8,128)S(1)} %collective-permute-done.3), channel_id=4, replica_groups=mesh['gx_0'=4,'gx_1'=2,'gy'=16,'gz'=8] {'gx_1'}, dimensions={0}, use_global_device_ids=true | all-gather | bytes 786432 | tf_op jit(solution)/shard_map/all_gather | solution.py:495
  47.4 16.3 %shard_map.60 = f32[4,136,128]{2,1,0:T(8,128)S(1)} custom-call(f32[16,16,128]{2,1,0:T(8,128)S(1)} %bitcast.15, f32[2,16,16,128]{3,2,1,0:T(8,128)S(1)} %bitcast.11, f32[2,2,16,16,128]{4,3,2,1,0:T(8,128)S(1)} %bitcast.8, f32[2,2,16,16,128]{4,3,2,1,0:T(8,128)S(1)} %bitcast.10, f32[2,2,16,16,128]{4,3,2,1,0:T(8,128)S(1)} %bitcast.9), custom_call_target="tpu_custom_call" | custom-call | tf_op jit(solution)/shard_map/pallas_call | solution.py:421
  63.7 10.0 %all_to_all.16.fields = f32[4,136,128]{2,1,0:T(8,128)S(1)} all-to-all(f32[4,136,128]{2,1,0:T(8,128)S(1)} %shard_map.60), channel_id=1, replica_groups=mesh['gx_0'=4,'gx_1'=2,'gy'=16,'gz'=8] {'gx_0'}, dimensions={0} | all-to-all | bytes 557056 | tf_op jit(solution)/shard_map/all_to_all | solution.py:496
  73.8 0.0 copy-start
  73.8 37.4 %all_to_all.17 = f32[128,1,128]{2,1,0:T(1,128)S(1)} all-to-all(f32[128,1,128]{2,1,0:T(1,128)S(1)} %broadcast_in_dim.3), channel_id=1, replica_groups=mesh['gx_0'=4,'gx_1'=2,'gy'=16,'gz'=8] {'gy','gz'}, dimensions={0} | all-to-all | bytes 131072 | tf_op jit(solution)/shard_map/all_to_all | solution.py:498
  111.3 0.0 copy-done
  111.3 0.9 shard_map.61
  (3 shorter events, 0.1 us)
Async XLA Ops:
  12.8 12.9 %collective-permute-start.2 = (f32[16,16,128]{2,1,0:T(8,128)S(1)}, f32[16,16,128]{2,1,0:T(8,128)S(1)}, u32[]{:S(2)}, u32[]{:S(2)}) collective-permute-start(f32[16,16,128]{2,1,0:T(8,128)S(1)} %bitcast.12), channel_id=1, source_target_pairs={{0,16},{8,24},{16,32},{24,40},{32,48},{40,56},{48,64},{56,72},{64,... | collective-permute-start | bytes 393224 | tf_op jit(solution)/shard_map/ppermute | solution.py:490
  18.9 6.8 %collective-permute-start.1 = (f32[16,16,128]{2,1,0:T(8,128)S(1)}, f32[16,16,128]{2,1,0:T(8,128)S(1)}, u32[]{:S(2)}, u32[]{:S(2)}) collective-permute-start(f32[16,16,128]{2,1,0:T(8,128)S(1)} %bitcast.13), channel_id=1, source_target_pairs={{0,8},{8,16},{16,24},{24,32},{32,40},{40,48},{48,56},{56,64},{64,7... | collective-permute-start | bytes 393224 | tf_op jit(solution)/shard_map/ppermute | solution.py:489
  23.2 11.3 %collective-permute-start = (f32[16,16,128]{2,1,0:T(8,128)S(1)}, f32[16,16,128]{2,1,0:T(8,128)S(1)}, u32[]{:S(2)}, u32[]{:S(2)}) collective-permute-start(f32[16,16,128]{2,1,0:T(8,128)S(1)} %bitcast.14), channel_id=1, source_target_pairs={{0,256},{256,512},{512,768},{768,1},{1,257},{257,513},{513,769},{7... | collective-permute-start | bytes 393224 | tf_op jit(solution)/shard_map/ppermute | solution.py:491
  25.7 14.8 %collective-permute-start.4 = (f32[2,16,16,128]{3,2,1,0:T(8,128)S(1)}, f32[2,16,16,128]{3,2,1,0:T(8,128)S(1)}, u32[]{:S(2)}, u32[]{:S(2)}) collective-permute-start(f32[2,16,16,128]{3,2,1,0:T(8,128)S(1)} %pad_maximum_fusion), channel_id=1, source_target_pairs={{256,0},{512,256},{768,512},{1,768},{257,1},{513,257},{769,513},{2... | collective-permute-start | bytes 786440 | tf_op jit(solution)/shard_map/ppermute | solution.py:494
  32.6 12.0 %collective-permute-start.3 = (f32[2,16,16,128]{3,2,1,0:T(8,128)S(1)}, f32[2,16,16,128]{3,2,1,0:T(8,128)S(1)}, u32[]{:S(2)}, u32[]{:S(2)}) collective-permute-start(f32[2,16,16,128]{3,2,1,0:T(8,128)S(1)} %pad_maximum_fusion), channel_id=1, source_target_pairs={{0,256},{256,512},{512,768},{768,1},{1,257},{257,513},{513,769},{7... | collective-permute-start | bytes 786440 | tf_op jit(solution)/shard_map/ppermute | solution.py:493
  73.8 37.4 %copy-start = (f32[8,16,128]{2,1,0:T(8,128)S(1)}, f32[8,16,128]{2,1,0:T(8,128)}, u32[]{:S(2)}) copy-start(f32[8,16,128]{2,1,0:T(8,128)} %get-tuple-element.4.rhs) | copy-start | bytes 196612

commit v5 on v4

v5 whole, which is shorter than its diff:
```python
import functools

import jax
import jax.numpy as jnp
from jax import lax
from jax.experimental import pallas as pl
from jax.experimental.pallas import tpu as pltpu
from jax.sharding import Mesh
from jax.sharding import PartitionSpec as P

AXES = ("gx_0", "gx_1", "gy", "gz")
GX = ("gx_0", "gx_1")
NX, NY, NZ = 64, 256, 1024
BX, BY, BZ = 8, 16, 128
CZ = 32
HY, HZ = 32, 32
ROWS, LANES = BY + 2 * HY, 128
relax = 1.0 / 9.0
coupling = 0.5
VMEM = pl.BlockSpec(memory_space=pltpu.VMEM)
HBM = pl.BlockSpec(memory_space=pltpu.MemorySpace.HBM)


def roll(x, shift, axis):
    return pltpu.roll(x, shift % x.shape[axis], axis)


def place():
    return tuple(lax.axis_index(axis) for axis in AXES)


def small(**more):
    return pltpu.CompilerParams(vmem_limit_bytes=4 * 1024 * 1024, **more)


def lane_index(shape):
    return lax.broadcasted_iota(jnp.int32, shape, 1)


def row_index(shape):
    return lax.broadcasted_iota(jnp.int32, shape, 0)


def rhs_kernel(density_in, xf_in, yf_in, zf_in, rhs, packed, scratch, density, xf, yf, zf, arrived):
    copies = [pltpu.make_async_copy(a, b, arrived.at[i]) for i, (a, b) in enumerate(((density_in, density), (xf_in, xf), (yf_in, yf), (zf_in, zf)))]
    for copy in copies:
        copy.start()
    gx0, core, gy, gz = place()
    gx = 2 * gx0 + core
    rows, lanes = row_index((BY, BZ)), lane_index((BY, BZ))
    eye = row_index((BY, BY)) == lane_index((BY, BY))
    low_y = (rows == 0) & (gy == 0)
    high_y = (rows == BY - 1) & (gy == NY // BY - 1)
    low_z = (lanes == 0) & (gz == 0)
    high_z = (lanes == BZ - 1) & (gz == NZ // BZ - 1)

    def column(row):
        return jnp.sum(jnp.where(eye, row, 0.0), axis=1, keepdims=True)

    for copy in copies:
        copy.wait()
    layers = []
    for x in range(BX):
        value = -coupling * density[x]
        if x == 0:
            value = value + jnp.where(gx == 0, xf[0], 0.0)
        if x == BX - 1:
            value = value + jnp.where(gx == NX // BX - 1, xf[1], 0.0)
        value = value + jnp.where(low_y, yf[0, x : x + 1, :], 0.0)
        value = value + jnp.where(high_y, yf[1, x : x + 1, :], 0.0)
        value = value + jnp.where(low_z, column(zf[0, x : x + 1, :]), 0.0)
        value = value + jnp.where(high_z, column(zf[1, x : x + 1, :]), 0.0)
        rhs[x] = value
        layers.append(value)
    for chunk in range(4):
        for quad in range(2):
            out = None
            for k in range(4):
                part = roll(layers[4 * quad + k], 32 * (k - chunk), 1)
                out = part if k == 0 else jnp.where(lanes >= 32 * k, part, out)
            scratch[chunk, quad] = out
    for chunk in range(4):
        for quad in range(2):
            for odd in range(2):
                part = scratch[chunk, quad, pl.ds(odd, 8, stride=2), :]
                packed[2 * chunk, quad, 8 * odd : 8 * odd + 8] = part
                packed[2 * chunk + 1, quad, 8 * odd : 8 * odd + 8] = part


def make_rhs(density, xf, yf, zf):
    return pl.pallas_call(
        rhs_kernel,
        out_shape=(
            jax.ShapeDtypeStruct((BX, BY, BZ), jnp.float32),
            jax.ShapeDtypeStruct((8, 2, BY, BZ), jnp.float32),
        ),
        in_specs=[HBM] * 4,
        out_specs=(VMEM, VMEM),
        scratch_shapes=[pltpu.VMEM((4, 2, BY, BZ), jnp.float32)]
        + [pltpu.VMEM(a.shape, a.dtype) for a in (density, xf, yf, zf)]
        + [pltpu.SemaphoreType.DMA((4,))],
        compiler_params=pltpu.CompilerParams(vmem_limit_bytes=60 * 1024 * 1024),
    )(density, xf, yf, zf)


def at(row, step=0):
    return pl.ds(8 + row + step, 8)


def every_other(row, step=0):
    return pl.ds(8 + 2 * row + step, 8, stride=2)


def sides(x, step):
    return roll(x, step, 1) + roll(x, -step, 1)


def third(x):
    return x * (1.0 / 3.0)


def chunks(count, size, body):
    size, unroll = size if isinstance(size, tuple) else (size, 1)
    if size == count:
        body(0)
    elif size * unroll == count:
        for i in range(unroll):
            body(i * size)
    else:
        lax.fori_loop(0, count // size, lambda i, _: body(i * size) or 0, 0, unroll=unroll)


def cycle_down(src, mask, mask2, fold, sum1, part1, f1, f2, rows1, rows2, size, nb):
    def gather(first, size=size):
        for r in rows1:
            layers = [2 * first + k for k in range(2 * size + 2)]
            cells = [src[x, 0, at(r)] + src[x, 1, at(r)] for x in layers]
            beyond = [src[x, 1, at(r, -1)] + src[x, 0, at(r, 1)] for x in layers[1:-1]]
            for i in range(size):
                before, a, b, after = cells[2 * i : 2 * i + 4]
                u = a + b
                y = beyond[2 * i] + beyond[2 * i + 1]
                sum1[first + i + 1, at(r)] = u
                part1[first + i + 1, at(r)] = third(u) + relax * (((u + u) + (before + after)) + y)

    chunks(NX // 2, size, gather)

    def across(first):
        for r in rows1:
            for x in [first + k for k in range(1, 32 + 1)]:
                f1[x, at(r)] = part1[x, at(r)] + relax * sides(sum1[x, at(r)], 1)

    chunks(NX // 2, 32, across)

    def level1(first):
        for r in rows1:
            m = mask[at(r)]
            for x in [first + k for k in range(1, 16 + 1)]:
                f1[x, at(r)] = fold(f1[x, at(r)], 1) * m

    chunks(NX // 2, 16, level1)

    def level2(first):
        for r in rows2:
            m = mask2[at(r)]
            layers = [2 * first + k for k in range(2 * nb + 2)]
            cells = [f1[x, every_other(r), :] + f1[x, every_other(r, 1), :] for x in layers]
            beyond = [f1[x, every_other(r, -1), :] + f1[x, every_other(r, 2), :] for x in layers[1:-1]]
            for i in range(nb):
                before, a, b, after = cells[2 * i : 2 * i + 4]
                u = a + b
                y = beyond[2 * i] + beyond[2 * i + 1]
                s = third(u) + relax * (((u + u) + (before + after)) + (y + sides(u, 2)))
                f2[first + i + 1, at(r)] = fold(s, 2) * m

    chunks(NX // 4, nb, level2)


def cycle_coarse(mask2, f2, t2, e2, rows, last):
    def around(ref, x, r):
        return (ref[x - 1, at(r)] + ref[x + 1, at(r)]) + (ref[x, at(r, -1)] + ref[x, at(r, 1)])

    def sweep1(first):
        for r in rows:
            m = mask2[at(r)]
            for x in range(1, 9):
                v = f2[first + x, at(r)]
                s = (4.0 / 3.0) * v + relax * (around(f2, first + x, r) + sides(v, 4))
                t2[first + x, at(r)] = (relax * s) * m

    chunks(NX // 4, 8, sweep1)

    def sweep2(first):
        for r in last:
            m = mask2[at(r)]
            for x in range(1, 9):
                v = t2[first + x, at(r)]
                s = (third(v) + relax * (f2[first + x, at(r)] + (around(t2, first + x, r) + sides(v, 4)))) * m
                e2[first + x, every_other(r), :] = s
                e2[first + x, every_other(r, 1), :] = s

    chunks(NX // 4, 8, sweep2)


def cycle_up(src, mask, f1, e2, v1, e1, v0, out, rows1, last1, rows0, last0, nd, ne):
    def correct1(first):
        for r in rows1:
            for i in range(4):
                e = e2[first + i + 1, at(r)]
                for k in (1, 2):
                    x = 2 * first + 2 * i + k
                    v1[x, at(r)] = relax * f1[x, at(r)] + e

    chunks(NX // 4, 4, correct1)

    def smooth1(first):
        for r in last1:
            m = mask[at(r)]
            for x in [first + k for k in range(1, nd + 1)]:
                v = v1[x, at(r)]
                y = v1[x, at(r, -1)] + v1[x, at(r, 1)]
                s = third(v) + relax * ((f1[x, at(r)] + (v1[x - 1, at(r)] + v1[x + 1, at(r)])) + (y + sides(v, 2)))
                e1[x, at(r)] = s * m

    chunks(NX // 2, nd, smooth1)

    def correct0(first):
        for odd in range(2):
            for r in rows0[odd]:
                for i in range(1, 5):
                    e = e1[first + i, at(r)]
                    for k in (-1, 0):
                        x = 2 * first + 2 * i + k
                        v0[x, odd, at(r)] = relax * src[x, odd, at(r)] + e

    chunks(NX // 2, 4, correct0)

    def smooth0(first):
        for odd in range(2):
            for r in last0[odd]:
                m = mask[at(r)]
                layers = [v0[first + k, odd, at(r)] for k in range(ne + 2)]
                for k in range(1, ne + 1):
                    x = first + k
                    v = layers[k]
                    y = v0[x, 1 - odd, at(r, odd - 1)] + v0[x, 1 - odd, at(r, odd)]
                    s = third(v) + relax * ((src[x, odd, at(r)] + (layers[k - 1] + layers[k + 1])) + (y + sides(v, 1)))
                    out[x, odd, at(r)] = s * m

    chunks(NX, ne, smooth0)


def images(src, first, odd, r, count):
    layers = [src[first + k, odd, at(r)] for k in range(count + 2)]
    result = []
    for k in range(1, count + 1):
        v = layers[k]
        y = src[first + k, 1 - odd, at(r, odd - 1)] + src[first + k, 1 - odd, at(r, odd)]
        result.append((v, 6.0 * v - ((layers[k - 1] + layers[k + 1]) + (y + sides(v, 1)))))
    return result


def cycles_kernel(own, beside, rows_, up, down, out, r0, z0, q0, w, v0, f1, v1, e1, e2, f2, t2, mask, mask2):
    gx0, core, gy, gz = place()

    def inside(count, height):
        rows, lanes = row_index((count, LANES)) - 8, lane_index((count, LANES))
        y = gy * BY - HY + height * rows
        z = (gz * 4 + gx0) * CZ - HZ + lanes
        return jnp.where((y >= 0) & (y < NY) & (z >= 0) & (z < NZ), 1.0, 0.0)

    mask[...] = inside(56, 2)
    mask2[...] = inside(40, 4)
    for ref, count in ((r0, NX), (z0, NX), (q0, NX), (w, NX), (v0, NX), (f1, NX // 2), (v1, NX // 2), (f2, NX // 4), (t2, NX // 4)):
        ref[0] = jnp.zeros(ref.shape[1:], jnp.float32)
        ref[count + 1] = jnp.zeros(ref.shape[1:], jnp.float32)
    lanes = lane_index((8, LANES))
    blocks = [(up, rows_, down, which) for which in ((0, 1), (0, 0), None, (1, 0), (1, 1))]

    def unpack(i, _):
        for b, (left, middle, right, which) in enumerate(blocks):
            for odd in range(2):
                part = pl.ds(8 * odd, 8)
                if which is None:
                    a, c, d = beside[0, i, part], own[i, part], beside[1, i, part]
                else:
                    a, c, d = (ref[which + (i, part)] for ref in (left, middle, right))
                for k in range(4):
                    value = jnp.where(lanes < 32, roll(a, -32 * k, 1), jnp.where(lanes < 64, roll(c, 32 - 32 * k, 1), roll(d, 64 - 32 * k, 1)))
                    r0[4 * i + k + 1, odd, at(8 * b)] = value
        return 0

    lax.fori_loop(0, NX // 4, unpack, 0, unroll=16)
    low = {step: lanes & step == 0 for step in (1, 2)}

    def fold(x, step):
        return 0.5 * (x + jnp.where(low[step], roll(x, -step, 1), roll(x, step, 1)))

    middle = (8, 16, 24)
    cycle_down(r0, mask, mask2, fold, v1, e1, f1, f2, (0, 8, 16, 24, 32), (0, 8, 12), 4, 8)
    cycle_coarse(mask2, f2, t2, e2, (0, 8, 12), (1, 9))
    cycle_up(r0, mask, f1, e2, v1, e1, v0, z0, (6, 14, 22, 26), (7, 15, 23, 25), ((8, 16, 24, 25), (7, 15, 23, 24)), (middle, middle), 32, 64)

    def image(first):
        for odd in range(2):
            for r in middle:
                m = mask[at(r)]
                for k, (_, value) in enumerate(images(z0, first, odd, r, 64)):
                    q0[first + k + 1, odd, at(r)] = value * m

    chunks(NX, 64, image)
    cycle_down(q0, mask, mask2, fold, v1, e1, f1, f2, middle, (5, 7), 8, 16)
    cycle_coarse(mask2, f2, t2, e2, (6,), (6,))
    cycle_up(q0, mask, f1, e2, v1, e1, v0, w, (14, 18), (15, 17), ((15, 17), (15, 17)), ((16, 17), (15, 16)), 32, 64)

    def sums(i, acc):
        acc = list(acc)
        for odd in range(2):
            for k, (ww, s) in enumerate(images(w, 64 * i, odd, 16, 64)):
                x = 64 * i + k + 1
                r, zz, q = r0[x, odd, at(16)], z0[x, odd, at(16)], q0[x, odd, at(16)]
                for n, term in enumerate((r * zz, zz * q, r * ww, q * ww, ww * s)):
                    acc[n] = acc[n] + term
                v0[x, odd, at(16)] = s
        return tuple(acc)

    acc = lax.fori_loop(0, NX // 64, sums, (jnp.zeros((8, LANES), jnp.float32),) * 5)

    def send(t, _):
        for k in range(BX):
            x = BX * (2 * t + core) + k + 1
            for odd in range(2):
                zz, q, ww, s = (ref[x, odd, at(16)] for ref in (z0, q0, w, v0))
                out[t, pl.ds(k * BY + 8 * odd, 8)] = jnp.where(
                    lanes < 32, roll(zz, -32, 1), jnp.where(lanes < 64, q, jnp.where(lanes < 96, roll(ww, 32, 1), roll(s, 64, 1)))
                )
        return 0

    lax.fori_loop(0, 4, send, 0, unroll=4)
    home = (lanes >= HZ) & (lanes < HZ + CZ)
    row = jnp.zeros((8, LANES), jnp.float32)
    for k, a in enumerate(acc):
        row = jnp.where(lanes == k, jnp.sum(jnp.where(home, a, 0.0)), row)
    for t in range(4):
        out[t, BX * BY : BX * BY + 8] = row


def cycles(*blocks):
    fine = pltpu.VMEM((NX + 2, 2, 56, LANES), jnp.float32)
    level1 = pltpu.VMEM((NX // 2 + 2, 56, LANES), jnp.float32)
    level2 = pltpu.VMEM((NX // 4 + 2, 40, LANES), jnp.float32)
    return pl.pallas_call(
        cycles_kernel,
        out_shape=jax.ShapeDtypeStruct((4, BX * BY + 8, LANES), jnp.float32),
        in_specs=[VMEM] * 5,
        out_specs=VMEM,
        scratch_shapes=[fine] * 5
        + [level1] * 3
        + [pltpu.VMEM((NX // 4 + 2, 56, LANES), jnp.float32), level2, level2, pltpu.VMEM((56, LANES), jnp.float32), pltpu.VMEM((40, LANES), jnp.float32)],
        compiler_params=pltpu.CompilerParams(vmem_limit_bytes=30 * 1024 * 1024),
    )(*blocks)


def finish_kernel(rhs, fields, sums, solution, residual):
    total = jnp.sum(sums[...], axis=0, keepdims=True)
    lanes = lane_index(total.shape)

    def pick(k):
        return jnp.sum(jnp.where(lanes == k, total, 0.0), axis=1, keepdims=True)

    rz, zq, rw, qw, ws = (pick(k) for k in range(5))
    step0 = rz / zq
    rz1 = rz - step0 * (rw + zq) + step0 * step0 * qw
    growth = rz1 / rz
    image1 = (zq - 2.0 * step0 * qw + step0 * step0 * ws) + 2.0 * growth * (zq - step0 * qw) + growth * growth * zq
    step1 = rz1 / image1
    on_z = step0 + step1 * (1.0 + growth)
    on_w = -step1 * step0
    wide = lane_index((BY, LANES))
    for x in range(BX):
        parts = [fields[c, x * BY : (x + 1) * BY] for c in range(4)]

        def field(f):
            value = None
            for c in range(4):
                part = roll(parts[c], 32 * (c - f), 1)
                value = part if c == 0 else jnp.where(wide >= 32 * c, part, value)
            return value

        z0, q0, w, s = (field(f) for f in range(4))
        u = on_z * z0 + on_w * w
        v = on_z * q0 + on_w * s
        for odd in range(2):
            rows = pl.ds(odd, 8, stride=2)
            solution[x, rows, :] = u[8 * odd : 8 * odd + 8]
            residual[x, rows, :] = rhs[x, rows, :] - v[8 * odd : 8 * odd + 8]


def finish(rhs, fields, sums):
    shape = jax.ShapeDtypeStruct((BX, BY, BZ), jnp.float32)
    return pl.pallas_call(finish_kernel, out_shape=(shape, shape), in_specs=[VMEM] * 3, out_specs=(VMEM, VMEM), compiler_params=small())(rhs, fields, sums)


def both_ways(count, step):
    pairs = [(i, i + step) for i in range(count - step)]
    return pairs + [(count + b, count + a) for a, b in pairs]


def z_pairs(steps):
    def number(core, block):
        return ((block % 4) * 2 + core) * 8 + block // 4

    return [(number(core, a), number(core, a + step)) for core, step in enumerate(steps) for a in range(32) if 0 <= a + step < 32]


Z_AXES = ("gx_0", "gx_1", "gz")


def local(density, x_faces, y_faces, z_faces):
    rhs, packed = make_rhs(density, x_faces, y_faces, z_faces)
    own = lax.all_to_all(packed, GX, 0, 0, tiled=True).reshape(16, BY, 128)
    near = lax.ppermute(own, ("gx_1", "gy"), both_ways(16, 1))
    far = lax.ppermute(own, ("gx_1", "gy"), both_ways(16, 2))
    side = lax.ppermute(own, Z_AXES, z_pairs((1, -1)))
    rows = jnp.stack([near, far])
    up = lax.ppermute(rows, Z_AXES, z_pairs((1, 1)))
    down = lax.ppermute(rows, Z_AXES, z_pairs((-1, -1)))
    packed = cycles(own, *(lax.all_gather(each, "gx_1") for each in (side, rows, up, down)))
    fields = lax.all_to_all(packed, "gx_0", 0, 0, tiled=True)
    sums = jnp.sum(fields[:, BX * BY, :], axis=0)
    sums = lax.all_to_all(jnp.broadcast_to(sums, (128, 1, 128)), ("gy", "gz"), 0, 0, tiled=True)
    return finish(rhs, fields, sums.reshape(128, 128))


def solution(mesh):
    torus = Mesh(mesh.devices.reshape(4, 2, mesh.shape["gy"], mesh.shape["gz"]), AXES)
    in_specs = (P(GX, "gy", "gz"), P(None, "gy", "gz"), P(None, GX, "gz"), P(None, GX, "gy"))
    out_specs = (P(GX, "gy", "gz"), P(GX, "gy", "gz"))
    return jax.shard_map(local, mesh=torus, in_specs=in_specs, out_specs=out_specs, check_vma=False)
```

time: 113 us -> 105 us (0.929)
  Pallas kernels: 19 us -> 11.7 us
    pallas_call x1, Pallas kernels: 16.3 us -> 9.01 us  [cycles(): pl.pallas_call(cycles_kernel, out_shape=jax.ShapeDtypeStruct((4, BX * BY...]
where the time goes in v5:
time: 105 us
  blocking collectives  68.8 us (66%)
  starting transfers between devices  21.6 us (21%)
  Pallas kernels  11.7 us (11%)
  waiting for transfers between devices  1.92 us (2%)
    all_to_all x1, blocking collectives, local(): lax.all_to_all(jnp.broadcast_to(sums, (128, 1, 128)), ('gy', 'gz'), 0, 0,...  37.4 us
    all_gather x4, blocking collectives, local(): lax.all_gather(each, 'gx_1')  11 us
    all_to_all x1, blocking collectives, local(): own = lax.all_to_all(packed, GX, 0, 0, tiled=True).reshape(16, BY, 128)  10.4 us
    all_to_all x1, blocking collectives, local(): fields = lax.all_to_all(packed, 'gx_0', 0, 0, tiled=True)  10 us
    pallas_call x1, Pallas kernels, cycles(): pl.pallas_call(cycles_kernel, out_shape=jax.ShapeDtypeStruct((4, BX * BY...  9.01 us
    ppermute x1, starting transfers between devices, local(): down = lax.ppermute(rows, Z_AXES, z_pairs((-1, -1)))  6.87 us
    ppermute x1, starting transfers between devices, local(): far = lax.ppermute(own, ('gx_1', 'gy'), both_ways(16, 2))  6.08 us
    ppermute x1, starting transfers between devices, local(): near = lax.ppermute(own, ('gx_1', 'gy'), both_ways(16, 1))  4.28 us
  transfers between devices with their start and end apart: 5, of which 1 were waited for; matrix products, arithmetic and copies ran while one was open for 0% of the time, Pallas kernels for 0%

profile of v5, /device:TPU:8, one launch (start us, length us, event | category | flops | bytes accessed | tf_op | source)
XLA Modules:
  0.0 104.9 jit_solution(18217967394050321416)
XLA Ops:
  0.6 1.8 %shard_map.59 = (f32[8,16,128]{2,1,0:T(8,128)}, f32[8,2,16,128]{3,2,1,0:T(8,128)}) custom-call(f32[8,16,128]{2,1,0:T(8,128)} %density_in.1, f32[2,16,128]{2,1,0:T(8,128)} %xf_in.1, f32[2,8,128]{2,1,0:T(8,128)} %yf_in.1, f32[2,8,16]{2,1,0:T(8,128)} %zf_in.1), custom_call_target="tpu_custom_call" | custom-call | tf_op jit(solution)/shard_map/pallas_call | solution.py:91
  2.4 10.4 %all_to_all.15 = f32[8,2,16,128]{3,2,1,0:T(8,128)S(1)} all-to-all(f32[8,2,16,128]{3,2,1,0:T(8,128)} %get-tuple-element.5), channel_id=1, replica_groups=mesh['gx_0'=4,'gx_1'=2,'gy'=16,'gz'=8] {'gx_0','gx_1'}, dimensions={0} | all-to-all | bytes 262144 | tf_op jit(solution)/shard_map/all_to_all | solution.py:421
  12.8 6.1 %collective-permute-start.2 = (f32[16,16,128]{2,1,0:T(8,128)S(1)}, f32[16,16,128]{2,1,0:T(8,128)S(1)}, u32[]{:S(2)}, u32[]{:S(2)}) collective-permute-start(f32[16,16,128]{2,1,0:T(8,128)S(1)} %bitcast.12), channel_id=1, source_target_pairs={{0,16},{8,24},{16,32},{24,40},{32,48},{40,56},{48,64},{56,72},{64,... | collective-permute-start | bytes 393224 | tf_op jit(solution)/shard_map/ppermute | solution.py:423
  18.9 4.3 %collective-permute-start.1 = (f32[16,16,128]{2,1,0:T(8,128)S(1)}, f32[16,16,128]{2,1,0:T(8,128)S(1)}, u32[]{:S(2)}, u32[]{:S(2)}) collective-permute-start(f32[16,16,128]{2,1,0:T(8,128)S(1)} %bitcast.13), channel_id=1, source_target_pairs={{0,8},{8,16},{16,24},{24,32},{32,40},{40,48},{48,56},{56,64},{64,7... | collective-permute-start | bytes 393224 | tf_op jit(solution)/shard_map/ppermute | solution.py:422
  23.2 2.5 %collective-permute-start = (f32[16,16,128]{2,1,0:T(8,128)S(1)}, f32[16,16,128]{2,1,0:T(8,128)S(1)}, u32[]{:S(2)}, u32[]{:S(2)}) collective-permute-start(f32[16,16,128]{2,1,0:T(8,128)S(1)} %bitcast.14), channel_id=1, source_target_pairs={{0,256},{256,512},{512,768},{768,1},{1,257},{257,513},{513,769},{7... | collective-permute-start | bytes 393224 | tf_op jit(solution)/shard_map/ppermute | solution.py:424
  25.7 0.0 collective-permute-done.2
  25.7 0.0 collective-permute-done.1
  25.7 6.9 %collective-permute-start.4 = (f32[2,16,16,128]{3,2,1,0:T(8,128)S(1)}, f32[2,16,16,128]{3,2,1,0:T(8,128)S(1)}, u32[]{:S(2)}, u32[]{:S(2)}) collective-permute-start(f32[2,16,16,128]{3,2,1,0:T(8,128)S(1)} %pad_maximum_fusion), channel_id=1, source_target_pairs={{256,0},{512,256},{768,512},{1,768},{257,1},{513,257},{769,513},{2... | collective-permute-start | bytes 786440 | tf_op jit(solution)/shard_map/ppermute | solution.py:427
  32.6 1.9 %collective-permute-start.3 = (f32[2,16,16,128]{3,2,1,0:T(8,128)S(1)}, f32[2,16,16,128]{3,2,1,0:T(8,128)S(1)}, u32[]{:S(2)}, u32[]{:S(2)}) collective-permute-start(f32[2,16,16,128]{3,2,1,0:T(8,128)S(1)} %pad_maximum_fusion), channel_id=1, source_target_pairs={{0,256},{256,512},{512,768},{768,1},{1,257},{257,513},{513,769},{7... | collective-permute-start | bytes 786440 | tf_op jit(solution)/shard_map/ppermute | solution.py:426
  34.5 0.0 collective-permute-done
  34.5 3.8 %all-gather = f32[32,16,128]{2,1,0:T(8,128)S(1)} all-gather(f32[16,16,128]{2,1,0:T(8,128)S(1)} %collective-permute-done), channel_id=2, replica_groups=mesh['gx_0'=4,'gx_1'=2,'gy'=16,'gz'=8] {'gx_1'}, dimensions={0}, use_global_device_ids=true | all-gather | bytes 393216 | tf_op jit(solution)/shard_map/all_gather | solution.py:428
  38.3 2.2 %all-gather.1 = f32[4,16,16,128]{3,2,1,0:T(8,128)S(1)} all-gather(f32[2,16,16,128]{3,2,1,0:T(8,128)S(1)} %pad_maximum_fusion), channel_id=3, replica_groups=mesh['gx_0'=4,'gx_1'=2,'gy'=16,'gz'=8] {'gx_1'}, dimensions={0}, use_global_device_ids=true | all-gather | bytes 786432 | tf_op jit(solution)/shard_map/all_gather | solution.py:428
  40.5 0.0 collective-permute-done.4
  40.5 2.2 %all-gather.3 = f32[4,16,16,128]{3,2,1,0:T(8,128)S(1)} all-gather(f32[2,16,16,128]{3,2,1,0:T(8,128)S(1)} %collective-permute-done.4), channel_id=5, replica_groups=mesh['gx_0'=4,'gx_1'=2,'gy'=16,'gz'=8] {'gx_1'}, dimensions={0}, use_global_device_ids=true | all-gather | bytes 786432 | tf_op jit(solution)/shard_map/all_gather | solution.py:428
  42.7 1.9 %collective-permute-done.3 = f32[2,16,16,128]{3,2,1,0:T(8,128)S(1)} collective-permute-done((f32[2,16,16,128]{3,2,1,0:T(8,128)S(1)}, f32[2,16,16,128]{3,2,1,0:T(8,128)S(1)}, u32[]{:S(2)}, u32[]{:S(2)}) %collective-permute-start.3) | collective-permute-done | bytes 262176 | tf_op jit(solution)/shard_map/ppermute | solution.py:426
  44.6 2.8 %all-gather.2 = f32[4,16,16,128]{3,2,1,0:T(8,128)S(1)} all-gather(f32[2,16,16,128]{3,2,1,0:T(8,128)S(1)} %collective-permute-done.3), channel_id=4, replica_groups=mesh['gx_0'=4,'gx_1'=2,'gy'=16,'gz'=8] {'gx_1'}, dimensions={0}, use_global_device_ids=true | all-gather | bytes 786432 | tf_op jit(solution)/shard_map/all_gather | solution.py:428
  47.4 9.0 %shard_map.60 = f32[4,136,128]{2,1,0:T(8,128)S(1)} custom-call(f32[16,16,128]{2,1,0:T(8,128)S(1)} %bitcast.15, f32[2,16,16,128]{3,2,1,0:T(8,128)S(1)} %bitcast.11, f32[2,2,16,16,128]{4,3,2,1,0:T(8,128)S(1)} %bitcast.8, f32[2,2,16,16,128]{4,3,2,1,0:T(8,128)S(1)} %bitcast.10, f32[2,2,16,16,128]{4,3,2,1,0:T(8,128)S(1)} %bitcast.9), custom_call_target="tpu_custom_call" | custom-call | tf_op jit(solution)/shard_map/pallas_call | solution.py:352
  56.4 10.0 %all_to_all.16.fields = f32[4,136,128]{2,1,0:T(8,128)S(1)} all-to-all(f32[4,136,128]{2,1,0:T(8,128)S(1)} %shard_map.60), channel_id=1, replica_groups=mesh['gx_0'=4,'gx_1'=2,'gy'=16,'gz'=8] {'gx_0'}, dimensions={0} | all-to-all | bytes 557056 | tf_op jit(solution)/shard_map/all_to_all | solution.py:429
  66.5 0.0 copy-start
  66.5 37.4 %all_to_all.17 = f32[128,1,128]{2,1,0:T(1,128)S(1)} all-to-all(f32[128,1,128]{2,1,0:T(1,128)S(1)} %broadcast_in_dim.3), channel_id=1, replica_groups=mesh['gx_0'=4,'gx_1'=2,'gy'=16,'gz'=8] {'gy','gz'}, dimensions={0} | all-to-all | bytes 131072 | tf_op jit(solution)/shard_map/all_to_all | solution.py:431
  103.9 0.0 copy-done
  103.9 0.9 shard_map.61
  (3 shorter events, 0.1 us)
Async XLA Ops:
  12.8 12.9 %collective-permute-start.2 = (f32[16,16,128]{2,1,0:T(8,128)S(1)}, f32[16,16,128]{2,1,0:T(8,128)S(1)}, u32[]{:S(2)}, u32[]{:S(2)}) collective-permute-start(f32[16,16,128]{2,1,0:T(8,128)S(1)} %bitcast.12), channel_id=1, source_target_pairs={{0,16},{8,24},{16,32},{24,40},{32,48},{40,56},{48,64},{56,72},{64,... | collective-permute-start | bytes 393224 | tf_op jit(solution)/shard_map/ppermute | solution.py:423
  18.9 6.8 %collective-permute-start.1 = (f32[16,16,128]{2,1,0:T(8,128)S(1)}, f32[16,16,128]{2,1,0:T(8,128)S(1)}, u32[]{:S(2)}, u32[]{:S(2)}) collective-permute-start(f32[16,16,128]{2,1,0:T(8,128)S(1)} %bitcast.13), channel_id=1, source_target_pairs={{0,8},{8,16},{16,24},{24,32},{32,40},{40,48},{48,56},{56,64},{64,7... | collective-permute-start | bytes 393224 | tf_op jit(solution)/shard_map/ppermute | solution.py:422
  23.2 11.3 %collective-permute-start = (f32[16,16,128]{2,1,0:T(8,128)S(1)}, f32[16,16,128]{2,1,0:T(8,128)S(1)}, u32[]{:S(2)}, u32[]{:S(2)}) collective-permute-start(f32[16,16,128]{2,1,0:T(8,128)S(1)} %bitcast.14), channel_id=1, source_target_pairs={{0,256},{256,512},{512,768},{768,1},{1,257},{257,513},{513,769},{7... | collective-permute-start | bytes 393224 | tf_op jit(solution)/shard_map/ppermute | solution.py:424
  25.7 14.8 %collective-permute-start.4 = (f32[2,16,16,128]{3,2,1,0:T(8,128)S(1)}, f32[2,16,16,128]{3,2,1,0:T(8,128)S(1)}, u32[]{:S(2)}, u32[]{:S(2)}) collective-permute-start(f32[2,16,16,128]{3,2,1,0:T(8,128)S(1)} %pad_maximum_fusion), channel_id=1, source_target_pairs={{256,0},{512,256},{768,512},{1,768},{257,1},{513,257},{769,513},{2... | collective-permute-start | bytes 786440 | tf_op jit(solution)/shard_map/ppermute | solution.py:427
  32.6 12.0 %collective-permute-start.3 = (f32[2,16,16,128]{3,2,1,0:T(8,128)S(1)}, f32[2,16,16,128]{3,2,1,0:T(8,128)S(1)}, u32[]{:S(2)}, u32[]{:S(2)}) collective-permute-start(f32[2,16,16,128]{3,2,1,0:T(8,128)S(1)} %pad_maximum_fusion), channel_id=1, source_target_pairs={{0,256},{256,512},{512,768},{768,1},{1,257},{257,513},{513,769},{7... | collective-permute-start | bytes 786440 | tf_op jit(solution)/shard_map/ppermute | solution.py:426
  66.5 37.4 %copy-start = (f32[8,16,128]{2,1,0:T(8,128)S(1)}, f32[8,16,128]{2,1,0:T(8,128)}, u32[]{:S(2)}) copy-start(f32[8,16,128]{2,1,0:T(8,128)} %get-tuple-element.4.rhs) | copy-start | bytes 196612

commit v6 on v5

--- a/solution.py
+++ b/solution.py
@@ -1,5 +1,3 @@
-import functools
-
 import jax
 import jax.numpy as jnp
 from jax import lax
@@ -8,13 +6,14 @@
 from jax.sharding import Mesh
 from jax.sharding import PartitionSpec as P
 
+
 AXES = ("gx_0", "gx_1", "gy", "gz")
 GX = ("gx_0", "gx_1")
 NX, NY, NZ = 64, 256, 1024
 BX, BY, BZ = 8, 16, 128
 CZ = 32
 HY, HZ = 32, 32
-ROWS, LANES = BY + 2 * HY, 128
+LANES = 128
 relax = 1.0 / 9.0
 coupling = 0.5
 VMEM = pl.BlockSpec(memory_space=pltpu.VMEM)
@@ -27,6 +26,10 @@
 
 def place():
     return tuple(lax.axis_index(axis) for axis in AXES)
+
+
+def z_block(gx0, gz):
+    return jnp.where(gz % 2 == 0, gx0, 3 - gx0)
 
 
 def small(**more):
@@ -79,12 +82,13 @@
                 part = roll(layers[4 * quad + k], 32 * (k - chunk), 1)
                 out = part if k == 0 else jnp.where(lanes >= 32 * k, part, out)
             scratch[chunk, quad] = out
-    for chunk in range(4):
+    for chip in range(4):
+        chunk = z_block(chip, gz)
         for quad in range(2):
             for odd in range(2):
                 part = scratch[chunk, quad, pl.ds(odd, 8, stride=2), :]
-                packed[2 * chunk, quad, 8 * odd : 8 * odd + 8] = part
-                packed[2 * chunk + 1, quad, 8 * odd : 8 * odd + 8] = part
+                packed[2 * chip, quad, 8 * odd : 8 * odd + 8] = part
+                packed[2 * chip + 1, quad, 8 * odd : 8 * odd + 8] = part
 
 
 def make_rhs(density, xf, yf, zf):
@@ -103,6 +107,23 @@
     )(density, xf, yf, zf)
 
 
+def join_kernel(*refs):
+    out = refs[-1]
+    for b, ref in enumerate(refs[:-1]):
+        for i in range(16):
+            out[i, BY * b : BY * b + BY] = ref[i]
+
+
+def join(*blocks):
+    return pl.pallas_call(
+        join_kernel,
+        out_shape=jax.ShapeDtypeStruct((16, 4 * BY, 128), jnp.float32),
+        in_specs=[VMEM] * 4,
+        out_specs=VMEM,
+        compiler_params=small(),
+    )(*blocks)
+
+
 def at(row, step=0):
     return pl.ds(8 + row + step, 8)
 
@@ -260,13 +281,13 @@
     return result
 
 
-def cycles_kernel(own, beside, rows_, up, down, out, r0, z0, q0, w, v0, f1, v1, e1, e2, f2, t2, mask, mask2):
-    gx0, core, gy, gz = place()
+def cycles_kernel(own, left, right, rows_, up, down, out, other, r0, z0, q0, w, v0, f1, v1, e1, e2, f2, t2, mask, mask2):
+    gx0, _, gy, gz = place()
 
     def inside(count, height):
         rows, lanes = row_index((count, LANES)) - 8, lane_index((count, LANES))
         y = gy * BY - HY + height * rows
-        z = (gz * 4 + gx0) * CZ - HZ + lanes
+        z = (gz * 4 + z_block(gx0, gz)) * CZ - HZ + lanes
         return jnp.where((y >= 0) & (y < NY) & (z >= 0) & (z < NZ), 1.0, 0.0)
 
     mask[...] = inside(56, 2)
@@ -275,16 +296,13 @@
         ref[0] = jnp.zeros(ref.shape[1:], jnp.float32)
         ref[count + 1] = jnp.zeros(ref.shape[1:], jnp.float32)
     lanes = lane_index((8, LANES))
-    blocks = [(up, rows_, down, which) for which in ((0, 1), (0, 0), None, (1, 0), (1, 1))]
+    y_blocks = [tuple(ref.at[:, pl.ds(BY * b, BY)] for ref in (up, rows_, down)) for b in range(4)]
+    y_blocks.insert(2, (left, own, right))
 
     def unpack(i, _):
-        for b, (left, middle, right, which) in enumerate(blocks):
+        for b, sources in enumerate(y_blocks):
             for odd in range(2):
-                part = pl.ds(8 * odd, 8)
-                if which is None:
-                    a, c, d = beside[0, i, part], own[i, part], beside[1, i, part]
-                else:
-                    a, c, d = (ref[which + (i, part)] for ref in (left, middle, right))
+                a, c, d = (ref[i, pl.ds(8 * odd, 8)] for ref in sources)
                 for k in range(4):
                     value = jnp.where(lanes < 32, roll(a, -32 * k, 1), jnp.where(lanes < 64, roll(c, 32 - 32 * k, 1), roll(d, 64 - 32 * k, 1)))
                     r0[4 * i + k + 1, odd, at(8 * b)] = value
@@ -326,23 +344,22 @@
 
     acc = lax.fori_loop(0, NX // 64, sums, (jnp.zeros((8, LANES), jnp.float32),) * 5)
 
-    def send(t, _):
-        for k in range(BX):
-            x = BX * (2 * t + core) + k + 1
-            for odd in range(2):
-                zz, q, ww, s = (ref[x, odd, at(16)] for ref in (z0, q0, w, v0))
-                out[t, pl.ds(k * BY + 8 * odd, 8)] = jnp.where(
-                    lanes < 32, roll(zz, -32, 1), jnp.where(lanes < 64, q, jnp.where(lanes < 96, roll(ww, 32, 1), roll(s, 64, 1)))
-                )
-        return 0
-
-    lax.fori_loop(0, 4, send, 0, unroll=4)
+    for odd_slab, ref in enumerate((other, out)):
+        for t in range(4):
+            for k in range(BX):
+                x = BX * (2 * t + odd_slab) + k + 1
+                for odd in range(2):
+                    zz, q, ww, s = (field[x, odd, at(16)] for field in (z0, q0, w, v0))
+                    ref[t, pl.ds(k * BY + 8 * odd, 8)] = jnp.where(
+                        lanes < 32, roll(zz, -32, 1), jnp.where(lanes < 64, q, jnp.where(lanes < 96, roll(ww, 32, 1), roll(s, 64, 1)))
+                    )
     home = (lanes >= HZ) & (lanes < HZ + CZ)
     row = jnp.zeros((8, LANES), jnp.float32)
     for k, a in enumerate(acc):
         row = jnp.where(lanes == k, jnp.sum(jnp.where(home, a, 0.0)), row)
     for t in range(4):
         out[t, BX * BY : BX * BY + 8] = row
+        other[t, BX * BY : BX * BY + 8] = row
 
 
 def cycles(*blocks):
@@ -351,9 +368,9 @@
     level2 = pltpu.VMEM((NX // 4 + 2, 40, LANES), jnp.float32)
     return pl.pallas_call(
         cycles_kernel,
-        out_shape=jax.ShapeDtypeStruct((4, BX * BY + 8, LANES), jnp.float32),
-        in_specs=[VMEM] * 5,
-        out_specs=VMEM,
+        out_shape=(jax.ShapeDtypeStruct((4, BX * BY + 8, LANES), jnp.float32),) * 2,
+        in_specs=[VMEM] * 6,
+        out_specs=(VMEM, VMEM),
         scratch_shapes=[fine] * 5
         + [level1] * 3
         + [pltpu.VMEM((NX // 4 + 2, 56, LANES), jnp.float32), level2, level2, pltpu.VMEM((56, LANES), jnp.float32), pltpu.VMEM((40, LANES), jnp.float32)],
@@ -377,8 +394,9 @@
     on_z = step0 + step1 * (1.0 + growth)
     on_w = -step1 * step0
     wide = lane_index((BY, LANES))
+    gz = lax.axis_index("gz")
     for x in range(BX):
-        parts = [fields[c, x * BY : (x + 1) * BY] for c in range(4)]
+        parts = [fields[z_block(c, gz), x * BY : (x + 1) * BY] for c in range(4)]
 
         def field(f):
             value = None
@@ -401,16 +419,16 @@
     return pl.pallas_call(finish_kernel, out_shape=(shape, shape), in_specs=[VMEM] * 3, out_specs=(VMEM, VMEM), compiler_params=small())(rhs, fields, sums)
 
 
-def both_ways(count, step):
-    pairs = [(i, i + step) for i in range(count - step)]
-    return pairs + [(count + b, count + a) for a, b in pairs]
-
-
-def z_pairs(steps):
+def y_pairs(step):
+    return [(16 + a, a + step) for a in range(16) if 0 <= a + step < 16]
+
+
+def z_pairs(step):
     def number(core, block):
-        return ((block % 4) * 2 + core) * 8 + block // 4
-
-    return [(number(core, a), number(core, a + step)) for core, step in enumerate(steps) for a in range(32) if 0 <= a + step < 32]
+        gz, at = block // 4, block % 4
+        return ((at if gz % 2 == 0 else 3 - at) * 2 + core) * 8 + gz
+
+    return [(number(0, a), number(1, a + step)) for a in range(32) if 0 <= a + step < 32]
 
 
 Z_AXES = ("gx_0", "gx_1", "gz")
@@ -419,13 +437,18 @@
 def local(density, x_faces, y_faces, z_faces):
     rhs, packed = make_rhs(density, x_faces, y_faces, z_faces)
     own = lax.all_to_all(packed, GX, 0, 0, tiled=True).reshape(16, BY, 128)
-    near = lax.ppermute(own, ("gx_1", "gy"), both_ways(16, 1))
-    far = lax.ppermute(own, ("gx_1", "gy"), both_ways(16, 2))
-    side = lax.ppermute(own, Z_AXES, z_pairs((1, -1)))
-    rows = jnp.stack([near, far])
-    up = lax.ppermute(rows, Z_AXES, z_pairs((1, 1)))
-    down = lax.ppermute(rows, Z_AXES, z_pairs((-1, -1)))
-    packed = cycles(own, *(lax.all_gather(each, "gx_1") for each in (side, rows, up, down)))
+    moved = []
+    for step in (1, -1, 2, -2):
+        moved.append(lax.ppermute(own, ("gx_1", "gy"), y_pairs(step)))
+    left = lax.ppermute(own, Z_AXES, z_pairs(1))
+    right = lax.ppermute(own, Z_AXES, z_pairs(-1))
+    rows = join(moved[2], moved[0], moved[1], moved[3])
+    up = lax.ppermute(rows, Z_AXES, z_pairs(1))
+    down = lax.ppermute(rows, Z_AXES, z_pairs(-1))
+    rows = lax.ppermute(rows, "gx_1", [(0, 1)])
+    packed, other = cycles(own, left, right, rows, up, down)
+    other = lax.ppermute(other, "gx_1", [(1, 0)])
+    packed = jnp.where(lax.axis_index("gx_1") == 0, other, packed)
     fields = lax.all_to_all(packed, "gx_0", 0, 0, tiled=True)
     sums = jnp.sum(fields[:, BX * BY, :], axis=0)
     sums = lax.all_to_all(jnp.broadcast_to(sums, (128, 1, 128)), ("gy", "gz"), 0, 0, tiled=True)

time: 105 us -> 105 us (level)
  waiting for transfers between devices: 1.92 us -> 22.2 us
  blocking collectives: 68.8 us -> 57.8 us
  starting transfers between devices: 21.6 us -> 11.8 us
    ppermute x5 -> x10, waiting for transfers between devices: 1.92 us -> 22.2 us  [the longest x4 13.9 us: local(): moved.append(lax.ppermute(own, ('gx_1', 'gy'), y_pairs(step)))]
    all_gather x4 -> x0, blocking collectives: 11 us -> none  [local(): lax.all_gather(each, 'gx_1')]
    ppermute x5 -> x10, starting transfers between devices: 21.6 us -> 11.8 us  [the longest x4 3.91 us: local(): moved.append(lax.ppermute(own, ('gx_1', 'gy'), y_pairs(step)))]
    pallas_call x1 -> x2, Pallas kernels: 9.01 us -> 9.22 us  [the longest x1 9.18 us: cycles(): pl.pallas_call(cycles_kernel, out_shape=(jax.ShapeDtypeStruct((4, BX * BY...]
  transfers between devices with their start and end apart: 5 -> 10, of which waited for: 1 -> 5; matrix products, arithmetic and copies ran while one was open for 0% -> 0% of each run, Pallas kernels for 0% -> 0%
where the time goes in v6:
time: 105 us
  blocking collectives  57.8 us (55%)
  waiting for transfers between devices  22.2 us (21%)
  Pallas kernels  11.9 us (11%)
  starting transfers between devices  11.8 us (11%)
    all_to_all x1, blocking collectives, local(): lax.all_to_all(jnp.broadcast_to(sums, (128, 1, 128)), ('gy', 'gz'), 0, 0,...  36.9 us
    ppermute x4, waiting for transfers between devices, local(): moved.append(lax.ppermute(own, ('gx_1', 'gy'), y_pairs(step)))  13.9 us
    all_to_all x1, blocking collectives, local(): fields = lax.all_to_all(packed, 'gx_0', 0, 0, tiled=True)  10.5 us
    all_to_all x1, blocking collectives, local(): own = lax.all_to_all(packed, GX, 0, 0, tiled=True).reshape(16, BY, 128)  10.4 us
    pallas_call x1, Pallas kernels, cycles(): pl.pallas_call(cycles_kernel, out_shape=(jax.ShapeDtypeStruct((4, BX * BY...  9.18 us
    ppermute x1, waiting for transfers between devices, local(): left = lax.ppermute(own, Z_AXES, z_pairs(1))  4.11 us
    ppermute x4, starting transfers between devices, local(): moved.append(lax.ppermute(own, ('gx_1', 'gy'), y_pairs(step)))  3.91 us
    ppermute x1, waiting for transfers between devices, local(): other = lax.ppermute(other, 'gx_1', [(1, 0)])  2.87 us
  transfers between devices with their start and end apart: 10, of which 5 were waited for; matrix products, arithmetic and copies ran while one was open for 0% of the time, Pallas kernels for 0%

profile of v6, /device:TPU:8, one launch (start us, length us, event | category | flops | bytes accessed | tf_op | source)
XLA Modules:
  0.0 104.6 jit_solution(10552717443753399078)
XLA Ops:
  0.6 1.8 %shard_map.59 = (f32[8,16,128]{2,1,0:T(8,128)}, f32[8,2,16,128]{3,2,1,0:T(8,128)}) custom-call(f32[8,16,128]{2,1,0:T(8,128)} %density_in.1, f32[2,16,128]{2,1,0:T(8,128)} %xf_in.1, f32[2,8,128]{2,1,0:T(8,128)} %yf_in.1, f32[2,8,16]{2,1,0:T(8,128)} %zf_in.1), custom_call_target="tpu_custom_call" | custom-call | tf_op jit(solution)/shard_map/pallas_call | solution.py:95
  2.4 10.4 %all_to_all.15 = f32[8,2,16,128]{3,2,1,0:T(8,128)S(1)} all-to-all(f32[8,2,16,128]{3,2,1,0:T(8,128)} %get-tuple-element.7), channel_id=1, replica_groups=mesh['gx_0'=4,'gx_1'=2,'gy'=16,'gz'=8] {'gx_0','gx_1'}, dimensions={0} | all-to-all | bytes 262144 | tf_op jit(solution)/shard_map/all_to_all | solution.py:439
  12.8 0.7 collective-permute-start.2
  13.5 0.7 collective-permute-start.3
  14.1 1.3 %collective-permute-start.4 = (f32[16,16,128]{2,1,0:T(8,128)S(1)}, f32[16,16,128]{2,1,0:T(8,128)S(1)}, u32[]{:S(2)}, u32[]{:S(2)}) collective-permute-start(f32[16,16,128]{2,1,0:T(8,128)S(1)} %bitcast.4), channel_id=1, source_target_pairs={{136,0},{144,8},{152,16},{160,24},{168,32},{176,40},{184,48},{192,... | collective-permute-start | bytes 393224 | tf_op jit(solution)/shard_map/ppermute | solution.py:442
  15.4 1.3 %collective-permute-start.5 = (f32[16,16,128]{2,1,0:T(8,128)S(1)}, f32[16,16,128]{2,1,0:T(8,128)S(1)}, u32[]{:S(2)}, u32[]{:S(2)}) collective-permute-start(f32[16,16,128]{2,1,0:T(8,128)S(1)} %bitcast.5), channel_id=1, source_target_pairs={{144,0},{152,8},{160,16},{168,24},{176,32},{184,40},{192,48},{200,... | collective-permute-start | bytes 393224 | tf_op jit(solution)/shard_map/ppermute | solution.py:442
  16.7 0.0 collective-permute-done.2.refs_0_
  16.8 0.0 collective-permute-done.3.refs_1_
  16.8 9.4 %collective-permute-done.4.refs_2_ = f32[16,16,128]{2,1,0:T(8,128)S(1)} collective-permute-done((f32[16,16,128]{2,1,0:T(8,128)S(1)}, f32[16,16,128]{2,1,0:T(8,128)S(1)}, u32[]{:S(2)}, u32[]{:S(2)}) %collective-permute-start.4) | collective-permute-done | bytes 131104 | tf_op jit(solution)/shard_map/ppermute | solution.py:442
  26.2 4.4 %collective-permute-done.5.refs_3_ = f32[16,16,128]{2,1,0:T(8,128)S(1)} collective-permute-done((f32[16,16,128]{2,1,0:T(8,128)S(1)}, f32[16,16,128]{2,1,0:T(8,128)S(1)}, u32[]{:S(2)}, u32[]{:S(2)}) %collective-permute-start.5) | collective-permute-done | bytes 131104 | tf_op jit(solution)/shard_map/ppermute | solution.py:442
  30.7 1.3 %collective-permute-start.6 = (f32[16,64,128]{2,1,0:T(8,128)S(1)}, f32[16,64,128]{2,1,0:T(8,128)S(1)}, u32[]{:S(2)}, u32[]{:S(2)}) collective-permute-start(f32[16,64,128]{2,1,0:T(8,128)S(1)} %shard_map.60), channel_id=1, source_target_pairs={{0,128},{1,129},{2,130},{3,131},{4,132},{5,133},{6,134},{7,135},{8... | collective-permute-start | bytes 1572872 | tf_op jit(solution)/shard_map/ppermute | solution.py:448
  32.0 1.3 %collective-permute-start.7 = (f32[16,64,128]{2,1,0:T(8,128)S(1)}, f32[16,64,128]{2,1,0:T(8,128)S(1)}, u32[]{:S(2)}, u32[]{:S(2)}) collective-permute-start(f32[16,64,128]{2,1,0:T(8,128)S(1)} %shard_map.60), channel_id=1, source_target_pairs={{0,384},{256,640},{512,896},{768,897},{769,641},{513,385},{257,129... | collective-permute-start | bytes 1572872 | tf_op jit(solution)/shard_map/ppermute | solution.py:446
  33.3 1.3 %collective-permute-start.8 = (f32[16,64,128]{2,1,0:T(8,128)S(1)}, f32[16,64,128]{2,1,0:T(8,128)S(1)}, u32[]{:S(2)}, u32[]{:S(2)}) collective-permute-start(f32[16,64,128]{2,1,0:T(8,128)S(1)} %shard_map.60), channel_id=1, source_target_pairs={{256,128},{512,384},{768,640},{769,896},{513,897},{257,641},{1,385... | collective-permute-start | bytes 1572872 | tf_op jit(solution)/shard_map/ppermute | solution.py:447
  34.7 1.3 %collective-permute-start = (f32[16,16,128]{2,1,0:T(8,128)S(1)}, f32[16,16,128]{2,1,0:T(8,128)S(1)}, u32[]{:S(2)}, u32[]{:S(2)}) collective-permute-start(f32[16,16,128]{2,1,0:T(8,128)S(1)} %bitcast.6), channel_id=1, source_target_pairs={{0,384},{256,640},{512,896},{768,897},{769,641},{513,385},{257,129... | collective-permute-start | bytes 393224 | tf_op jit(solution)/shard_map/ppermute | solution.py:443
  36.0 1.3 %collective-permute-start.1 = (f32[16,16,128]{2,1,0:T(8,128)S(1)}, f32[16,16,128]{2,1,0:T(8,128)S(1)}, u32[]{:S(2)}, u32[]{:S(2)}) collective-permute-start(f32[16,16,128]{2,1,0:T(8,128)S(1)} %bitcast.7), channel_id=1, source_target_pairs={{256,128},{512,384},{768,640},{769,896},{513,897},{257,641},{1,385... | collective-permute-start | bytes 393224 | tf_op jit(solution)/shard_map/ppermute | solution.py:444
  37.3 4.1 %collective-permute-done.left = f32[16,16,128]{2,1,0:T(8,128)S(1)} collective-permute-done((f32[16,16,128]{2,1,0:T(8,128)S(1)}, f32[16,16,128]{2,1,0:T(8,128)S(1)}, u32[]{:S(2)}, u32[]{:S(2)}) %collective-permute-start) | collective-permute-done | bytes 131104 | tf_op jit(solution)/shard_map/ppermute | solution.py:443
  41.4 1.3 %collective-permute-done.1.right = f32[16,16,128]{2,1,0:T(8,128)S(1)} collective-permute-done((f32[16,16,128]{2,1,0:T(8,128)S(1)}, f32[16,16,128]{2,1,0:T(8,128)S(1)}, u32[]{:S(2)}, u32[]{:S(2)}) %collective-permute-start.1) | collective-permute-done | bytes 131104 | tf_op jit(solution)/shard_map/ppermute | solution.py:444
  42.7 0.0 collective-permute-done.6.rows_
  42.7 0.0 collective-permute-done.7.up
  42.7 0.0 collective-permute-done.8.down
  42.7 9.2 %shard_map.61 = (f32[4,136,128]{2,1,0:T(8,128)S(1)}, f32[4,136,128]{2,1,0:T(8,128)S(1)}) custom-call(f32[16,16,128]{2,1,0:T(8,128)S(1)} %bitcast.8, f32[16,16,128]{2,1,0:T(8,128)S(1)} %collective-permute-done.left, f32[16,16,128]{2,1,0:T(8,128)S(1)} %collective-permute-done.1.right, f32[16,64,128]{2,1,0:T(8,128)S(1)} %collective-permute-done.6.rows_, ...), custom_call_target="tpu_custom_call" | custom-call | tf_op jit(solution)/shard_map/pallas_call | solution.py:369
  51.9 1.3 %collective-permute-start.9 = (f32[4,136,128]{2,1,0:T(8,128)S(1)}, f32[4,136,128]{2,1,0:T(8,128)S(1)}, u32[]{:S(2)}, u32[]{:S(2)}) collective-permute-start(f32[4,136,128]{2,1,0:T(8,128)S(1)} %get-tuple-element.8), channel_id=1, source_target_pairs={{128,0},{129,1},{130,2},{131,3},{132,4},{133,5},{134,6},{135,7},{1... | collective-permute-start | bytes 835592 | tf_op jit(solution)/shard_map/ppermute | solution.py:450
  53.2 2.9 %collective-permute-done.9 = f32[4,136,128]{2,1,0:T(8,128)S(1)} collective-permute-done((f32[4,136,128]{2,1,0:T(8,128)S(1)}, f32[4,136,128]{2,1,0:T(8,128)S(1)}, u32[]{:S(2)}, u32[]{:S(2)}) %collective-permute-start.9) | collective-permute-done | bytes 278560 | tf_op jit(solution)/shard_map/ppermute | solution.py:450
  56.1 10.5 %all_to_all.16.fields = f32[4,136,128]{2,1,0:T(8,128)S(1)} all-to-all(f32[4,136,128]{2,1,0:T(8,128)S(1)} %broadcast_select_fusion), channel_id=1, replica_groups=mesh['gx_0'=4,'gx_1'=2,'gy'=16,'gz'=8] {'gx_0'}, dimensions={0} | all-to-all | bytes 557056 | tf_op jit(solution)/shard_map/all_to_all | solution.py:452
  66.7 0.0 copy-start
  66.7 36.9 %all_to_all.17 = f32[128,1,128]{2,1,0:T(1,128)S(1)} all-to-all(f32[128,1,128]{2,1,0:T(1,128)S(1)} %broadcast_in_dim.3), channel_id=1, replica_groups=mesh['gx_0'=4,'gx_1'=2,'gy'=16,'gz'=8] {'gy','gz'}, dimensions={0} | all-to-all | bytes 131072 | tf_op jit(solution)/shard_map/all_to_all | solution.py:454
  103.6 0.0 copy-done
  103.6 1.0 shard_map.62
  (4 shorter events, 0.1 us)
Async XLA Ops:
  12.8 3.9 %collective-permute-start.2 = (f32[16,16,128]{2,1,0:T(8,128)S(1)}, f32[16,16,128]{2,1,0:T(8,128)S(1)}, u32[]{:S(2)}, u32[]{:S(2)}) collective-permute-start(f32[16,16,128]{2,1,0:T(8,128)S(1)} %bitcast.2), channel_id=1, source_target_pairs={{128,16},{136,24},{144,32},{152,40},{160,48},{168,56},{176,64},{18... | collective-permute-start | bytes 393224 | tf_op jit(solution)/shard_map/ppermute | solution.py:442
  13.5 3.3 %collective-permute-start.3 = (f32[16,16,128]{2,1,0:T(8,128)S(1)}, f32[16,16,128]{2,1,0:T(8,128)S(1)}, u32[]{:S(2)}, u32[]{:S(2)}) collective-permute-start(f32[16,16,128]{2,1,0:T(8,128)S(1)} %bitcast.3), channel_id=1, source_target_pairs={{128,8},{136,16},{144,24},{152,32},{160,40},{168,48},{176,56},{184... | collective-permute-start | bytes 393224 | tf_op jit(solution)/shard_map/ppermute | solution.py:442
  14.1 12.1 %collective-permute-start.4 = (f32[16,16,128]{2,1,0:T(8,128)S(1)}, f32[16,16,128]{2,1,0:T(8,128)S(1)}, u32[]{:S(2)}, u32[]{:S(2)}) collective-permute-start(f32[16,16,128]{2,1,0:T(8,128)S(1)} %bitcast.4), channel_id=1, source_target_pairs={{136,0},{144,8},{152,16},{160,24},{168,32},{176,40},{184,48},{192,... | collective-permute-start | bytes 393224 | tf_op jit(solution)/shard_map/ppermute | solution.py:442
  15.4 15.2 %collective-permute-start.5 = (f32[16,16,128]{2,1,0:T(8,128)S(1)}, f32[16,16,128]{2,1,0:T(8,128)S(1)}, u32[]{:S(2)}, u32[]{:S(2)}) collective-permute-start(f32[16,16,128]{2,1,0:T(8,128)S(1)} %bitcast.5), channel_id=1, source_target_pairs={{144,0},{152,8},{160,16},{168,24},{176,32},{184,40},{192,48},{200,... | collective-permute-start | bytes 393224 | tf_op jit(solution)/shard_map/ppermute | solution.py:442
  30.7 12.0 %collective-permute-start.6 = (f32[16,64,128]{2,1,0:T(8,128)S(1)}, f32[16,64,128]{2,1,0:T(8,128)S(1)}, u32[]{:S(2)}, u32[]{:S(2)}) collective-permute-start(f32[16,64,128]{2,1,0:T(8,128)S(1)} %shard_map.60), channel_id=1, source_target_pairs={{0,128},{1,129},{2,130},{3,131},{4,132},{5,133},{6,134},{7,135},{8... | collective-permute-start | bytes 1572872 | tf_op jit(solution)/shard_map/ppermute | solution.py:448
  32.0 10.7 %collective-permute-start.7 = (f32[16,64,128]{2,1,0:T(8,128)S(1)}, f32[16,64,128]{2,1,0:T(8,128)S(1)}, u32[]{:S(2)}, u32[]{:S(2)}) collective-permute-start(f32[16,64,128]{2,1,0:T(8,128)S(1)} %shard_map.60), channel_id=1, source_target_pairs={{0,384},{256,640},{512,896},{768,897},{769,641},{513,385},{257,129... | collective-permute-start | bytes 1572872 | tf_op jit(solution)/shard_map/ppermute | solution.py:446
  33.3 9.4 %collective-permute-start.8 = (f32[16,64,128]{2,1,0:T(8,128)S(1)}, f32[16,64,128]{2,1,0:T(8,128)S(1)}, u32[]{:S(2)}, u32[]{:S(2)}) collective-permute-start(f32[16,64,128]{2,1,0:T(8,128)S(1)} %shard_map.60), channel_id=1, source_target_pairs={{256,128},{512,384},{768,640},{769,896},{513,897},{257,641},{1,385... | collective-permute-start | bytes 1572872 | tf_op jit(solution)/shard_map/ppermute | solution.py:447
  34.7 6.7 %collective-permute-start = (f32[16,16,128]{2,1,0:T(8,128)S(1)}, f32[16,16,128]{2,1,0:T(8,128)S(1)}, u32[]{:S(2)}, u32[]{:S(2)}) collective-permute-start(f32[16,16,128]{2,1,0:T(8,128)S(1)} %bitcast.6), channel_id=1, source_target_pairs={{0,384},{256,640},{512,896},{768,897},{769,641},{513,385},{257,129... | collective-permute-start | bytes 393224 | tf_op jit(solution)/shard_map/ppermute | solution.py:443
  36.0 6.7 %collective-permute-start.1 = (f32[16,16,128]{2,1,0:T(8,128)S(1)}, f32[16,16,128]{2,1,0:T(8,128)S(1)}, u32[]{:S(2)}, u32[]{:S(2)}) collective-permute-start(f32[16,16,128]{2,1,0:T(8,128)S(1)} %bitcast.7), channel_id=1, source_target_pairs={{256,128},{512,384},{768,640},{769,896},{513,897},{257,641},{1,385... | collective-permute-start | bytes 393224 | tf_op jit(solution)/shard_map/ppermute | solution.py:444
  51.9 4.2 %collective-permute-start.9 = (f32[4,136,128]{2,1,0:T(8,128)S(1)}, f32[4,136,128]{2,1,0:T(8,128)S(1)}, u32[]{:S(2)}, u32[]{:S(2)}) collective-permute-start(f32[4,136,128]{2,1,0:T(8,128)S(1)} %get-tuple-element.8), channel_id=1, source_target_pairs={{128,0},{129,1},{130,2},{131,3},{132,4},{133,5},{134,6},{135,7},{1... | collective-permute-start | bytes 835592 | tf_op jit(solution)/shard_map/ppermute | solution.py:450
  66.7 36.9 %copy-start = (f32[8,16,128]{2,1,0:T(8,128)S(1)}, f32[8,16,128]{2,1,0:T(8,128)}, u32[]{:S(2)}) copy-start(f32[8,16,128]{2,1,0:T(8,128)} %get-tuple-element.6.rhs) | copy-start | bytes 196612

commit v7 on v6

--- a/solution.py
+++ b/solution.py
@@ -281,7 +281,11 @@
     return result
 
 
-def cycles_kernel(own, left, right, rows_, up, down, out, other, r0, z0, q0, w, v0, f1, v1, e1, e2, f2, t2, mask, mask2):
+def cycles_kernel(*refs):
+    pl.when(lax.axis_index("gx_1") == 0)(lambda: cycles_on_core(*refs))
+
+
+def cycles_on_core(own, left, right, rows_, up, down, out, other, r0, z0, q0, w, v0, f1, v1, e1, e2, f2, t2, mask, mask2):
     gx0, _, gy, gz = place()
 
     def inside(count, height):
@@ -344,7 +348,7 @@
 
     acc = lax.fori_loop(0, NX // 64, sums, (jnp.zeros((8, LANES), jnp.float32),) * 5)
 
-    for odd_slab, ref in enumerate((other, out)):
+    for odd_slab, ref in enumerate((out, other)):
         for t in range(4):
             for k in range(BX):
                 x = BX * (2 * t + odd_slab) + k + 1
@@ -420,7 +424,7 @@
 
 
 def y_pairs(step):
-    return [(16 + a, a + step) for a in range(16) if 0 <= a + step < 16]
+    return [(a, 16 + a + step) for a in range(16) if 0 <= a + step < 16]
 
 
 def z_pairs(step):
@@ -428,7 +432,7 @@
         gz, at = block // 4, block % 4
         return ((at if gz % 2 == 0 else 3 - at) * 2 + core) * 8 + gz
 
-    return [(number(0, a), number(1, a + step)) for a in range(32) if 0 <= a + step < 32]
+    return [(number(1, a), number(0, a + step)) for a in range(32) if 0 <= a + step < 32]
 
 
 Z_AXES = ("gx_0", "gx_1", "gz")
@@ -438,17 +442,17 @@
     rhs, packed = make_rhs(density, x_faces, y_faces, z_faces)
     own = lax.all_to_all(packed, GX, 0, 0, tiled=True).reshape(16, BY, 128)
     moved = []
-    for step in (1, -1, 2, -2):
+    for step in (2, -2, 1, -1):
         moved.append(lax.ppermute(own, ("gx_1", "gy"), y_pairs(step)))
     left = lax.ppermute(own, Z_AXES, z_pairs(1))
     right = lax.ppermute(own, Z_AXES, z_pairs(-1))
-    rows = join(moved[2], moved[0], moved[1], moved[3])
+    rows = join(moved[0], moved[2], moved[3], moved[1])
     up = lax.ppermute(rows, Z_AXES, z_pairs(1))
     down = lax.ppermute(rows, Z_AXES, z_pairs(-1))
-    rows = lax.ppermute(rows, "gx_1", [(0, 1)])
+    rows = lax.ppermute(rows, "gx_1", [(1, 0)])
     packed, other = cycles(own, left, right, rows, up, down)
-    other = lax.ppermute(other, "gx_1", [(1, 0)])
-    packed = jnp.where(lax.axis_index("gx_1") == 0, other, packed)
+    other = lax.ppermute(other, "gx_1", [(0, 1)])
+    packed = jnp.where(lax.axis_index("gx_1") == 1, other, packed)
     fields = lax.all_to_all(packed, "gx_0", 0, 0, tiled=True)
     sums = jnp.sum(fields[:, BX * BY, :], axis=0)
     sums = lax.all_to_all(jnp.broadcast_to(sums, (128, 1, 128)), ("gy", "gz"), 0, 0, tiled=True)

time: 105 us -> 105 us (level)
  waiting for transfers between devices: 22.2 us -> 17.5 us
  starting transfers between devices: 11.8 us -> 15.7 us
    ppermute x4, waiting for transfers between devices: 13.9 us -> 1.2 us  [local(): moved.append(lax.ppermute(own, ('gx_1', 'gy'), y_pairs(step)))]
    ppermute x1, waiting for transfers between devices: 4.11 us -> 12.8 us  [local(): left = lax.ppermute(own, Z_AXES, z_pairs(1))]
    ppermute x4, starting transfers between devices: 3.91 us -> 7.97 us  [local(): moved.append(lax.ppermute(own, ('gx_1', 'gy'), y_pairs(step)))]
    ppermute x2, waiting for transfers between devices: 2.88 us -> 1.15 us  [the longest x1 1.15 us: local(): other = lax.ppermute(other, 'gx_1', [(0, 1)])]
  transfers between devices with their start and end apart: 10 -> 10, of which waited for: 5 -> 4; matrix products, arithmetic and copies ran while one was open for 0% -> 0% of each run, Pallas kernels for 0% -> 0%
where the time goes in v7:
time: 105 us; the launch traced here: 104 us
  blocking collectives  58.1 us (55%)
  waiting for transfers between devices  17.5 us (17%)
  starting transfers between devices  15.7 us (15%)
  Pallas kernels  11.9 us (11%)
    all_to_all x1, blocking collectives, local(): lax.all_to_all(jnp.broadcast_to(sums, (128, 1, 128)), ('gy', 'gz'), 0, 0,...  36.9 us
    ppermute x1, waiting for transfers between devices, local(): left = lax.ppermute(own, Z_AXES, z_pairs(1))  12.8 us
    all_to_all x1, blocking collectives, local(): fields = lax.all_to_all(packed, 'gx_0', 0, 0, tiled=True)  10.8 us
    all_to_all x1, blocking collectives, local(): own = lax.all_to_all(packed, GX, 0, 0, tiled=True).reshape(16, BY, 128)  10.4 us
    pallas_call x1, Pallas kernels, cycles(): pl.pallas_call(cycles_kernel, out_shape=(jax.ShapeDtypeStruct((4, BX * BY...  9.19 us
    ppermute x4, starting transfers between devices, local(): moved.append(lax.ppermute(own, ('gx_1', 'gy'), y_pairs(step)))  7.97 us
    ppermute x1, waiting for transfers between devices, local(): right = lax.ppermute(own, Z_AXES, z_pairs(-1))  2.34 us
  transfers between devices with their start and end apart: 10, of which 4 were waited for; matrix products, arithmetic and copies ran while one was open for 0% of the time, Pallas kernels for 0%

profile of v7, /device:TPU:8, one launch (start us, length us, event | category | flops | bytes accessed | tf_op | source)
XLA Modules:
  0.0 104.1 jit_solution(9715557808700884998)
XLA Ops:
  0.6 1.8 %shard_map.59 = (f32[8,16,128]{2,1,0:T(8,128)}, f32[8,2,16,128]{3,2,1,0:T(8,128)}) custom-call(f32[8,16,128]{2,1,0:T(8,128)} %density_in.1, f32[2,16,128]{2,1,0:T(8,128)} %xf_in.1, f32[2,8,128]{2,1,0:T(8,128)} %yf_in.1, f32[2,8,16]{2,1,0:T(8,128)} %zf_in.1), custom_call_target="tpu_custom_call" | custom-call | tf_op jit(solution)/shard_map/pallas_call | solution.py:95
  2.4 10.4 %all_to_all.15 = f32[8,2,16,128]{3,2,1,0:T(8,128)S(1)} all-to-all(f32[8,2,16,128]{3,2,1,0:T(8,128)} %get-tuple-element.7), channel_id=1, replica_groups=mesh['gx_0'=4,'gx_1'=2,'gy'=16,'gz'=8] {'gx_0','gx_1'}, dimensions={0} | all-to-all | bytes 262144 | tf_op jit(solution)/shard_map/all_to_all | solution.py:443
  12.8 5.3 %collective-permute-start.2 = (f32[16,16,128]{2,1,0:T(8,128)S(1)}, f32[16,16,128]{2,1,0:T(8,128)S(1)}, u32[]{:S(2)}, u32[]{:S(2)}) collective-permute-start(f32[16,16,128]{2,1,0:T(8,128)S(1)} %bitcast.2), channel_id=1, source_target_pairs={{0,144},{8,152},{16,160},{24,168},{32,176},{40,184},{48,192},{56,2... | collective-permute-start | bytes 393224 | tf_op jit(solution)/shard_map/ppermute | solution.py:446
  18.1 1.3 %collective-permute-start.3 = (f32[16,16,128]{2,1,0:T(8,128)S(1)}, f32[16,16,128]{2,1,0:T(8,128)S(1)}, u32[]{:S(2)}, u32[]{:S(2)}) collective-permute-start(f32[16,16,128]{2,1,0:T(8,128)S(1)} %bitcast.3), channel_id=1, source_target_pairs={{0,136},{8,144},{16,152},{24,160},{32,168},{40,176},{48,184},{56,1... | collective-permute-start | bytes 393224 | tf_op jit(solution)/shard_map/ppermute | solution.py:446
  19.4 0.7 collective-permute-start.4
  20.1 0.7 collective-permute-start.5
  20.8 0.0 collective-permute-done.2.refs_0_
  20.8 1.2 %collective-permute-done.3.refs_1_ = f32[16,16,128]{2,1,0:T(8,128)S(1)} collective-permute-done((f32[16,16,128]{2,1,0:T(8,128)S(1)}, f32[16,16,128]{2,1,0:T(8,128)S(1)}, u32[]{:S(2)}, u32[]{:S(2)}) %collective-permute-start.3) | collective-permute-done | bytes 131104 | tf_op jit(solution)/shard_map/ppermute | solution.py:446
  22.0 0.0 collective-permute-done.4.refs_2_
  22.0 0.0 collective-permute-done.5.refs_3_
  22.1 1.3 %collective-permute-start.6 = (f32[16,64,128]{2,1,0:T(8,128)S(1)}, f32[16,64,128]{2,1,0:T(8,128)S(1)}, u32[]{:S(2)}, u32[]{:S(2)}) collective-permute-start(f32[16,64,128]{2,1,0:T(8,128)S(1)} %shard_map.60), channel_id=1, source_target_pairs={{128,0},{129,1},{130,2},{131,3},{132,4},{133,5},{134,6},{135,7},{1... | collective-permute-start | bytes 1572872 | tf_op jit(solution)/shard_map/ppermute | solution.py:452
  23.4 1.3 %collective-permute-start.7 = (f32[16,64,128]{2,1,0:T(8,128)S(1)}, f32[16,64,128]{2,1,0:T(8,128)S(1)}, u32[]{:S(2)}, u32[]{:S(2)}) collective-permute-start(f32[16,64,128]{2,1,0:T(8,128)S(1)} %shard_map.60), channel_id=1, source_target_pairs={{128,256},{384,512},{640,768},{896,769},{897,513},{641,257},{385,1... | collective-permute-start | bytes 1572872 | tf_op jit(solution)/shard_map/ppermute | solution.py:450
  24.7 1.3 %collective-permute-start.8 = (f32[16,64,128]{2,1,0:T(8,128)S(1)}, f32[16,64,128]{2,1,0:T(8,128)S(1)}, u32[]{:S(2)}, u32[]{:S(2)}) collective-permute-start(f32[16,64,128]{2,1,0:T(8,128)S(1)} %shard_map.60), channel_id=1, source_target_pairs={{384,0},{640,256},{896,512},{897,768},{641,769},{385,513},{129,257... | collective-permute-start | bytes 1572872 | tf_op jit(solution)/shard_map/ppermute | solution.py:451
  26.0 1.3 %collective-permute-start = (f32[16,16,128]{2,1,0:T(8,128)S(1)}, f32[16,16,128]{2,1,0:T(8,128)S(1)}, u32[]{:S(2)}, u32[]{:S(2)}) collective-permute-start(f32[16,16,128]{2,1,0:T(8,128)S(1)} %bitcast.6), channel_id=1, source_target_pairs={{128,256},{384,512},{640,768},{896,769},{897,513},{641,257},{385,1... | collective-permute-start | bytes 393224 | tf_op jit(solution)/shard_map/ppermute | solution.py:447
  27.3 1.3 %collective-permute-start.1 = (f32[16,16,128]{2,1,0:T(8,128)S(1)}, f32[16,16,128]{2,1,0:T(8,128)S(1)}, u32[]{:S(2)}, u32[]{:S(2)}) collective-permute-start(f32[16,16,128]{2,1,0:T(8,128)S(1)} %bitcast.7), channel_id=1, source_target_pairs={{384,0},{640,256},{896,512},{897,768},{641,769},{385,513},{129,257... | collective-permute-start | bytes 393224 | tf_op jit(solution)/shard_map/ppermute | solution.py:448
  28.6 12.8 %collective-permute-done.refs_1_ = f32[16,16,128]{2,1,0:T(8,128)S(1)} collective-permute-done((f32[16,16,128]{2,1,0:T(8,128)S(1)}, f32[16,16,128]{2,1,0:T(8,128)S(1)}, u32[]{:S(2)}, u32[]{:S(2)}) %collective-permute-start) | collective-permute-done | bytes 131104 | tf_op jit(solution)/shard_map/ppermute | solution.py:447
  41.4 2.3 %collective-permute-done.1.refs_2_ = f32[16,16,128]{2,1,0:T(8,128)S(1)} collective-permute-done((f32[16,16,128]{2,1,0:T(8,128)S(1)}, f32[16,16,128]{2,1,0:T(8,128)S(1)}, u32[]{:S(2)}, u32[]{:S(2)}) %collective-permute-start.1) | collective-permute-done | bytes 131104 | tf_op jit(solution)/shard_map/ppermute | solution.py:448
  43.7 0.0 collective-permute-done.6.refs_3_
  43.7 0.0 collective-permute-done.7.refs_4_
  43.7 0.0 collective-permute-done.8.refs_5_
  43.7 9.2 %shard_map.61 = (f32[4,136,128]{2,1,0:T(8,128)S(1)}, f32[4,136,128]{2,1,0:T(8,128)S(1)}) custom-call(f32[16,16,128]{2,1,0:T(8,128)S(1)} %bitcast.8, f32[16,16,128]{2,1,0:T(8,128)S(1)} %collective-permute-done.refs_1_, f32[16,16,128]{2,1,0:T(8,128)S(1)} %collective-permute-done.1.refs_2_, f32[16,64,128]{2,1,0:T(8,128)S(1)} %collective-permute-done.6.refs_3_, ...), custom_call_target="tpu_custom_call" | custom-call | tf_op jit(solution)/shard_map/pallas_call | solution.py:373
  52.9 1.3 %collective-permute-start.9 = (f32[4,136,128]{2,1,0:T(8,128)S(1)}, f32[4,136,128]{2,1,0:T(8,128)S(1)}, u32[]{:S(2)}, u32[]{:S(2)}) collective-permute-start(f32[4,136,128]{2,1,0:T(8,128)S(1)} %get-tuple-element.8), channel_id=1, source_target_pairs={{0,128},{1,129},{2,130},{3,131},{4,132},{5,133},{6,134},{7,135},{8... | collective-permute-start | bytes 835592 | tf_op jit(solution)/shard_map/ppermute | solution.py:454
  54.2 1.1 %collective-permute-done.9 = f32[4,136,128]{2,1,0:T(8,128)S(1)} collective-permute-done((f32[4,136,128]{2,1,0:T(8,128)S(1)}, f32[4,136,128]{2,1,0:T(8,128)S(1)}, u32[]{:S(2)}, u32[]{:S(2)}) %collective-permute-start.9) | collective-permute-done | bytes 278560 | tf_op jit(solution)/shard_map/ppermute | solution.py:454
  55.4 10.8 %all_to_all.16.fields = f32[4,136,128]{2,1,0:T(8,128)S(1)} all-to-all(f32[4,136,128]{2,1,0:T(8,128)S(1)} %broadcast_select_fusion), channel_id=1, replica_groups=mesh['gx_0'=4,'gx_1'=2,'gy'=16,'gz'=8] {'gx_0'}, dimensions={0} | all-to-all | bytes 557056 | tf_op jit(solution)/shard_map/all_to_all | solution.py:456
  66.2 0.0 copy-start
  66.2 36.9 %all_to_all.17 = f32[128,1,128]{2,1,0:T(1,128)S(1)} all-to-all(f32[128,1,128]{2,1,0:T(1,128)S(1)} %broadcast_in_dim.3), channel_id=1, replica_groups=mesh['gx_0'=4,'gx_1'=2,'gy'=16,'gz'=8] {'gy','gz'}, dimensions={0} | all-to-all | bytes 131072 | tf_op jit(solution)/shard_map/all_to_all | solution.py:458
  103.1 0.0 copy-done
  103.2 1.0 shard_map.62
  (4 shorter events, 0.1 us)
Async XLA Ops:
  12.8 8.0 %collective-permute-start.2 = (f32[16,16,128]{2,1,0:T(8,128)S(1)}, f32[16,16,128]{2,1,0:T(8,128)S(1)}, u32[]{:S(2)}, u32[]{:S(2)}) collective-permute-start(f32[16,16,128]{2,1,0:T(8,128)S(1)} %bitcast.2), channel_id=1, source_target_pairs={{0,144},{8,152},{16,160},{24,168},{32,176},{40,184},{48,192},{56,2... | collective-permute-start | bytes 393224 | tf_op jit(solution)/shard_map/ppermute | solution.py:446
  18.1 3.9 %collective-permute-start.3 = (f32[16,16,128]{2,1,0:T(8,128)S(1)}, f32[16,16,128]{2,1,0:T(8,128)S(1)}, u32[]{:S(2)}, u32[]{:S(2)}) collective-permute-start(f32[16,16,128]{2,1,0:T(8,128)S(1)} %bitcast.3), channel_id=1, source_target_pairs={{0,136},{8,144},{16,152},{24,160},{32,168},{40,176},{48,184},{56,1... | collective-permute-start | bytes 393224 | tf_op jit(solution)/shard_map/ppermute | solution.py:446
  19.4 2.6 %collective-permute-start.4 = (f32[16,16,128]{2,1,0:T(8,128)S(1)}, f32[16,16,128]{2,1,0:T(8,128)S(1)}, u32[]{:S(2)}, u32[]{:S(2)}) collective-permute-start(f32[16,16,128]{2,1,0:T(8,128)S(1)} %bitcast.4), channel_id=1, source_target_pairs={{8,128},{16,136},{24,144},{32,152},{40,160},{48,168},{56,176},{64,... | collective-permute-start | bytes 393224 | tf_op jit(solution)/shard_map/ppermute | solution.py:446
  20.1 1.9 %collective-permute-start.5 = (f32[16,16,128]{2,1,0:T(8,128)S(1)}, f32[16,16,128]{2,1,0:T(8,128)S(1)}, u32[]{:S(2)}, u32[]{:S(2)}) collective-permute-start(f32[16,16,128]{2,1,0:T(8,128)S(1)} %bitcast.5), channel_id=1, source_target_pairs={{16,128},{24,136},{32,144},{40,152},{48,160},{56,168},{64,176},{72... | collective-permute-start | bytes 393224 | tf_op jit(solution)/shard_map/ppermute | solution.py:446
  22.1 21.7 %collective-permute-start.6 = (f32[16,64,128]{2,1,0:T(8,128)S(1)}, f32[16,64,128]{2,1,0:T(8,128)S(1)}, u32[]{:S(2)}, u32[]{:S(2)}) collective-permute-start(f32[16,64,128]{2,1,0:T(8,128)S(1)} %shard_map.60), channel_id=1, source_target_pairs={{128,0},{129,1},{130,2},{131,3},{132,4},{133,5},{134,6},{135,7},{1... | collective-permute-start | bytes 1572872 | tf_op jit(solution)/shard_map/ppermute | solution.py:452
  23.4 20.4 %collective-permute-start.7 = (f32[16,64,128]{2,1,0:T(8,128)S(1)}, f32[16,64,128]{2,1,0:T(8,128)S(1)}, u32[]{:S(2)}, u32[]{:S(2)}) collective-permute-start(f32[16,64,128]{2,1,0:T(8,128)S(1)} %shard_map.60), channel_id=1, source_target_pairs={{128,256},{384,512},{640,768},{896,769},{897,513},{641,257},{385,1... | collective-permute-start | bytes 1572872 | tf_op jit(solution)/shard_map/ppermute | solution.py:450
  24.7 19.1 %collective-permute-start.8 = (f32[16,64,128]{2,1,0:T(8,128)S(1)}, f32[16,64,128]{2,1,0:T(8,128)S(1)}, u32[]{:S(2)}, u32[]{:S(2)}) collective-permute-start(f32[16,64,128]{2,1,0:T(8,128)S(1)} %shard_map.60), channel_id=1, source_target_pairs={{384,0},{640,256},{896,512},{897,768},{641,769},{385,513},{129,257... | collective-permute-start | bytes 1572872 | tf_op jit(solution)/shard_map/ppermute | solution.py:451
  26.0 15.4 %collective-permute-start = (f32[16,16,128]{2,1,0:T(8,128)S(1)}, f32[16,16,128]{2,1,0:T(8,128)S(1)}, u32[]{:S(2)}, u32[]{:S(2)}) collective-permute-start(f32[16,16,128]{2,1,0:T(8,128)S(1)} %bitcast.6), channel_id=1, source_target_pairs={{128,256},{384,512},{640,768},{896,769},{897,513},{641,257},{385,1... | collective-permute-start | bytes 393224 | tf_op jit(solution)/shard_map/ppermute | solution.py:447
  27.3 16.5 %collective-permute-start.1 = (f32[16,16,128]{2,1,0:T(8,128)S(1)}, f32[16,16,128]{2,1,0:T(8,128)S(1)}, u32[]{:S(2)}, u32[]{:S(2)}) collective-permute-start(f32[16,16,128]{2,1,0:T(8,128)S(1)} %bitcast.7), channel_id=1, source_target_pairs={{384,0},{640,256},{896,512},{897,768},{641,769},{385,513},{129,257... | collective-permute-start | bytes 393224 | tf_op jit(solution)/shard_map/ppermute | solution.py:448
  52.9 2.5 %collective-permute-start.9 = (f32[4,136,128]{2,1,0:T(8,128)S(1)}, f32[4,136,128]{2,1,0:T(8,128)S(1)}, u32[]{:S(2)}, u32[]{:S(2)}) collective-permute-start(f32[4,136,128]{2,1,0:T(8,128)S(1)} %get-tuple-element.8), channel_id=1, source_target_pairs={{0,128},{1,129},{2,130},{3,131},{4,132},{5,133},{6,134},{7,135},{8... | collective-permute-start | bytes 835592 | tf_op jit(solution)/shard_map/ppermute | solution.py:454
  66.2 36.9 %copy-start = (f32[8,16,128]{2,1,0:T(8,128)S(1)}, f32[8,16,128]{2,1,0:T(8,128)}, u32[]{:S(2)}) copy-start(f32[8,16,128]{2,1,0:T(8,128)} %get-tuple-element.6.rhs) | copy-start | bytes 196612

commit v8 on v7

--- a/solution.py
+++ b/solution.py
@@ -124,6 +124,39 @@
     )(*blocks)
 
 
+def unpack_kernel(*refs):
+    pl.when(lax.axis_index("gx_1") == 0)(lambda: unpack_on_core(*refs))
+
+
+def unpack_on_core(own, left, right, rows_, out):
+    lanes = lane_index((8, LANES))
+    even = lanes // 32 % 2 == 0
+    for i in range(16):
+        for odd in range(2):
+            for b in range(4):
+                c = rows_[i, pl.ds(BY * b + 8 * odd, 8)]
+                for k in range(4):
+                    out[4 * i + k, odd, pl.ds(8 * (b + b // 2), 8)] = roll(c, 32 - 32 * k, 1)
+            part = pl.ds(8 * odd, 8)
+            a, c, d = left[i, part], own[i, part], right[i, part]
+            low = jnp.where(lanes < 64, a, roll(d, 64, 1))
+            high = jnp.where(lanes < 64, roll(a, 64, 1), d)
+            out[4 * i, odd, 16:24] = jnp.where(even, low, roll(c, 32, 1))
+            out[4 * i + 1, odd, 16:24] = jnp.where(even, roll(low, -32, 1), c)
+            out[4 * i + 2, odd, 16:24] = jnp.where(even, high, roll(c, -32, 1))
+            out[4 * i + 3, odd, 16:24] = jnp.where(even, roll(high, -32, 1), roll(c, 64, 1))
+
+
+def unpack(own, left, right, rows):
+    return pl.pallas_call(
+        unpack_kernel,
+        out_shape=jax.ShapeDtypeStruct((NX, 2, 40, LANES), jnp.float32),
+        in_specs=[VMEM] * 4,
+        out_specs=VMEM,
+        compiler_params=small(),
+    )(own, left, right, rows)
+
+
 def at(row, step=0):
     return pl.ds(8 + row + step, 8)
 
@@ -204,23 +237,23 @@
     def sweep1(first):
         for r in rows:
             m = mask2[at(r)]
-            for x in range(1, 9):
+            for x in range(1, 17):
                 v = f2[first + x, at(r)]
                 s = (4.0 / 3.0) * v + relax * (around(f2, first + x, r) + sides(v, 4))
                 t2[first + x, at(r)] = (relax * s) * m
 
-    chunks(NX // 4, 8, sweep1)
+    chunks(NX // 4, 16, sweep1)
 
     def sweep2(first):
         for r in last:
             m = mask2[at(r)]
-            for x in range(1, 9):
+            for x in range(1, 17):
                 v = t2[first + x, at(r)]
                 s = (third(v) + relax * (f2[first + x, at(r)] + (around(t2, first + x, r) + sides(v, 4)))) * m
                 e2[first + x, every_other(r), :] = s
                 e2[first + x, every_other(r, 1), :] = s
 
-    chunks(NX // 4, 8, sweep2)
+    chunks(NX // 4, 16, sweep2)
 
 
 def cycle_up(src, mask, f1, e2, v1, e1, v0, out, rows1, last1, rows0, last0, nd, ne):
@@ -248,13 +281,13 @@
     def correct0(first):
         for odd in range(2):
             for r in rows0[odd]:
-                for i in range(1, 5):
+                for i in range(1, 33):
                     e = e1[first + i, at(r)]
                     for k in (-1, 0):
                         x = 2 * first + 2 * i + k
                         v0[x, odd, at(r)] = relax * src[x, odd, at(r)] + e
 
-    chunks(NX // 2, 4, correct0)
+    chunks(NX // 2, 32, correct0)
 
     def smooth0(first):
         for odd in range(2):
@@ -285,7 +318,7 @@
     pl.when(lax.axis_index("gx_1") == 0)(lambda: cycles_on_core(*refs))
 
 
-def cycles_on_core(own, left, right, rows_, up, down, out, other, r0, z0, q0, w, v0, f1, v1, e1, e2, f2, t2, mask, mask2):
+def cycles_on_core(known, up, down, out, other, r0, z0, q0, w, v0, f1, v1, e1, e2, f2, t2, mask, mask2):
     gx0, _, gy, gz = place()
 
     def inside(count, height):
@@ -300,19 +333,25 @@
         ref[0] = jnp.zeros(ref.shape[1:], jnp.float32)
         ref[count + 1] = jnp.zeros(ref.shape[1:], jnp.float32)
     lanes = lane_index((8, LANES))
-    y_blocks = [tuple(ref.at[:, pl.ds(BY * b, BY)] for ref in (up, rows_, down)) for b in range(4)]
-    y_blocks.insert(2, (left, own, right))
-
-    def unpack(i, _):
-        for b, sources in enumerate(y_blocks):
-            for odd in range(2):
-                a, c, d = (ref[i, pl.ds(8 * odd, 8)] for ref in sources)
-                for k in range(4):
-                    value = jnp.where(lanes < 32, roll(a, -32 * k, 1), jnp.where(lanes < 64, roll(c, 32 - 32 * k, 1), roll(d, 64 - 32 * k, 1)))
-                    r0[4 * i + k + 1, odd, at(8 * b)] = value
+    between = (lanes >= HZ) & (lanes < HZ + CZ)
+
+    def corners_in(i, _):
+        for odd in range(2):
+            for b in range(5):
+                if b == 2:
+                    corners = (None,) * 4
+                else:
+                    part = pl.ds(BY * (b - b // 3) + 8 * odd, 8)
+                    a, d = up[i, part], down[i, part]
+                    one = jnp.where(lanes < 64, a, roll(d, 64, 1))
+                    two = jnp.where(lanes < 64, roll(a, 64, 1), d)
+                    corners = (one, roll(one, -32, 1), two, roll(two, -32, 1))
+                for k, corner in enumerate(corners):
+                    value = known[4 * i + k, odd, pl.ds(8 * b, 8)]
+                    r0[4 * i + k + 1, odd, at(8 * b)] = value if corner is None else jnp.where(between, value, corner)
         return 0
 
-    lax.fori_loop(0, NX // 4, unpack, 0, unroll=16)
+    lax.fori_loop(0, 16, corners_in, 0, unroll=4)
     low = {step: lanes & step == 0 for step in (1, 2)}
 
     def fold(x, step):
@@ -373,7 +412,7 @@
     return pl.pallas_call(
         cycles_kernel,
         out_shape=(jax.ShapeDtypeStruct((4, BX * BY + 8, LANES), jnp.float32),) * 2,
-        in_specs=[VMEM] * 6,
+        in_specs=[VMEM] * 3,
         out_specs=(VMEM, VMEM),
         scratch_shapes=[fine] * 5
         + [level1] * 3
@@ -450,7 +489,8 @@
     up = lax.ppermute(rows, Z_AXES, z_pairs(1))
     down = lax.ppermute(rows, Z_AXES, z_pairs(-1))
     rows = lax.ppermute(rows, "gx_1", [(1, 0)])
-    packed, other = cycles(own, left, right, rows, up, down)
+    known = unpack(own, left, right, rows)
+    packed, other = cycles(known, up, down)
     other = lax.ppermute(other, "gx_1", [(0, 1)])
     packed = jnp.where(lax.axis_index("gx_1") == 1, other, packed)
     fields = lax.all_to_all(packed, "gx_0", 0, 0, tiled=True)

time: 105 us -> 106 us (level)
  Pallas kernels: 11.9 us -> 13.1 us
    pallas_call x0 -> x1, Pallas kernels: none -> 2.43 us  [unpack(): pl.pallas_call(unpack_kernel, out_shape=jax.ShapeDtypeStruct((NX, 2, 40,...]
    pallas_call x1, Pallas kernels: 9.19 us -> 7.92 us  [cycles(): pl.pallas_call(cycles_kernel, out_shape=(jax.ShapeDtypeStruct((4, BX * BY...]
  transfers between devices with their start and end apart: 10 -> 10, of which waited for: 4 -> 4; matrix products, arithmetic and copies ran while one was open for 0% -> 0% of each run, Pallas kernels for 0% -> 2%
where the time goes in v8:
time: 106 us; the launch traced here: 105 us
  blocking collectives  57.9 us (55%)
  waiting for transfers between devices  17.5 us (17%)
  starting transfers between devices  15.7 us (15%)
  Pallas kernels  13.1 us (12%)
    all_to_all x1, blocking collectives, local(): lax.all_to_all(jnp.broadcast_to(sums, (128, 1, 128)), ('gy', 'gz'), 0, 0,...  36.8 us
    ppermute x1, waiting for transfers between devices, local(): left = lax.ppermute(own, Z_AXES, z_pairs(1))  12.8 us
    all_to_all x1, blocking collectives, local(): fields = lax.all_to_all(packed, 'gx_0', 0, 0, tiled=True)  10.8 us
    all_to_all x1, blocking collectives, local(): own = lax.all_to_all(packed, GX, 0, 0, tiled=True).reshape(16, BY, 128)  10.4 us
    ppermute x4, starting transfers between devices, local(): moved.append(lax.ppermute(own, ('gx_1', 'gy'), y_pairs(step)))  7.97 us
    pallas_call x1, Pallas kernels, cycles(): pl.pallas_call(cycles_kernel, out_shape=(jax.ShapeDtypeStruct((4, BX * BY...  7.92 us
    pallas_call x1, Pallas kernels, unpack(): pl.pallas_call(unpack_kernel, out_shape=jax.ShapeDtypeStruct((NX, 2, 40,...  2.43 us
    ppermute x1, waiting for transfers between devices, local(): right = lax.ppermute(own, Z_AXES, z_pairs(-1))  2.34 us
  transfers between devices with their start and end apart: 10, of which 4 were waited for; matrix products, arithmetic and copies ran while one was open for 0% of the time, Pallas kernels for 2%

profile of v8, /device:TPU:8, one launch (start us, length us, event | category | flops | bytes accessed | tf_op | source)
XLA Modules:
  0.0 105.1 jit_solution(3169251626207439509)
XLA Ops:
  0.6 1.8 %shard_map.59 = (f32[8,16,128]{2,1,0:T(8,128)}, f32[8,2,16,128]{3,2,1,0:T(8,128)}) custom-call(f32[8,16,128]{2,1,0:T(8,128)} %density_in.1, f32[2,16,128]{2,1,0:T(8,128)} %xf_in.1, f32[2,8,128]{2,1,0:T(8,128)} %yf_in.1, f32[2,8,16]{2,1,0:T(8,128)} %zf_in.1), custom_call_target="tpu_custom_call" | custom-call | tf_op jit(solution)/shard_map/pallas_call | solution.py:95
  2.4 10.4 %all_to_all.15 = f32[8,2,16,128]{3,2,1,0:T(8,128)S(1)} all-to-all(f32[8,2,16,128]{3,2,1,0:T(8,128)} %get-tuple-element.7), channel_id=1, replica_groups=mesh['gx_0'=4,'gx_1'=2,'gy'=16,'gz'=8] {'gx_0','gx_1'}, dimensions={0} | all-to-all | bytes 262144 | tf_op jit(solution)/shard_map/all_to_all | solution.py:482
  12.8 5.3 %collective-permute-start.2 = (f32[16,16,128]{2,1,0:T(8,128)S(1)}, f32[16,16,128]{2,1,0:T(8,128)S(1)}, u32[]{:S(2)}, u32[]{:S(2)}) collective-permute-start(f32[16,16,128]{2,1,0:T(8,128)S(1)} %bitcast.2), channel_id=1, source_target_pairs={{0,144},{8,152},{16,160},{24,168},{32,176},{40,184},{48,192},{56,2... | collective-permute-start | bytes 393224 | tf_op jit(solution)/shard_map/ppermute | solution.py:485
  18.1 1.3 %collective-permute-start.3 = (f32[16,16,128]{2,1,0:T(8,128)S(1)}, f32[16,16,128]{2,1,0:T(8,128)S(1)}, u32[]{:S(2)}, u32[]{:S(2)}) collective-permute-start(f32[16,16,128]{2,1,0:T(8,128)S(1)} %bitcast.3), channel_id=1, source_target_pairs={{0,136},{8,144},{16,152},{24,160},{32,168},{40,176},{48,184},{56,1... | collective-permute-start | bytes 393224 | tf_op jit(solution)/shard_map/ppermute | solution.py:485
  19.4 0.7 collective-permute-start.4
  20.1 0.7 collective-permute-start.5
  20.8 0.0 collective-permute-done.2.refs_0_
  20.8 1.2 %collective-permute-done.3.refs_1_ = f32[16,16,128]{2,1,0:T(8,128)S(1)} collective-permute-done((f32[16,16,128]{2,1,0:T(8,128)S(1)}, f32[16,16,128]{2,1,0:T(8,128)S(1)}, u32[]{:S(2)}, u32[]{:S(2)}) %collective-permute-start.3) | collective-permute-done | bytes 131104 | tf_op jit(solution)/shard_map/ppermute | solution.py:485
  22.0 0.0 collective-permute-done.4.refs_2_
  22.0 0.0 collective-permute-done.5.refs_3_
  22.1 1.3 %collective-permute-start.6 = (f32[16,64,128]{2,1,0:T(8,128)S(1)}, f32[16,64,128]{2,1,0:T(8,128)S(1)}, u32[]{:S(2)}, u32[]{:S(2)}) collective-permute-start(f32[16,64,128]{2,1,0:T(8,128)S(1)} %shard_map.60), channel_id=1, source_target_pairs={{128,0},{129,1},{130,2},{131,3},{132,4},{133,5},{134,6},{135,7},{1... | collective-permute-start | bytes 1572872 | tf_op jit(solution)/shard_map/ppermute | solution.py:491
  23.4 1.3 %collective-permute-start.7 = (f32[16,64,128]{2,1,0:T(8,128)S(1)}, f32[16,64,128]{2,1,0:T(8,128)S(1)}, u32[]{:S(2)}, u32[]{:S(2)}) collective-permute-start(f32[16,64,128]{2,1,0:T(8,128)S(1)} %shard_map.60), channel_id=1, source_target_pairs={{128,256},{384,512},{640,768},{896,769},{897,513},{641,257},{385,1... | collective-permute-start | bytes 1572872 | tf_op jit(solution)/shard_map/ppermute | solution.py:489
  24.7 1.3 %collective-permute-start.8 = (f32[16,64,128]{2,1,0:T(8,128)S(1)}, f32[16,64,128]{2,1,0:T(8,128)S(1)}, u32[]{:S(2)}, u32[]{:S(2)}) collective-permute-start(f32[16,64,128]{2,1,0:T(8,128)S(1)} %shard_map.60), channel_id=1, source_target_pairs={{384,0},{640,256},{896,512},{897,768},{641,769},{385,513},{129,257... | collective-permute-start | bytes 1572872 | tf_op jit(solution)/shard_map/ppermute | solution.py:490
  26.0 1.3 %collective-permute-start = (f32[16,16,128]{2,1,0:T(8,128)S(1)}, f32[16,16,128]{2,1,0:T(8,128)S(1)}, u32[]{:S(2)}, u32[]{:S(2)}) collective-permute-start(f32[16,16,128]{2,1,0:T(8,128)S(1)} %bitcast.6), channel_id=1, source_target_pairs={{128,256},{384,512},{640,768},{896,769},{897,513},{641,257},{385,1... | collective-permute-start | bytes 393224 | tf_op jit(solution)/shard_map/ppermute | solution.py:486
  27.3 1.3 %collective-permute-start.1 = (f32[16,16,128]{2,1,0:T(8,128)S(1)}, f32[16,16,128]{2,1,0:T(8,128)S(1)}, u32[]{:S(2)}, u32[]{:S(2)}) collective-permute-start(f32[16,16,128]{2,1,0:T(8,128)S(1)} %bitcast.7), channel_id=1, source_target_pairs={{384,0},{640,256},{896,512},{897,768},{641,769},{385,513},{129,257... | collective-permute-start | bytes 393224 | tf_op jit(solution)/shard_map/ppermute | solution.py:487
  28.6 12.8 %collective-permute-done.refs_1_ = f32[16,16,128]{2,1,0:T(8,128)S(1)} collective-permute-done((f32[16,16,128]{2,1,0:T(8,128)S(1)}, f32[16,16,128]{2,1,0:T(8,128)S(1)}, u32[]{:S(2)}, u32[]{:S(2)}) %collective-permute-start) | collective-permute-done | bytes 131104 | tf_op jit(solution)/shard_map/ppermute | solution.py:486
  41.4 2.3 %collective-permute-done.1.refs_2_ = f32[16,16,128]{2,1,0:T(8,128)S(1)} collective-permute-done((f32[16,16,128]{2,1,0:T(8,128)S(1)}, f32[16,16,128]{2,1,0:T(8,128)S(1)}, u32[]{:S(2)}, u32[]{:S(2)}) %collective-permute-start.1) | collective-permute-done | bytes 131104 | tf_op jit(solution)/shard_map/ppermute | solution.py:487
  43.7 0.0 collective-permute-done.6.refs_3_
  43.7 2.4 %shard_map.61.refs_0_ = f32[64,2,40,128]{3,2,1,0:T(8,128)S(1)} custom-call(f32[16,16,128]{2,1,0:T(8,128)S(1)} %bitcast.8, f32[16,16,128]{2,1,0:T(8,128)S(1)} %collective-permute-done.refs_1_, f32[16,16,128]{2,1,0:T(8,128)S(1)} %collective-permute-done.1.refs_2_, f32[16,64,128]{2,1,0:T(8,128)S(1)} %collective-permute-done.6.refs_3_), custom_call_target="tpu_custom_call" | custom-call | tf_op jit(solution)/shard_map/pallas_call | solution.py:151
  46.1 0.0 copy-start
  46.2 0.0 collective-permute-done.7.refs_1_
  46.2 0.0 collective-permute-done.8.refs_2_
  46.2 7.9 %shard_map.62 = (f32[4,136,128]{2,1,0:T(8,128)S(1)}, f32[4,136,128]{2,1,0:T(8,128)S(1)}) custom-call(f32[64,2,40,128]{3,2,1,0:T(8,128)S(1)} %shard_map.61.refs_0_, f32[16,64,128]{2,1,0:T(8,128)S(1)} %collective-permute-done.7.refs_1_, f32[16,64,128]{2,1,0:T(8,128)S(1)} %collective-permute-done.8.refs_2_), custom_call_target="tpu_custom_call" | custom-call | tf_op jit(solution)/shard_map/pallas_call | solution.py:412
  54.1 1.3 %collective-permute-start.9 = (f32[4,136,128]{2,1,0:T(8,128)S(1)}, f32[4,136,128]{2,1,0:T(8,128)S(1)}, u32[]{:S(2)}, u32[]{:S(2)}) collective-permute-start(f32[4,136,128]{2,1,0:T(8,128)S(1)} %get-tuple-element.8), channel_id=1, source_target_pairs={{0,128},{1,129},{2,130},{3,131},{4,132},{5,133},{6,134},{7,135},{8... | collective-permute-start | bytes 835592 | tf_op jit(solution)/shard_map/ppermute | solution.py:494
  55.4 1.1 %collective-permute-done.9 = f32[4,136,128]{2,1,0:T(8,128)S(1)} collective-permute-done((f32[4,136,128]{2,1,0:T(8,128)S(1)}, f32[4,136,128]{2,1,0:T(8,128)S(1)}, u32[]{:S(2)}, u32[]{:S(2)}) %collective-permute-start.9) | collective-permute-done | bytes 278560 | tf_op jit(solution)/shard_map/ppermute | solution.py:494
  56.6 10.8 %all_to_all.16.fields = f32[4,136,128]{2,1,0:T(8,128)S(1)} all-to-all(f32[4,136,128]{2,1,0:T(8,128)S(1)} %broadcast_select_fusion), channel_id=1, replica_groups=mesh['gx_0'=4,'gx_1'=2,'gy'=16,'gz'=8] {'gx_0'}, dimensions={0} | all-to-all | bytes 557056 | tf_op jit(solution)/shard_map/all_to_all | solution.py:496
  67.4 36.8 %all_to_all.17 = f32[128,1,128]{2,1,0:T(1,128)S(1)} all-to-all(f32[128,1,128]{2,1,0:T(1,128)S(1)} %broadcast_in_dim.3), channel_id=1, replica_groups=mesh['gx_0'=4,'gx_1'=2,'gy'=16,'gz'=8] {'gy','gz'}, dimensions={0} | all-to-all | bytes 131072 | tf_op jit(solution)/shard_map/all_to_all | solution.py:498
  104.2 0.0 copy-done
  104.2 1.0 shard_map.63
  (4 shorter events, 0.1 us)
Async XLA Ops:
  12.8 8.0 %collective-permute-start.2 = (f32[16,16,128]{2,1,0:T(8,128)S(1)}, f32[16,16,128]{2,1,0:T(8,128)S(1)}, u32[]{:S(2)}, u32[]{:S(2)}) collective-permute-start(f32[16,16,128]{2,1,0:T(8,128)S(1)} %bitcast.2), channel_id=1, source_target_pairs={{0,144},{8,152},{16,160},{24,168},{32,176},{40,184},{48,192},{56,2... | collective-permute-start | bytes 393224 | tf_op jit(solution)/shard_map/ppermute | solution.py:485
  18.1 3.9 %collective-permute-start.3 = (f32[16,16,128]{2,1,0:T(8,128)S(1)}, f32[16,16,128]{2,1,0:T(8,128)S(1)}, u32[]{:S(2)}, u32[]{:S(2)}) collective-permute-start(f32[16,16,128]{2,1,0:T(8,128)S(1)} %bitcast.3), channel_id=1, source_target_pairs={{0,136},{8,144},{16,152},{24,160},{32,168},{40,176},{48,184},{56,1... | collective-permute-start | bytes 393224 | tf_op jit(solution)/shard_map/ppermute | solution.py:485
  19.4 2.6 %collective-permute-start.4 = (f32[16,16,128]{2,1,0:T(8,128)S(1)}, f32[16,16,128]{2,1,0:T(8,128)S(1)}, u32[]{:S(2)}, u32[]{:S(2)}) collective-permute-start(f32[16,16,128]{2,1,0:T(8,128)S(1)} %bitcast.4), channel_id=1, source_target_pairs={{8,128},{16,136},{24,144},{32,152},{40,160},{48,168},{56,176},{64,... | collective-permute-start | bytes 393224 | tf_op jit(solution)/shard_map/ppermute | solution.py:485
  20.1 1.9 %collective-permute-start.5 = (f32[16,16,128]{2,1,0:T(8,128)S(1)}, f32[16,16,128]{2,1,0:T(8,128)S(1)}, u32[]{:S(2)}, u32[]{:S(2)}) collective-permute-start(f32[16,16,128]{2,1,0:T(8,128)S(1)} %bitcast.5), channel_id=1, source_target_pairs={{16,128},{24,136},{32,144},{40,152},{48,160},{56,168},{64,176},{72... | collective-permute-start | bytes 393224 | tf_op jit(solution)/shard_map/ppermute | solution.py:485
  22.1 21.7 %collective-permute-start.6 = (f32[16,64,128]{2,1,0:T(8,128)S(1)}, f32[16,64,128]{2,1,0:T(8,128)S(1)}, u32[]{:S(2)}, u32[]{:S(2)}) collective-permute-start(f32[16,64,128]{2,1,0:T(8,128)S(1)} %shard_map.60), channel_id=1, source_target_pairs={{128,0},{129,1},{130,2},{131,3},{132,4},{133,5},{134,6},{135,7},{1... | collective-permute-start | bytes 1572872 | tf_op jit(solution)/shard_map/ppermute | solution.py:491
  23.4 22.8 %collective-permute-start.7 = (f32[16,64,128]{2,1,0:T(8,128)S(1)}, f32[16,64,128]{2,1,0:T(8,128)S(1)}, u32[]{:S(2)}, u32[]{:S(2)}) collective-permute-start(f32[16,64,128]{2,1,0:T(8,128)S(1)} %shard_map.60), channel_id=1, source_target_pairs={{128,256},{384,512},{640,768},{896,769},{897,513},{641,257},{385,1... | collective-permute-start | bytes 1572872 | tf_op jit(solution)/shard_map/ppermute | solution.py:489
  24.7 21.5 %collective-permute-start.8 = (f32[16,64,128]{2,1,0:T(8,128)S(1)}, f32[16,64,128]{2,1,0:T(8,128)S(1)}, u32[]{:S(2)}, u32[]{:S(2)}) collective-permute-start(f32[16,64,128]{2,1,0:T(8,128)S(1)} %shard_map.60), channel_id=1, source_target_pairs={{384,0},{640,256},{896,512},{897,768},{641,769},{385,513},{129,257... | collective-permute-start | bytes 1572872 | tf_op jit(solution)/shard_map/ppermute | solution.py:490
  26.0 15.4 %collective-permute-start = (f32[16,16,128]{2,1,0:T(8,128)S(1)}, f32[16,16,128]{2,1,0:T(8,128)S(1)}, u32[]{:S(2)}, u32[]{:S(2)}) collective-permute-start(f32[16,16,128]{2,1,0:T(8,128)S(1)} %bitcast.6), channel_id=1, source_target_pairs={{128,256},{384,512},{640,768},{896,769},{897,513},{641,257},{385,1... | collective-permute-start | bytes 393224 | tf_op jit(solution)/shard_map/ppermute | solution.py:486
  27.3 16.5 %collective-permute-start.1 = (f32[16,16,128]{2,1,0:T(8,128)S(1)}, f32[16,16,128]{2,1,0:T(8,128)S(1)}, u32[]{:S(2)}, u32[]{:S(2)}) collective-permute-start(f32[16,16,128]{2,1,0:T(8,128)S(1)} %bitcast.7), channel_id=1, source_target_pairs={{384,0},{640,256},{896,512},{897,768},{641,769},{385,513},{129,257... | collective-permute-start | bytes 393224 | tf_op jit(solution)/shard_map/ppermute | solution.py:487
  46.1 58.0 %copy-start = (f32[8,16,128]{2,1,0:T(8,128)S(1)}, f32[8,16,128]{2,1,0:T(8,128)}, u32[]{:S(2)}) copy-start(f32[8,16,128]{2,1,0:T(8,128)} %get-tuple-element.6.rhs) | copy-start | bytes 196612
  54.1 2.5 %collective-permute-start.9 = (f32[4,136,128]{2,1,0:T(8,128)S(1)}, f32[4,136,128]{2,1,0:T(8,128)S(1)}, u32[]{:S(2)}, u32[]{:S(2)}) collective-permute-start(f32[4,136,128]{2,1,0:T(8,128)S(1)} %get-tuple-element.8), channel_id=1, source_target_pairs={{0,128},{1,129},{2,130},{3,131},{4,132},{5,133},{6,134},{7,135},{8... | collective-permute-start | bytes 835592 | tf_op jit(solution)/shard_map/ppermute | solution.py:494

commit v9 on v8

--- a/solution.py
+++ b/solution.py
@@ -184,7 +184,7 @@
         lax.fori_loop(0, count // size, lambda i, _: body(i * size) or 0, 0, unroll=unroll)
 
 
-def cycle_down(src, mask, mask2, fold, sum1, part1, f1, f2, rows1, rows2, size, nb):
+def cycle_down(src, mask, mask2, fold, outer, sum1, part1, f1, f2, rows1, rows2, size, nb):
     def gather(first, size=size):
         for r in rows1:
             layers = [2 * first + k for k in range(2 * size + 2)]
@@ -202,7 +202,7 @@
     def across(first):
         for r in rows1:
             for x in [first + k for k in range(1, 32 + 1)]:
-                f1[x, at(r)] = part1[x, at(r)] + relax * sides(sum1[x, at(r)], 1)
+                f1[x, at(r)] = part1[x, at(r)] + relax * (sum1[x, at(r)] + outer(sum1[x, at(r)], 1))
 
     chunks(NX // 2, 32, across)
 
@@ -224,7 +224,7 @@
                 before, a, b, after = cells[2 * i : 2 * i + 4]
                 u = a + b
                 y = beyond[2 * i] + beyond[2 * i + 1]
-                s = third(u) + relax * (((u + u) + (before + after)) + (y + sides(u, 2)))
+                s = third(u) + relax * (((u + u) + (before + after)) + (y + (u + outer(u, 2))))
                 f2[first + i + 1, at(r)] = fold(s, 2) * m
 
     chunks(NX // 4, nb, level2)
@@ -352,13 +352,17 @@
         return 0
 
     lax.fori_loop(0, 16, corners_in, 0, unroll=4)
-    low = {step: lanes & step == 0 for step in (1, 2)}
+    partner = {step: lanes ^ step for step in (1, 2)}
+    outside = {step: (lanes + jnp.where(lanes & step == 0, -step, step)) & 127 for step in (1, 2)}
 
     def fold(x, step):
-        return 0.5 * (x + jnp.where(low[step], roll(x, -step, 1), roll(x, step, 1)))
+        return 0.5 * (x + jnp.take_along_axis(x, partner[step], axis=1))
+
+    def outer(x, step):
+        return jnp.take_along_axis(x, outside[step], axis=1)
 
     middle = (8, 16, 24)
-    cycle_down(r0, mask, mask2, fold, v1, e1, f1, f2, (0, 8, 16, 24, 32), (0, 8, 12), 4, 8)
+    cycle_down(r0, mask, mask2, fold, outer, v1, e1, f1, f2, (0, 8, 16, 24, 32), (0, 8, 12), 4, 8)
     cycle_coarse(mask2, f2, t2, e2, (0, 8, 12), (1, 9))
     cycle_up(r0, mask, f1, e2, v1, e1, v0, z0, (6, 14, 22, 26), (7, 15, 23, 25), ((8, 16, 24, 25), (7, 15, 23, 24)), (middle, middle), 32, 64)
 
@@ -370,7 +374,7 @@
                     q0[first + k + 1, odd, at(r)] = value * m
 
     chunks(NX, 64, image)
-    cycle_down(q0, mask, mask2, fold, v1, e1, f1, f2, middle, (5, 7), 8, 16)
+    cycle_down(q0, mask, mask2, fold, outer, v1, e1, f1, f2, middle, (5, 7), 8, 16)
     cycle_coarse(mask2, f2, t2, e2, (6,), (6,))
     cycle_up(q0, mask, f1, e2, v1, e1, v0, w, (14, 18), (15, 17), ((15, 17), (15, 17)), ((16, 17), (15, 16)), 32, 64)
 
@@ -491,8 +495,8 @@
     rows = lax.ppermute(rows, "gx_1", [(1, 0)])
     known = unpack(own, left, right, rows)
     packed, other = cycles(known, up, down)
-    other = lax.ppermute(other, "gx_1", [(0, 1)])
-    packed = jnp.where(lax.axis_index("gx_1") == 1, other, packed)
+    other = lax.all_gather(other, "gx_1")
+    packed = jnp.where(lax.axis_index("gx_1") == 1, other[0], packed)
     fields = lax.all_to_all(packed, "gx_0", 0, 0, tiled=True)
     sums = jnp.sum(fields[:, BX * BY, :], axis=0)
     sums = lax.all_to_all(jnp.broadcast_to(sums, (128, 1, 128)), ("gy", "gz"), 0, 0, tiled=True)

time: 106 us -> 105 us (level)
  blocking collectives: 57.9 us -> 59.9 us
  starting transfers between devices: 15.7 us -> 14.4 us
  waiting for transfers between devices: 17.5 us -> 16.4 us
    all_gather x0 -> x1, blocking collectives: none -> 2.2 us  [local(): other = lax.all_gather(other, 'gx_1')]
    ppermute x1 -> x0, starting transfers between devices: 1.31 us -> none  [local(): other = lax.ppermute(other, 'gx_1', [(0, 1)])]
    ppermute x1 -> x0, waiting for transfers between devices: 1.15 us -> none  [local(): other = lax.ppermute(other, 'gx_1', [(0, 1)])]
  transfers between devices with their start and end apart: 10 -> 9, of which waited for: 4 -> 3; matrix products, arithmetic and copies ran while one was open for 0% -> 0% of each run, Pallas kernels for 2% -> 2%
where the time goes in v9:
time: 105 us; the launch traced here: 104 us
  blocking collectives  59.9 us (57%)
  waiting for transfers between devices  16.4 us (16%)
  starting transfers between devices  14.4 us (14%)
  Pallas kernels  12.5 us (12%)
    all_to_all x1, blocking collectives, local(): lax.all_to_all(jnp.broadcast_to(sums, (128, 1, 128)), ('gy', 'gz'), 0, 0,...  36.8 us
    ppermute x1, waiting for transfers between devices, local(): left = lax.ppermute(own, Z_AXES, z_pairs(1))  12.8 us
    all_to_all x1, blocking collectives, local(): fields = lax.all_to_all(packed, 'gx_0', 0, 0, tiled=True)  10.5 us
    all_to_all x1, blocking collectives, local(): own = lax.all_to_all(packed, GX, 0, 0, tiled=True).reshape(16, BY, 128)  10.4 us
    ppermute x4, starting transfers between devices, local(): moved.append(lax.ppermute(own, ('gx_1', 'gy'), y_pairs(step)))  7.97 us
    pallas_call x1, Pallas kernels, cycles(): pl.pallas_call(cycles_kernel, out_shape=(jax.ShapeDtypeStruct((4, BX * BY...  7.3 us
    pallas_call x1, Pallas kernels, unpack(): pl.pallas_call(unpack_kernel, out_shape=jax.ShapeDtypeStruct((NX, 2, 40,...  2.43 us
    ppermute x1, waiting for transfers between devices, local(): right = lax.ppermute(own, Z_AXES, z_pairs(-1))  2.34 us
  transfers between devices with their start and end apart: 9, of which 3 were waited for; matrix products, arithmetic and copies ran while one was open for 0% of the time, Pallas kernels for 2%

profile of v9, /device:TPU:8, one launch (start us, length us, event | category | flops | bytes accessed | tf_op | source)
XLA Modules:
  0.0 104.0 jit_solution(15446286132318854938)
XLA Ops:
  0.6 1.8 %shard_map.59 = (f32[8,16,128]{2,1,0:T(8,128)}, f32[8,2,16,128]{3,2,1,0:T(8,128)}) custom-call(f32[8,16,128]{2,1,0:T(8,128)} %density_in.1, f32[2,16,128]{2,1,0:T(8,128)} %xf_in.1, f32[2,8,128]{2,1,0:T(8,128)} %yf_in.1, f32[2,8,16]{2,1,0:T(8,128)} %zf_in.1), custom_call_target="tpu_custom_call" | custom-call | tf_op jit(solution)/shard_map/pallas_call | solution.py:95
  2.4 10.4 %all_to_all.15 = f32[8,2,16,128]{3,2,1,0:T(8,128)S(1)} all-to-all(f32[8,2,16,128]{3,2,1,0:T(8,128)} %get-tuple-element.7), channel_id=1, replica_groups=mesh['gx_0'=4,'gx_1'=2,'gy'=16,'gz'=8] {'gx_0','gx_1'}, dimensions={0} | all-to-all | bytes 262144 | tf_op jit(solution)/shard_map/all_to_all | solution.py:486
  12.8 5.3 %collective-permute-start.2 = (f32[16,16,128]{2,1,0:T(8,128)S(1)}, f32[16,16,128]{2,1,0:T(8,128)S(1)}, u32[]{:S(2)}, u32[]{:S(2)}) collective-permute-start(f32[16,16,128]{2,1,0:T(8,128)S(1)} %bitcast.2), channel_id=1, source_target_pairs={{0,144},{8,152},{16,160},{24,168},{32,176},{40,184},{48,192},{56,2... | collective-permute-start | bytes 393224 | tf_op jit(solution)/shard_map/ppermute | solution.py:489
  18.1 1.3 %collective-permute-start.3 = (f32[16,16,128]{2,1,0:T(8,128)S(1)}, f32[16,16,128]{2,1,0:T(8,128)S(1)}, u32[]{:S(2)}, u32[]{:S(2)}) collective-permute-start(f32[16,16,128]{2,1,0:T(8,128)S(1)} %bitcast.3), channel_id=1, source_target_pairs={{0,136},{8,144},{16,152},{24,160},{32,168},{40,176},{48,184},{56,1... | collective-permute-start | bytes 393224 | tf_op jit(solution)/shard_map/ppermute | solution.py:489
  19.4 0.7 collective-permute-start.4
  20.1 0.7 collective-permute-start.5
  20.8 0.0 collective-permute-done.2.refs_0_
  20.8 1.2 %collective-permute-done.3.refs_1_ = f32[16,16,128]{2,1,0:T(8,128)S(1)} collective-permute-done((f32[16,16,128]{2,1,0:T(8,128)S(1)}, f32[16,16,128]{2,1,0:T(8,128)S(1)}, u32[]{:S(2)}, u32[]{:S(2)}) %collective-permute-start.3) | collective-permute-done | bytes 131104 | tf_op jit(solution)/shard_map/ppermute | solution.py:489
  22.0 0.0 collective-permute-done.4.refs_2_
  22.0 0.0 collective-permute-done.5.refs_3_
  22.1 1.3 %collective-permute-start.6 = (f32[16,64,128]{2,1,0:T(8,128)S(1)}, f32[16,64,128]{2,1,0:T(8,128)S(1)}, u32[]{:S(2)}, u32[]{:S(2)}) collective-permute-start(f32[16,64,128]{2,1,0:T(8,128)S(1)} %shard_map.60), channel_id=1, source_target_pairs={{128,0},{129,1},{130,2},{131,3},{132,4},{133,5},{134,6},{135,7},{1... | collective-permute-start | bytes 1572872 | tf_op jit(solution)/shard_map/ppermute | solution.py:495
  23.4 1.3 %collective-permute-start.7 = (f32[16,64,128]{2,1,0:T(8,128)S(1)}, f32[16,64,128]{2,1,0:T(8,128)S(1)}, u32[]{:S(2)}, u32[]{:S(2)}) collective-permute-start(f32[16,64,128]{2,1,0:T(8,128)S(1)} %shard_map.60), channel_id=1, source_target_pairs={{128,256},{384,512},{640,768},{896,769},{897,513},{641,257},{385,1... | collective-permute-start | bytes 1572872 | tf_op jit(solution)/shard_map/ppermute | solution.py:493
  24.7 1.3 %collective-permute-start.8 = (f32[16,64,128]{2,1,0:T(8,128)S(1)}, f32[16,64,128]{2,1,0:T(8,128)S(1)}, u32[]{:S(2)}, u32[]{:S(2)}) collective-permute-start(f32[16,64,128]{2,1,0:T(8,128)S(1)} %shard_map.60), channel_id=1, source_target_pairs={{384,0},{640,256},{896,512},{897,768},{641,769},{385,513},{129,257... | collective-permute-start | bytes 1572872 | tf_op jit(solution)/shard_map/ppermute | solution.py:494
  26.0 1.3 %collective-permute-start = (f32[16,16,128]{2,1,0:T(8,128)S(1)}, f32[16,16,128]{2,1,0:T(8,128)S(1)}, u32[]{:S(2)}, u32[]{:S(2)}) collective-permute-start(f32[16,16,128]{2,1,0:T(8,128)S(1)} %bitcast.6), channel_id=1, source_target_pairs={{128,256},{384,512},{640,768},{896,769},{897,513},{641,257},{385,1... | collective-permute-start | bytes 393224 | tf_op jit(solution)/shard_map/ppermute | solution.py:490
  27.3 1.3 %collective-permute-start.1 = (f32[16,16,128]{2,1,0:T(8,128)S(1)}, f32[16,16,128]{2,1,0:T(8,128)S(1)}, u32[]{:S(2)}, u32[]{:S(2)}) collective-permute-start(f32[16,16,128]{2,1,0:T(8,128)S(1)} %bitcast.7), channel_id=1, source_target_pairs={{384,0},{640,256},{896,512},{897,768},{641,769},{385,513},{129,257... | collective-permute-start | bytes 393224 | tf_op jit(solution)/shard_map/ppermute | solution.py:491
  28.6 12.8 %collective-permute-done.refs_1_ = f32[16,16,128]{2,1,0:T(8,128)S(1)} collective-permute-done((f32[16,16,128]{2,1,0:T(8,128)S(1)}, f32[16,16,128]{2,1,0:T(8,128)S(1)}, u32[]{:S(2)}, u32[]{:S(2)}) %collective-permute-start) | collective-permute-done | bytes 131104 | tf_op jit(solution)/shard_map/ppermute | solution.py:490
  41.4 2.3 %collective-permute-done.1.refs_2_ = f32[16,16,128]{2,1,0:T(8,128)S(1)} collective-permute-done((f32[16,16,128]{2,1,0:T(8,128)S(1)}, f32[16,16,128]{2,1,0:T(8,128)S(1)}, u32[]{:S(2)}, u32[]{:S(2)}) %collective-permute-start.1) | collective-permute-done | bytes 131104 | tf_op jit(solution)/shard_map/ppermute | solution.py:491
  43.7 0.0 collective-permute-done.6.refs_3_
  43.7 2.4 %shard_map.61.refs_0_ = f32[64,2,40,128]{3,2,1,0:T(8,128)S(1)} custom-call(f32[16,16,128]{2,1,0:T(8,128)S(1)} %bitcast.8, f32[16,16,128]{2,1,0:T(8,128)S(1)} %collective-permute-done.refs_1_, f32[16,16,128]{2,1,0:T(8,128)S(1)} %collective-permute-done.1.refs_2_, f32[16,64,128]{2,1,0:T(8,128)S(1)} %collective-permute-done.6.refs_3_), custom_call_target="tpu_custom_call" | custom-call | tf_op jit(solution)/shard_map/pallas_call | solution.py:151
  46.1 0.0 copy-start
  46.2 0.0 collective-permute-done.7.refs_1_
  46.2 0.0 collective-permute-done.8.refs_2_
  46.2 7.3 %shard_map.62 = (f32[4,136,128]{2,1,0:T(8,128)S(1)}, f32[4,136,128]{2,1,0:T(8,128)S(1)}) custom-call(f32[64,2,40,128]{3,2,1,0:T(8,128)S(1)} %shard_map.61.refs_0_, f32[16,64,128]{2,1,0:T(8,128)S(1)} %collective-permute-done.7.refs_1_, f32[16,64,128]{2,1,0:T(8,128)S(1)} %collective-permute-done.8.refs_2_), custom_call_target="tpu_custom_call" | custom-call | tf_op jit(solution)/shard_map/pallas_call | solution.py:416
  53.5 2.2 %all-gather = f32[8,136,128]{2,1,0:T(8,128)S(1)} all-gather(f32[4,136,128]{2,1,0:T(8,128)S(1)} %get-tuple-element.8), channel_id=2, replica_groups=mesh['gx_0'=4,'gx_1'=2,'gy'=16,'gz'=8] {'gx_1'}, dimensions={0}, use_global_device_ids=true | all-gather | bytes 835584 | tf_op jit(solution)/shard_map/all_gather | solution.py:498
  55.7 10.5 %all_to_all.16.fields = f32[4,136,128]{2,1,0:T(8,128)S(1)} all-to-all(f32[4,136,128]{2,1,0:T(8,128)S(1)} %slice_select_fusion), channel_id=1, replica_groups=mesh['gx_0'=4,'gx_1'=2,'gy'=16,'gz'=8] {'gx_0'}, dimensions={0} | all-to-all | bytes 557056 | tf_op jit(solution)/shard_map/all_to_all | solution.py:500
  66.3 36.8 %all_to_all.17 = f32[128,1,128]{2,1,0:T(1,128)S(1)} all-to-all(f32[128,1,128]{2,1,0:T(1,128)S(1)} %broadcast_in_dim.3), channel_id=1, replica_groups=mesh['gx_0'=4,'gx_1'=2,'gy'=16,'gz'=8] {'gy','gz'}, dimensions={0} | all-to-all | bytes 131072 | tf_op jit(solution)/shard_map/all_to_all | solution.py:502
  103.1 0.0 copy-done
  103.1 1.0 shard_map.63
  (4 shorter events, 0.1 us)
Async XLA Ops:
  12.8 8.0 %collective-permute-start.2 = (f32[16,16,128]{2,1,0:T(8,128)S(1)}, f32[16,16,128]{2,1,0:T(8,128)S(1)}, u32[]{:S(2)}, u32[]{:S(2)}) collective-permute-start(f32[16,16,128]{2,1,0:T(8,128)S(1)} %bitcast.2), channel_id=1, source_target_pairs={{0,144},{8,152},{16,160},{24,168},{32,176},{40,184},{48,192},{56,2... | collective-permute-start | bytes 393224 | tf_op jit(solution)/shard_map/ppermute | solution.py:489
  18.1 3.9 %collective-permute-start.3 = (f32[16,16,128]{2,1,0:T(8,128)S(1)}, f32[16,16,128]{2,1,0:T(8,128)S(1)}, u32[]{:S(2)}, u32[]{:S(2)}) collective-permute-start(f32[16,16,128]{2,1,0:T(8,128)S(1)} %bitcast.3), channel_id=1, source_target_pairs={{0,136},{8,144},{16,152},{24,160},{32,168},{40,176},{48,184},{56,1... | collective-permute-start | bytes 393224 | tf_op jit(solution)/shard_map/ppermute | solution.py:489
  19.4 2.6 %collective-permute-start.4 = (f32[16,16,128]{2,1,0:T(8,128)S(1)}, f32[16,16,128]{2,1,0:T(8,128)S(1)}, u32[]{:S(2)}, u32[]{:S(2)}) collective-permute-start(f32[16,16,128]{2,1,0:T(8,128)S(1)} %bitcast.4), channel_id=1, source_target_pairs={{8,128},{16,136},{24,144},{32,152},{40,160},{48,168},{56,176},{64,... | collective-permute-start | bytes 393224 | tf_op jit(solution)/shard_map/ppermute | solution.py:489
  20.1 1.9 %collective-permute-start.5 = (f32[16,16,128]{2,1,0:T(8,128)S(1)}, f32[16,16,128]{2,1,0:T(8,128)S(1)}, u32[]{:S(2)}, u32[]{:S(2)}) collective-permute-start(f32[16,16,128]{2,1,0:T(8,128)S(1)} %bitcast.5), channel_id=1, source_target_pairs={{16,128},{24,136},{32,144},{40,152},{48,160},{56,168},{64,176},{72... | collective-permute-start | bytes 393224 | tf_op jit(solution)/shard_map/ppermute | solution.py:489
  22.1 21.7 %collective-permute-start.6 = (f32[16,64,128]{2,1,0:T(8,128)S(1)}, f32[16,64,128]{2,1,0:T(8,128)S(1)}, u32[]{:S(2)}, u32[]{:S(2)}) collective-permute-start(f32[16,64,128]{2,1,0:T(8,128)S(1)} %shard_map.60), channel_id=1, source_target_pairs={{128,0},{129,1},{130,2},{131,3},{132,4},{133,5},{134,6},{135,7},{1... | collective-permute-start | bytes 1572872 | tf_op jit(solution)/shard_map/ppermute | solution.py:495
  23.4 22.8 %collective-permute-start.7 = (f32[16,64,128]{2,1,0:T(8,128)S(1)}, f32[16,64,128]{2,1,0:T(8,128)S(1)}, u32[]{:S(2)}, u32[]{:S(2)}) collective-permute-start(f32[16,64,128]{2,1,0:T(8,128)S(1)} %shard_map.60), channel_id=1, source_target_pairs={{128,256},{384,512},{640,768},{896,769},{897,513},{641,257},{385,1... | collective-permute-start | bytes 1572872 | tf_op jit(solution)/shard_map/ppermute | solution.py:493
  24.7 21.5 %collective-permute-start.8 = (f32[16,64,128]{2,1,0:T(8,128)S(1)}, f32[16,64,128]{2,1,0:T(8,128)S(1)}, u32[]{:S(2)}, u32[]{:S(2)}) collective-permute-start(f32[16,64,128]{2,1,0:T(8,128)S(1)} %shard_map.60), channel_id=1, source_target_pairs={{384,0},{640,256},{896,512},{897,768},{641,769},{385,513},{129,257... | collective-permute-start | bytes 1572872 | tf_op jit(solution)/shard_map/ppermute | solution.py:494
  26.0 15.4 %collective-permute-start = (f32[16,16,128]{2,1,0:T(8,128)S(1)}, f32[16,16,128]{2,1,0:T(8,128)S(1)}, u32[]{:S(2)}, u32[]{:S(2)}) collective-permute-start(f32[16,16,128]{2,1,0:T(8,128)S(1)} %bitcast.6), channel_id=1, source_target_pairs={{128,256},{384,512},{640,768},{896,769},{897,513},{641,257},{385,1... | collective-permute-start | bytes 393224 | tf_op jit(solution)/shard_map/ppermute | solution.py:490
  27.3 16.5 %collective-permute-start.1 = (f32[16,16,128]{2,1,0:T(8,128)S(1)}, f32[16,16,128]{2,1,0:T(8,128)S(1)}, u32[]{:S(2)}, u32[]{:S(2)}) collective-permute-start(f32[16,16,128]{2,1,0:T(8,128)S(1)} %bitcast.7), channel_id=1, source_target_pairs={{384,0},{640,256},{896,512},{897,768},{641,769},{385,513},{129,257... | collective-permute-start | bytes 393224 | tf_op jit(solution)/shard_map/ppermute | solution.py:491
  46.1 56.9 %copy-start = (f32[8,16,128]{2,1,0:T(8,128)S(1)}, f32[8,16,128]{2,1,0:T(8,128)}, u32[]{:S(2)}) copy-start(f32[8,16,128]{2,1,0:T(8,128)} %get-tuple-element.6.rhs) | copy-start | bytes 196612

commit v10 on v9

--- a/solution.py
+++ b/solution.py
@@ -209,10 +209,10 @@
     def level1(first):
         for r in rows1:
             m = mask[at(r)]
-            for x in [first + k for k in range(1, 16 + 1)]:
+            for x in [first + k for k in range(1, 32 + 1)]:
                 f1[x, at(r)] = fold(f1[x, at(r)], 1) * m
 
-    chunks(NX // 2, 16, level1)
+    chunks(NX // 2, 32, level1)
 
     def level2(first):
         for r in rows2:
@@ -362,7 +362,7 @@
         return jnp.take_along_axis(x, outside[step], axis=1)
 
     middle = (8, 16, 24)
-    cycle_down(r0, mask, mask2, fold, outer, v1, e1, f1, f2, (0, 8, 16, 24, 32), (0, 8, 12), 4, 8)
+    cycle_down(r0, mask, mask2, fold, outer, v1, e1, f1, f2, (0, 8, 16, 24, 32), (0, 8, 12), 8, 8)
     cycle_coarse(mask2, f2, t2, e2, (0, 8, 12), (1, 9))
     cycle_up(r0, mask, f1, e2, v1, e1, v0, z0, (6, 14, 22, 26), (7, 15, 23, 25), ((8, 16, 24, 25), (7, 15, 23, 24)), (middle, middle), 32, 64)
 

time: 105 us -> 104 us (level)
  no operation moved by 1% of the time
where the time goes in v10:
time: 104 us
  blocking collectives  59.9 us (58%)
  waiting for transfers between devices  16.4 us (16%)
  starting transfers between devices  14.4 us (14%)
  Pallas kernels  12.2 us (12%)
    all_to_all x1, blocking collectives, local(): lax.all_to_all(jnp.broadcast_to(sums, (128, 1, 128)), ('gy', 'gz'), 0, 0,...  36.8 us
    ppermute x1, waiting for transfers between devices, local(): left = lax.ppermute(own, Z_AXES, z_pairs(1))  12.8 us
    all_to_all x1, blocking collectives, local(): fields = lax.all_to_all(packed, 'gx_0', 0, 0, tiled=True)  10.5 us
    all_to_all x1, blocking collectives, local(): own = lax.all_to_all(packed, GX, 0, 0, tiled=True).reshape(16, BY, 128)  10.4 us
    ppermute x4, starting transfers between devices, local(): moved.append(lax.ppermute(own, ('gx_1', 'gy'), y_pairs(step)))  7.97 us
    pallas_call x1, Pallas kernels, cycles(): pl.pallas_call(cycles_kernel, out_shape=(jax.ShapeDtypeStruct((4, BX * BY...  7.02 us
    pallas_call x1, Pallas kernels, unpack(): pl.pallas_call(unpack_kernel, out_shape=jax.ShapeDtypeStruct((NX, 2, 40,...  2.43 us
    ppermute x1, waiting for transfers between devices, local(): right = lax.ppermute(own, Z_AXES, z_pairs(-1))  2.34 us
  transfers between devices with their start and end apart: 9, of which 3 were waited for; matrix products, arithmetic and copies ran while one was open for 0% of the time, Pallas kernels for 2%

profile of v10, /device:TPU:8, one launch (start us, length us, event | category | flops | bytes accessed | tf_op | source)
XLA Modules:
  0.0 103.8 jit_solution(13502441524050218182)
XLA Ops:
  0.6 1.8 %shard_map.59 = (f32[8,16,128]{2,1,0:T(8,128)}, f32[8,2,16,128]{3,2,1,0:T(8,128)}) custom-call(f32[8,16,128]{2,1,0:T(8,128)} %density_in.1, f32[2,16,128]{2,1,0:T(8,128)} %xf_in.1, f32[2,8,128]{2,1,0:T(8,128)} %yf_in.1, f32[2,8,16]{2,1,0:T(8,128)} %zf_in.1), custom_call_target="tpu_custom_call" | custom-call | tf_op jit(solution)/shard_map/pallas_call | solution.py:95
  2.4 10.4 %all_to_all.15 = f32[8,2,16,128]{3,2,1,0:T(8,128)S(1)} all-to-all(f32[8,2,16,128]{3,2,1,0:T(8,128)} %get-tuple-element.7), channel_id=1, replica_groups=mesh['gx_0'=4,'gx_1'=2,'gy'=16,'gz'=8] {'gx_0','gx_1'}, dimensions={0} | all-to-all | bytes 262144 | tf_op jit(solution)/shard_map/all_to_all | solution.py:486
  12.8 5.3 %collective-permute-start.2 = (f32[16,16,128]{2,1,0:T(8,128)S(1)}, f32[16,16,128]{2,1,0:T(8,128)S(1)}, u32[]{:S(2)}, u32[]{:S(2)}) collective-permute-start(f32[16,16,128]{2,1,0:T(8,128)S(1)} %bitcast.2), channel_id=1, source_target_pairs={{0,144},{8,152},{16,160},{24,168},{32,176},{40,184},{48,192},{56,2... | collective-permute-start | bytes 393224 | tf_op jit(solution)/shard_map/ppermute | solution.py:489
  18.1 1.3 %collective-permute-start.3 = (f32[16,16,128]{2,1,0:T(8,128)S(1)}, f32[16,16,128]{2,1,0:T(8,128)S(1)}, u32[]{:S(2)}, u32[]{:S(2)}) collective-permute-start(f32[16,16,128]{2,1,0:T(8,128)S(1)} %bitcast.3), channel_id=1, source_target_pairs={{0,136},{8,144},{16,152},{24,160},{32,168},{40,176},{48,184},{56,1... | collective-permute-start | bytes 393224 | tf_op jit(solution)/shard_map/ppermute | solution.py:489
  19.4 0.7 collective-permute-start.4
  20.1 0.7 collective-permute-start.5
  20.8 0.0 collective-permute-done.2.refs_0_
  20.8 1.2 %collective-permute-done.3.refs_1_ = f32[16,16,128]{2,1,0:T(8,128)S(1)} collective-permute-done((f32[16,16,128]{2,1,0:T(8,128)S(1)}, f32[16,16,128]{2,1,0:T(8,128)S(1)}, u32[]{:S(2)}, u32[]{:S(2)}) %collective-permute-start.3) | collective-permute-done | bytes 131104 | tf_op jit(solution)/shard_map/ppermute | solution.py:489
  22.0 0.0 collective-permute-done.4.refs_2_
  22.0 0.0 collective-permute-done.5.refs_3_
  22.1 1.3 %collective-permute-start.6 = (f32[16,64,128]{2,1,0:T(8,128)S(1)}, f32[16,64,128]{2,1,0:T(8,128)S(1)}, u32[]{:S(2)}, u32[]{:S(2)}) collective-permute-start(f32[16,64,128]{2,1,0:T(8,128)S(1)} %shard_map.60), channel_id=1, source_target_pairs={{128,0},{129,1},{130,2},{131,3},{132,4},{133,5},{134,6},{135,7},{1... | collective-permute-start | bytes 1572872 | tf_op jit(solution)/shard_map/ppermute | solution.py:495
  23.4 1.3 %collective-permute-start.7 = (f32[16,64,128]{2,1,0:T(8,128)S(1)}, f32[16,64,128]{2,1,0:T(8,128)S(1)}, u32[]{:S(2)}, u32[]{:S(2)}) collective-permute-start(f32[16,64,128]{2,1,0:T(8,128)S(1)} %shard_map.60), channel_id=1, source_target_pairs={{128,256},{384,512},{640,768},{896,769},{897,513},{641,257},{385,1... | collective-permute-start | bytes 1572872 | tf_op jit(solution)/shard_map/ppermute | solution.py:493
  24.7 1.3 %collective-permute-start.8 = (f32[16,64,128]{2,1,0:T(8,128)S(1)}, f32[16,64,128]{2,1,0:T(8,128)S(1)}, u32[]{:S(2)}, u32[]{:S(2)}) collective-permute-start(f32[16,64,128]{2,1,0:T(8,128)S(1)} %shard_map.60), channel_id=1, source_target_pairs={{384,0},{640,256},{896,512},{897,768},{641,769},{385,513},{129,257... | collective-permute-start | bytes 1572872 | tf_op jit(solution)/shard_map/ppermute | solution.py:494
  26.0 1.3 %collective-permute-start = (f32[16,16,128]{2,1,0:T(8,128)S(1)}, f32[16,16,128]{2,1,0:T(8,128)S(1)}, u32[]{:S(2)}, u32[]{:S(2)}) collective-permute-start(f32[16,16,128]{2,1,0:T(8,128)S(1)} %bitcast.6), channel_id=1, source_target_pairs={{128,256},{384,512},{640,768},{896,769},{897,513},{641,257},{385,1... | collective-permute-start | bytes 393224 | tf_op jit(solution)/shard_map/ppermute | solution.py:490
  27.3 1.3 %collective-permute-start.1 = (f32[16,16,128]{2,1,0:T(8,128)S(1)}, f32[16,16,128]{2,1,0:T(8,128)S(1)}, u32[]{:S(2)}, u32[]{:S(2)}) collective-permute-start(f32[16,16,128]{2,1,0:T(8,128)S(1)} %bitcast.7), channel_id=1, source_target_pairs={{384,0},{640,256},{896,512},{897,768},{641,769},{385,513},{129,257... | collective-permute-start | bytes 393224 | tf_op jit(solution)/shard_map/ppermute | solution.py:491
  28.6 12.8 %collective-permute-done.refs_1_ = f32[16,16,128]{2,1,0:T(8,128)S(1)} collective-permute-done((f32[16,16,128]{2,1,0:T(8,128)S(1)}, f32[16,16,128]{2,1,0:T(8,128)S(1)}, u32[]{:S(2)}, u32[]{:S(2)}) %collective-permute-start) | collective-permute-done | bytes 131104 | tf_op jit(solution)/shard_map/ppermute | solution.py:490
  41.4 2.3 %collective-permute-done.1.refs_2_ = f32[16,16,128]{2,1,0:T(8,128)S(1)} collective-permute-done((f32[16,16,128]{2,1,0:T(8,128)S(1)}, f32[16,16,128]{2,1,0:T(8,128)S(1)}, u32[]{:S(2)}, u32[]{:S(2)}) %collective-permute-start.1) | collective-permute-done | bytes 131104 | tf_op jit(solution)/shard_map/ppermute | solution.py:491
  43.7 0.0 collective-permute-done.6.refs_3_
  43.7 2.4 %shard_map.61.refs_0_ = f32[64,2,40,128]{3,2,1,0:T(8,128)S(1)} custom-call(f32[16,16,128]{2,1,0:T(8,128)S(1)} %bitcast.8, f32[16,16,128]{2,1,0:T(8,128)S(1)} %collective-permute-done.refs_1_, f32[16,16,128]{2,1,0:T(8,128)S(1)} %collective-permute-done.1.refs_2_, f32[16,64,128]{2,1,0:T(8,128)S(1)} %collective-permute-done.6.refs_3_), custom_call_target="tpu_custom_call" | custom-call | tf_op jit(solution)/shard_map/pallas_call | solution.py:151
  46.1 0.0 copy-start
  46.2 0.0 collective-permute-done.7.refs_1_
  46.2 0.0 collective-permute-done.8.refs_2_
  46.2 7.0 %shard_map.62 = (f32[4,136,128]{2,1,0:T(8,128)S(1)}, f32[4,136,128]{2,1,0:T(8,128)S(1)}) custom-call(f32[64,2,40,128]{3,2,1,0:T(8,128)S(1)} %shard_map.61.refs_0_, f32[16,64,128]{2,1,0:T(8,128)S(1)} %collective-permute-done.7.refs_1_, f32[16,64,128]{2,1,0:T(8,128)S(1)} %collective-permute-done.8.refs_2_), custom_call_target="tpu_custom_call" | custom-call | tf_op jit(solution)/shard_map/pallas_call | solution.py:416
  53.2 2.2 %all-gather = f32[8,136,128]{2,1,0:T(8,128)S(1)} all-gather(f32[4,136,128]{2,1,0:T(8,128)S(1)} %get-tuple-element.8), channel_id=2, replica_groups=mesh['gx_0'=4,'gx_1'=2,'gy'=16,'gz'=8] {'gx_1'}, dimensions={0}, use_global_device_ids=true | all-gather | bytes 835584 | tf_op jit(solution)/shard_map/all_gather | solution.py:498
  55.4 10.5 %all_to_all.16.fields = f32[4,136,128]{2,1,0:T(8,128)S(1)} all-to-all(f32[4,136,128]{2,1,0:T(8,128)S(1)} %slice_select_fusion), channel_id=1, replica_groups=mesh['gx_0'=4,'gx_1'=2,'gy'=16,'gz'=8] {'gx_0'}, dimensions={0} | all-to-all | bytes 557056 | tf_op jit(solution)/shard_map/all_to_all | solution.py:500
  66.0 36.8 %all_to_all.17 = f32[128,1,128]{2,1,0:T(1,128)S(1)} all-to-all(f32[128,1,128]{2,1,0:T(1,128)S(1)} %broadcast_in_dim.3), channel_id=1, replica_groups=mesh['gx_0'=4,'gx_1'=2,'gy'=16,'gz'=8] {'gy','gz'}, dimensions={0} | all-to-all | bytes 131072 | tf_op jit(solution)/shard_map/all_to_all | solution.py:502
  102.8 0.0 copy-done
  102.8 1.0 shard_map.63
  (4 shorter events, 0.1 us)
Async XLA Ops:
  12.8 8.0 %collective-permute-start.2 = (f32[16,16,128]{2,1,0:T(8,128)S(1)}, f32[16,16,128]{2,1,0:T(8,128)S(1)}, u32[]{:S(2)}, u32[]{:S(2)}) collective-permute-start(f32[16,16,128]{2,1,0:T(8,128)S(1)} %bitcast.2), channel_id=1, source_target_pairs={{0,144},{8,152},{16,160},{24,168},{32,176},{40,184},{48,192},{56,2... | collective-permute-start | bytes 393224 | tf_op jit(solution)/shard_map/ppermute | solution.py:489
  18.1 3.9 %collective-permute-start.3 = (f32[16,16,128]{2,1,0:T(8,128)S(1)}, f32[16,16,128]{2,1,0:T(8,128)S(1)}, u32[]{:S(2)}, u32[]{:S(2)}) collective-permute-start(f32[16,16,128]{2,1,0:T(8,128)S(1)} %bitcast.3), channel_id=1, source_target_pairs={{0,136},{8,144},{16,152},{24,160},{32,168},{40,176},{48,184},{56,1... | collective-permute-start | bytes 393224 | tf_op jit(solution)/shard_map/ppermute | solution.py:489
  19.4 2.6 %collective-permute-start.4 = (f32[16,16,128]{2,1,0:T(8,128)S(1)}, f32[16,16,128]{2,1,0:T(8,128)S(1)}, u32[]{:S(2)}, u32[]{:S(2)}) collective-permute-start(f32[16,16,128]{2,1,0:T(8,128)S(1)} %bitcast.4), channel_id=1, source_target_pairs={{8,128},{16,136},{24,144},{32,152},{40,160},{48,168},{56,176},{64,... | collective-permute-start | bytes 393224 | tf_op jit(solution)/shard_map/ppermute | solution.py:489
  20.1 1.9 %collective-permute-start.5 = (f32[16,16,128]{2,1,0:T(8,128)S(1)}, f32[16,16,128]{2,1,0:T(8,128)S(1)}, u32[]{:S(2)}, u32[]{:S(2)}) collective-permute-start(f32[16,16,128]{2,1,0:T(8,128)S(1)} %bitcast.5), channel_id=1, source_target_pairs={{16,128},{24,136},{32,144},{40,152},{48,160},{56,168},{64,176},{72... | collective-permute-start | bytes 393224 | tf_op jit(solution)/shard_map/ppermute | solution.py:489
  22.1 21.7 %collective-permute-start.6 = (f32[16,64,128]{2,1,0:T(8,128)S(1)}, f32[16,64,128]{2,1,0:T(8,128)S(1)}, u32[]{:S(2)}, u32[]{:S(2)}) collective-permute-start(f32[16,64,128]{2,1,0:T(8,128)S(1)} %shard_map.60), channel_id=1, source_target_pairs={{128,0},{129,1},{130,2},{131,3},{132,4},{133,5},{134,6},{135,7},{1... | collective-permute-start | bytes 1572872 | tf_op jit(solution)/shard_map/ppermute | solution.py:495
  23.4 22.8 %collective-permute-start.7 = (f32[16,64,128]{2,1,0:T(8,128)S(1)}, f32[16,64,128]{2,1,0:T(8,128)S(1)}, u32[]{:S(2)}, u32[]{:S(2)}) collective-permute-start(f32[16,64,128]{2,1,0:T(8,128)S(1)} %shard_map.60), channel_id=1, source_target_pairs={{128,256},{384,512},{640,768},{896,769},{897,513},{641,257},{385,1... | collective-permute-start | bytes 1572872 | tf_op jit(solution)/shard_map/ppermute | solution.py:493
  24.7 21.5 %collective-permute-start.8 = (f32[16,64,128]{2,1,0:T(8,128)S(1)}, f32[16,64,128]{2,1,0:T(8,128)S(1)}, u32[]{:S(2)}, u32[]{:S(2)}) collective-permute-start(f32[16,64,128]{2,1,0:T(8,128)S(1)} %shard_map.60), channel_id=1, source_target_pairs={{384,0},{640,256},{896,512},{897,768},{641,769},{385,513},{129,257... | collective-permute-start | bytes 1572872 | tf_op jit(solution)/shard_map/ppermute | solution.py:494
  26.0 15.4 %collective-permute-start = (f32[16,16,128]{2,1,0:T(8,128)S(1)}, f32[16,16,128]{2,1,0:T(8,128)S(1)}, u32[]{:S(2)}, u32[]{:S(2)}) collective-permute-start(f32[16,16,128]{2,1,0:T(8,128)S(1)} %bitcast.6), channel_id=1, source_target_pairs={{128,256},{384,512},{640,768},{896,769},{897,513},{641,257},{385,1... | collective-permute-start | bytes 393224 | tf_op jit(solution)/shard_map/ppermute | solution.py:490
  27.3 16.5 %collective-permute-start.1 = (f32[16,16,128]{2,1,0:T(8,128)S(1)}, f32[16,16,128]{2,1,0:T(8,128)S(1)}, u32[]{:S(2)}, u32[]{:S(2)}) collective-permute-start(f32[16,16,128]{2,1,0:T(8,128)S(1)} %bitcast.7), channel_id=1, source_target_pairs={{384,0},{640,256},{896,512},{897,768},{641,769},{385,513},{129,257... | collective-permute-start | bytes 393224 | tf_op jit(solution)/shard_map/ppermute | solution.py:491
  46.1 56.6 %copy-start = (f32[8,16,128]{2,1,0:T(8,128)S(1)}, f32[8,16,128]{2,1,0:T(8,128)}, u32[]{:S(2)}) copy-start(f32[8,16,128]{2,1,0:T(8,128)} %get-tuple-element.6.rhs) | copy-start | bytes 196612

commit v11 on v10

--- a/solution.py
+++ b/solution.py
@@ -62,7 +62,6 @@
 
     for copy in copies:
         copy.wait()
-    layers = []
     for x in range(BX):
         value = -coupling * density[x]
         if x == 0:
@@ -70,11 +69,15 @@
         if x == BX - 1:
             value = value + jnp.where(gx == NX // BX - 1, xf[1], 0.0)
         value = value + jnp.where(low_y, yf[0, x : x + 1, :], 0.0)
-        value = value + jnp.where(high_y, yf[1, x : x + 1, :], 0.0)
-        value = value + jnp.where(low_z, column(zf[0, x : x + 1, :]), 0.0)
-        value = value + jnp.where(high_z, column(zf[1, x : x + 1, :]), 0.0)
-        rhs[x] = value
-        layers.append(value)
+        rhs[x] = value + jnp.where(high_y, yf[1, x : x + 1, :], 0.0)
+
+    @pl.when((gz == 0) | (gz == NZ // BZ - 1))
+    def _():
+        for x in range(BX):
+            value = rhs[x] + jnp.where(low_z, column(zf[0, x : x + 1, :]), 0.0)
+            rhs[x] = value + jnp.where(high_z, column(zf[1, x : x + 1, :]), 0.0)
+
+    layers = [rhs[x] for x in range(BX)]
     for chunk in range(4):
         for quad in range(2):
             out = None
@@ -441,20 +444,18 @@
     on_z = step0 + step1 * (1.0 + growth)
     on_w = -step1 * step0
     wide = lane_index((BY, LANES))
+    even = wide // 32 % 2 == 0
+    scale = jnp.where(wide < 64, on_z, on_w)
     gz = lax.axis_index("gz")
+
+    def pair(a, b):
+        return jnp.where(wide < 64, a, b) + roll(jnp.where(wide < 64, b, a), 64, 1)
+
     for x in range(BX):
-        parts = [fields[z_block(c, gz), x * BY : (x + 1) * BY] for c in range(4)]
-
-        def field(f):
-            value = None
-            for c in range(4):
-                part = roll(parts[c], 32 * (c - f), 1)
-                value = part if c == 0 else jnp.where(wide >= 32 * c, part, value)
-            return value
-
-        z0, q0, w, s = (field(f) for f in range(4))
-        u = on_z * z0 + on_w * w
-        v = on_z * q0 + on_w * s
+        parts = [scale * fields[z_block(c, gz), x * BY : (x + 1) * BY] for c in range(4)]
+        one, two = pair(parts[0], parts[2]), pair(parts[1], parts[3])
+        u = jnp.where(even, one, roll(two, 32, 1))
+        v = jnp.where(even, roll(one, -32, 1), two)
         for odd in range(2):
             rows = pl.ds(odd, 8, stride=2)
             solution[x, rows, :] = u[8 * odd : 8 * odd + 8]

time: 104 us -> 104 us (level)
  no operation moved by 1% of the time
where the time goes in v11:
time: 104 us
  blocking collectives  59.9 us (58%)
  waiting for transfers between devices  16.4 us (16%)
  starting transfers between devices  14.4 us (14%)
  Pallas kernels  12.1 us (12%)
    all_to_all x1, blocking collectives, local(): lax.all_to_all(jnp.broadcast_to(sums, (128, 1, 128)), ('gy', 'gz'), 0, 0,...  36.7 us
    ppermute x1, waiting for transfers between devices, local(): left = lax.ppermute(own, Z_AXES, z_pairs(1))  12.8 us
    all_to_all x1, blocking collectives, local(): fields = lax.all_to_all(packed, 'gx_0', 0, 0, tiled=True)  10.6 us
    all_to_all x1, blocking collectives, local(): own = lax.all_to_all(packed, GX, 0, 0, tiled=True).reshape(16, BY, 128)  10.4 us
    ppermute x4, starting transfers between devices, local(): moved.append(lax.ppermute(own, ('gx_1', 'gy'), y_pairs(step)))  7.97 us
    pallas_call x1, Pallas kernels, cycles(): pl.pallas_call(cycles_kernel, out_shape=(jax.ShapeDtypeStruct((4, BX * BY...  7.02 us
    pallas_call x1, Pallas kernels, unpack(): pl.pallas_call(unpack_kernel, out_shape=jax.ShapeDtypeStruct((NX, 2, 40,...  2.43 us
    ppermute x1, waiting for transfers between devices, local(): right = lax.ppermute(own, Z_AXES, z_pairs(-1))  2.34 us
  transfers between devices with their start and end apart: 9, of which 3 were waited for; matrix products, arithmetic and copies ran while one was open for 0% of the time, Pallas kernels for 2%

profile of v11, /device:TPU:8, one launch (start us, length us, event | category | flops | bytes accessed | tf_op | source)
XLA Modules:
  0.0 103.6 jit_solution(3356178963574447824)
XLA Ops:
  0.6 1.7 %shard_map.59 = (f32[8,16,128]{2,1,0:T(8,128)}, f32[8,2,16,128]{3,2,1,0:T(8,128)}) custom-call(f32[8,16,128]{2,1,0:T(8,128)} %density_in.1, f32[2,16,128]{2,1,0:T(8,128)} %xf_in.1, f32[2,8,128]{2,1,0:T(8,128)} %yf_in.1, f32[2,8,16]{2,1,0:T(8,128)} %zf_in.1), custom_call_target="tpu_custom_call" | custom-call | tf_op jit(solution)/shard_map/pallas_call | solution.py:98
  2.3 10.4 %all_to_all.15 = f32[8,2,16,128]{3,2,1,0:T(8,128)S(1)} all-to-all(f32[8,2,16,128]{3,2,1,0:T(8,128)} %get-tuple-element.7), channel_id=1, replica_groups=mesh['gx_0'=4,'gx_1'=2,'gy'=16,'gz'=8] {'gx_0','gx_1'}, dimensions={0} | all-to-all | bytes 262144 | tf_op jit(solution)/shard_map/all_to_all | solution.py:487
  12.7 5.3 %collective-permute-start.2 = (f32[16,16,128]{2,1,0:T(8,128)S(1)}, f32[16,16,128]{2,1,0:T(8,128)S(1)}, u32[]{:S(2)}, u32[]{:S(2)}) collective-permute-start(f32[16,16,128]{2,1,0:T(8,128)S(1)} %bitcast.2), channel_id=1, source_target_pairs={{0,144},{8,152},{16,160},{24,168},{32,176},{40,184},{48,192},{56,2... | collective-permute-start | bytes 393224 | tf_op jit(solution)/shard_map/ppermute | solution.py:490
  18.1 1.3 %collective-permute-start.3 = (f32[16,16,128]{2,1,0:T(8,128)S(1)}, f32[16,16,128]{2,1,0:T(8,128)S(1)}, u32[]{:S(2)}, u32[]{:S(2)}) collective-permute-start(f32[16,16,128]{2,1,0:T(8,128)S(1)} %bitcast.3), channel_id=1, source_target_pairs={{0,136},{8,144},{16,152},{24,160},{32,168},{40,176},{48,184},{56,1... | collective-permute-start | bytes 393224 | tf_op jit(solution)/shard_map/ppermute | solution.py:490
  19.4 0.7 collective-permute-start.4
  20.0 0.7 collective-permute-start.5
  20.7 0.0 collective-permute-done.2.refs_0_
  20.7 1.2 %collective-permute-done.3.refs_1_ = f32[16,16,128]{2,1,0:T(8,128)S(1)} collective-permute-done((f32[16,16,128]{2,1,0:T(8,128)S(1)}, f32[16,16,128]{2,1,0:T(8,128)S(1)}, u32[]{:S(2)}, u32[]{:S(2)}) %collective-permute-start.3) | collective-permute-done | bytes 131104 | tf_op jit(solution)/shard_map/ppermute | solution.py:490
  21.9 0.0 collective-permute-done.4.refs_2_
  21.9 0.0 collective-permute-done.5.refs_3_
  22.0 1.3 %collective-permute-start.6 = (f32[16,64,128]{2,1,0:T(8,128)S(1)}, f32[16,64,128]{2,1,0:T(8,128)S(1)}, u32[]{:S(2)}, u32[]{:S(2)}) collective-permute-start(f32[16,64,128]{2,1,0:T(8,128)S(1)} %shard_map.60), channel_id=1, source_target_pairs={{128,0},{129,1},{130,2},{131,3},{132,4},{133,5},{134,6},{135,7},{1... | collective-permute-start | bytes 1572872 | tf_op jit(solution)/shard_map/ppermute | solution.py:496
  23.3 1.3 %collective-permute-start.7 = (f32[16,64,128]{2,1,0:T(8,128)S(1)}, f32[16,64,128]{2,1,0:T(8,128)S(1)}, u32[]{:S(2)}, u32[]{:S(2)}) collective-permute-start(f32[16,64,128]{2,1,0:T(8,128)S(1)} %shard_map.60), channel_id=1, source_target_pairs={{128,256},{384,512},{640,768},{896,769},{897,513},{641,257},{385,1... | collective-permute-start | bytes 1572872 | tf_op jit(solution)/shard_map/ppermute | solution.py:494
  24.6 1.3 %collective-permute-start.8 = (f32[16,64,128]{2,1,0:T(8,128)S(1)}, f32[16,64,128]{2,1,0:T(8,128)S(1)}, u32[]{:S(2)}, u32[]{:S(2)}) collective-permute-start(f32[16,64,128]{2,1,0:T(8,128)S(1)} %shard_map.60), channel_id=1, source_target_pairs={{384,0},{640,256},{896,512},{897,768},{641,769},{385,513},{129,257... | collective-permute-start | bytes 1572872 | tf_op jit(solution)/shard_map/ppermute | solution.py:495
  25.9 1.3 %collective-permute-start = (f32[16,16,128]{2,1,0:T(8,128)S(1)}, f32[16,16,128]{2,1,0:T(8,128)S(1)}, u32[]{:S(2)}, u32[]{:S(2)}) collective-permute-start(f32[16,16,128]{2,1,0:T(8,128)S(1)} %bitcast.6), channel_id=1, source_target_pairs={{128,256},{384,512},{640,768},{896,769},{897,513},{641,257},{385,1... | collective-permute-start | bytes 393224 | tf_op jit(solution)/shard_map/ppermute | solution.py:491
  27.2 1.3 %collective-permute-start.1 = (f32[16,16,128]{2,1,0:T(8,128)S(1)}, f32[16,16,128]{2,1,0:T(8,128)S(1)}, u32[]{:S(2)}, u32[]{:S(2)}) collective-permute-start(f32[16,16,128]{2,1,0:T(8,128)S(1)} %bitcast.7), channel_id=1, source_target_pairs={{384,0},{640,256},{896,512},{897,768},{641,769},{385,513},{129,257... | collective-permute-start | bytes 393224 | tf_op jit(solution)/shard_map/ppermute | solution.py:492
  28.5 12.8 %collective-permute-done.refs_1_ = f32[16,16,128]{2,1,0:T(8,128)S(1)} collective-permute-done((f32[16,16,128]{2,1,0:T(8,128)S(1)}, f32[16,16,128]{2,1,0:T(8,128)S(1)}, u32[]{:S(2)}, u32[]{:S(2)}) %collective-permute-start) | collective-permute-done | bytes 131104 | tf_op jit(solution)/shard_map/ppermute | solution.py:491
  41.3 2.3 %collective-permute-done.1.refs_2_ = f32[16,16,128]{2,1,0:T(8,128)S(1)} collective-permute-done((f32[16,16,128]{2,1,0:T(8,128)S(1)}, f32[16,16,128]{2,1,0:T(8,128)S(1)}, u32[]{:S(2)}, u32[]{:S(2)}) %collective-permute-start.1) | collective-permute-done | bytes 131104 | tf_op jit(solution)/shard_map/ppermute | solution.py:492
  43.6 0.0 collective-permute-done.6.refs_3_
  43.6 2.4 %shard_map.61.refs_0_ = f32[64,2,40,128]{3,2,1,0:T(8,128)S(1)} custom-call(f32[16,16,128]{2,1,0:T(8,128)S(1)} %bitcast.8, f32[16,16,128]{2,1,0:T(8,128)S(1)} %collective-permute-done.refs_1_, f32[16,16,128]{2,1,0:T(8,128)S(1)} %collective-permute-done.1.refs_2_, f32[16,64,128]{2,1,0:T(8,128)S(1)} %collective-permute-done.6.refs_3_), custom_call_target="tpu_custom_call" | custom-call | tf_op jit(solution)/shard_map/pallas_call | solution.py:154
  46.1 0.0 copy-start
  46.1 0.0 collective-permute-done.7.refs_1_
  46.1 0.0 collective-permute-done.8.refs_2_
  46.1 7.0 %shard_map.62 = (f32[4,136,128]{2,1,0:T(8,128)S(1)}, f32[4,136,128]{2,1,0:T(8,128)S(1)}) custom-call(f32[64,2,40,128]{3,2,1,0:T(8,128)S(1)} %shard_map.61.refs_0_, f32[16,64,128]{2,1,0:T(8,128)S(1)} %collective-permute-done.7.refs_1_, f32[16,64,128]{2,1,0:T(8,128)S(1)} %collective-permute-done.8.refs_2_), custom_call_target="tpu_custom_call" | custom-call | tf_op jit(solution)/shard_map/pallas_call | solution.py:419
  53.1 2.2 %all-gather = f32[8,136,128]{2,1,0:T(8,128)S(1)} all-gather(f32[4,136,128]{2,1,0:T(8,128)S(1)} %get-tuple-element.8), channel_id=2, replica_groups=mesh['gx_0'=4,'gx_1'=2,'gy'=16,'gz'=8] {'gx_1'}, dimensions={0}, use_global_device_ids=true | all-gather | bytes 835584 | tf_op jit(solution)/shard_map/all_gather | solution.py:499
  55.4 10.6 %all_to_all.16.fields = f32[4,136,128]{2,1,0:T(8,128)S(1)} all-to-all(f32[4,136,128]{2,1,0:T(8,128)S(1)} %slice_select_fusion), channel_id=1, replica_groups=mesh['gx_0'=4,'gx_1'=2,'gy'=16,'gz'=8] {'gx_0'}, dimensions={0} | all-to-all | bytes 557056 | tf_op jit(solution)/shard_map/all_to_all | solution.py:501
  66.0 36.7 %all_to_all.17 = f32[128,1,128]{2,1,0:T(1,128)S(1)} all-to-all(f32[128,1,128]{2,1,0:T(1,128)S(1)} %broadcast_in_dim.3), channel_id=1, replica_groups=mesh['gx_0'=4,'gx_1'=2,'gy'=16,'gz'=8] {'gy','gz'}, dimensions={0} | all-to-all | bytes 131072 | tf_op jit(solution)/shard_map/all_to_all | solution.py:503
  102.7 0.0 copy-done
  102.7 0.9 shard_map.63
  (4 shorter events, 0.1 us)
Async XLA Ops:
  12.7 8.0 %collective-permute-start.2 = (f32[16,16,128]{2,1,0:T(8,128)S(1)}, f32[16,16,128]{2,1,0:T(8,128)S(1)}, u32[]{:S(2)}, u32[]{:S(2)}) collective-permute-start(f32[16,16,128]{2,1,0:T(8,128)S(1)} %bitcast.2), channel_id=1, source_target_pairs={{0,144},{8,152},{16,160},{24,168},{32,176},{40,184},{48,192},{56,2... | collective-permute-start | bytes 393224 | tf_op jit(solution)/shard_map/ppermute | solution.py:490
  18.1 3.9 %collective-permute-start.3 = (f32[16,16,128]{2,1,0:T(8,128)S(1)}, f32[16,16,128]{2,1,0:T(8,128)S(1)}, u32[]{:S(2)}, u32[]{:S(2)}) collective-permute-start(f32[16,16,128]{2,1,0:T(8,128)S(1)} %bitcast.3), channel_id=1, source_target_pairs={{0,136},{8,144},{16,152},{24,160},{32,168},{40,176},{48,184},{56,1... | collective-permute-start | bytes 393224 | tf_op jit(solution)/shard_map/ppermute | solution.py:490
  19.4 2.6 %collective-permute-start.4 = (f32[16,16,128]{2,1,0:T(8,128)S(1)}, f32[16,16,128]{2,1,0:T(8,128)S(1)}, u32[]{:S(2)}, u32[]{:S(2)}) collective-permute-start(f32[16,16,128]{2,1,0:T(8,128)S(1)} %bitcast.4), channel_id=1, source_target_pairs={{8,128},{16,136},{24,144},{32,152},{40,160},{48,168},{56,176},{64,... | collective-permute-start | bytes 393224 | tf_op jit(solution)/shard_map/ppermute | solution.py:490
  20.0 1.9 %collective-permute-start.5 = (f32[16,16,128]{2,1,0:T(8,128)S(1)}, f32[16,16,128]{2,1,0:T(8,128)S(1)}, u32[]{:S(2)}, u32[]{:S(2)}) collective-permute-start(f32[16,16,128]{2,1,0:T(8,128)S(1)} %bitcast.5), channel_id=1, source_target_pairs={{16,128},{24,136},{32,144},{40,152},{48,160},{56,168},{64,176},{72... | collective-permute-start | bytes 393224 | tf_op jit(solution)/shard_map/ppermute | solution.py:490
  22.0 21.7 %collective-permute-start.6 = (f32[16,64,128]{2,1,0:T(8,128)S(1)}, f32[16,64,128]{2,1,0:T(8,128)S(1)}, u32[]{:S(2)}, u32[]{:S(2)}) collective-permute-start(f32[16,64,128]{2,1,0:T(8,128)S(1)} %shard_map.60), channel_id=1, source_target_pairs={{128,0},{129,1},{130,2},{131,3},{132,4},{133,5},{134,6},{135,7},{1... | collective-permute-start | bytes 1572872 | tf_op jit(solution)/shard_map/ppermute | solution.py:496
  23.3 22.8 %collective-permute-start.7 = (f32[16,64,128]{2,1,0:T(8,128)S(1)}, f32[16,64,128]{2,1,0:T(8,128)S(1)}, u32[]{:S(2)}, u32[]{:S(2)}) collective-permute-start(f32[16,64,128]{2,1,0:T(8,128)S(1)} %shard_map.60), channel_id=1, source_target_pairs={{128,256},{384,512},{640,768},{896,769},{897,513},{641,257},{385,1... | collective-permute-start | bytes 1572872 | tf_op jit(solution)/shard_map/ppermute | solution.py:494
  24.6 21.5 %collective-permute-start.8 = (f32[16,64,128]{2,1,0:T(8,128)S(1)}, f32[16,64,128]{2,1,0:T(8,128)S(1)}, u32[]{:S(2)}, u32[]{:S(2)}) collective-permute-start(f32[16,64,128]{2,1,0:T(8,128)S(1)} %shard_map.60), channel_id=1, source_target_pairs={{384,0},{640,256},{896,512},{897,768},{641,769},{385,513},{129,257... | collective-permute-start | bytes 1572872 | tf_op jit(solution)/shard_map/ppermute | solution.py:495
  25.9 15.4 %collective-permute-start = (f32[16,16,128]{2,1,0:T(8,128)S(1)}, f32[16,16,128]{2,1,0:T(8,128)S(1)}, u32[]{:S(2)}, u32[]{:S(2)}) collective-permute-start(f32[16,16,128]{2,1,0:T(8,128)S(1)} %bitcast.6), channel_id=1, source_target_pairs={{128,256},{384,512},{640,768},{896,769},{897,513},{641,257},{385,1... | collective-permute-start | bytes 393224 | tf_op jit(solution)/shard_map/ppermute | solution.py:491
  27.2 16.5 %collective-permute-start.1 = (f32[16,16,128]{2,1,0:T(8,128)S(1)}, f32[16,16,128]{2,1,0:T(8,128)S(1)}, u32[]{:S(2)}, u32[]{:S(2)}) collective-permute-start(f32[16,16,128]{2,1,0:T(8,128)S(1)} %bitcast.7), channel_id=1, source_target_pairs={{384,0},{640,256},{896,512},{897,768},{641,769},{385,513},{129,257... | collective-permute-start | bytes 393224 | tf_op jit(solution)/shard_map/ppermute | solution.py:492
  46.1 56.6 %copy-start = (f32[8,16,128]{2,1,0:T(8,128)S(1)}, f32[8,16,128]{2,1,0:T(8,128)}, u32[]{:S(2)}) copy-start(f32[8,16,128]{2,1,0:T(8,128)} %get-tuple-element.6.rhs) | copy-start | bytes 196612

commit v12 on v11

--- a/solution.py
+++ b/solution.py
@@ -307,6 +307,20 @@
     chunks(NX, ne, smooth0)
 
 
+def smooth_row(src, mask, v0, out, odd, row):
+    def layers(parity, at_row, x):
+        return pl.ds((2 * x + parity) * 56 + 8 + at_row, 8, stride=112)
+
+    source, before, target = (ref.reshape((NX + 2) * 112, LANES) for ref in (src, v0, out))
+    m = mask[8 + row : 9 + row]
+    for x in range(1, NX + 1, 8):
+        v = before[layers(odd, row, x), :]
+        y = before[layers(1 - odd, row + odd - 1, x), :] + before[layers(1 - odd, row + odd, x), :]
+        across = before[layers(odd, row, x - 1), :] + before[layers(odd, row, x + 1), :]
+        s = third(v) + relax * ((source[layers(odd, row, x), :] + across) + (y + sides(v, 1)))
+        target[layers(odd, row, x), :] = s * m
+
+
 def images(src, first, odd, r, count):
     layers = [src[first + k, odd, at(r)] for k in range(count + 2)]
     result = []
@@ -379,7 +393,9 @@
     chunks(NX, 64, image)
     cycle_down(q0, mask, mask2, fold, outer, v1, e1, f1, f2, middle, (5, 7), 8, 16)
     cycle_coarse(mask2, f2, t2, e2, (6,), (6,))
-    cycle_up(q0, mask, f1, e2, v1, e1, v0, w, (14, 18), (15, 17), ((15, 17), (15, 17)), ((16, 17), (15, 16)), 32, 64)
+    cycle_up(q0, mask, f1, e2, v1, e1, v0, w, (14, 18), (15, 17), ((15, 17), (15, 17)), ((16,), (16,)), 32, 64)
+    smooth_row(q0, mask, v0, w, 0, 24)
+    smooth_row(q0, mask, v0, w, 1, 15)
 
     def sums(i, acc):
         acc = list(acc)

time: 104 us -> 104 us (level)
  no operation moved by 1% of the time
where the time goes in v12:
time: 104 us; the launch traced here: 103 us
  blocking collectives  59.9 us (58%)
  waiting for transfers between devices  16.4 us (16%)
  starting transfers between devices  14.4 us (14%)
  Pallas kernels  11.9 us (11%)
    all_to_all x1, blocking collectives, local(): lax.all_to_all(jnp.broadcast_to(sums, (128, 1, 128)), ('gy', 'gz'), 0, 0,...  36.7 us
    ppermute x1, waiting for transfers between devices, local(): left = lax.ppermute(own, Z_AXES, z_pairs(1))  12.8 us
    all_to_all x1, blocking collectives, local(): fields = lax.all_to_all(packed, 'gx_0', 0, 0, tiled=True)  10.6 us
    all_to_all x1, blocking collectives, local(): own = lax.all_to_all(packed, GX, 0, 0, tiled=True).reshape(16, BY, 128)  10.4 us
    ppermute x4, starting transfers between devices, local(): moved.append(lax.ppermute(own, ('gx_1', 'gy'), y_pairs(step)))  7.97 us
    pallas_call x1, Pallas kernels, cycles(): pl.pallas_call(cycles_kernel, out_shape=(jax.ShapeDtypeStruct((4, BX * BY...  6.86 us
    pallas_call x1, Pallas kernels, unpack(): pl.pallas_call(unpack_kernel, out_shape=jax.ShapeDtypeStruct((NX, 2, 40,...  2.43 us
    ppermute x1, waiting for transfers between devices, local(): right = lax.ppermute(own, Z_AXES, z_pairs(-1))  2.34 us
  transfers between devices with their start and end apart: 9, of which 3 were waited for; matrix products, arithmetic and copies ran while one was open for 0% of the time, Pallas kernels for 2%

profile of v12, /device:TPU:8, one launch (start us, length us, event | category | flops | bytes accessed | tf_op | source)
XLA Modules:
  0.0 103.5 jit_solution(12209559642144066857)
XLA Ops:
  0.6 1.7 %shard_map.59 = (f32[8,16,128]{2,1,0:T(8,128)}, f32[8,2,16,128]{3,2,1,0:T(8,128)}) custom-call(f32[8,16,128]{2,1,0:T(8,128)} %density_in.1, f32[2,16,128]{2,1,0:T(8,128)} %xf_in.1, f32[2,8,128]{2,1,0:T(8,128)} %yf_in.1, f32[2,8,16]{2,1,0:T(8,128)} %zf_in.1), custom_call_target="tpu_custom_call" | custom-call | tf_op jit(solution)/shard_map/pallas_call | solution.py:98
  2.3 10.4 %all_to_all.15 = f32[8,2,16,128]{3,2,1,0:T(8,128)S(1)} all-to-all(f32[8,2,16,128]{3,2,1,0:T(8,128)} %get-tuple-element.7), channel_id=1, replica_groups=mesh['gx_0'=4,'gx_1'=2,'gy'=16,'gz'=8] {'gx_0','gx_1'}, dimensions={0} | all-to-all | bytes 262144 | tf_op jit(solution)/shard_map/all_to_all | solution.py:503
  12.7 5.3 %collective-permute-start.2 = (f32[16,16,128]{2,1,0:T(8,128)S(1)}, f32[16,16,128]{2,1,0:T(8,128)S(1)}, u32[]{:S(2)}, u32[]{:S(2)}) collective-permute-start(f32[16,16,128]{2,1,0:T(8,128)S(1)} %bitcast.2), channel_id=1, source_target_pairs={{0,144},{8,152},{16,160},{24,168},{32,176},{40,184},{48,192},{56,2... | collective-permute-start | bytes 393224 | tf_op jit(solution)/shard_map/ppermute | solution.py:506
  18.1 1.3 %collective-permute-start.3 = (f32[16,16,128]{2,1,0:T(8,128)S(1)}, f32[16,16,128]{2,1,0:T(8,128)S(1)}, u32[]{:S(2)}, u32[]{:S(2)}) collective-permute-start(f32[16,16,128]{2,1,0:T(8,128)S(1)} %bitcast.3), channel_id=1, source_target_pairs={{0,136},{8,144},{16,152},{24,160},{32,168},{40,176},{48,184},{56,1... | collective-permute-start | bytes 393224 | tf_op jit(solution)/shard_map/ppermute | solution.py:506
  19.4 0.7 collective-permute-start.4
  20.0 0.7 collective-permute-start.5
  20.7 0.0 collective-permute-done.2.refs_0_
  20.7 1.2 %collective-permute-done.3.refs_1_ = f32[16,16,128]{2,1,0:T(8,128)S(1)} collective-permute-done((f32[16,16,128]{2,1,0:T(8,128)S(1)}, f32[16,16,128]{2,1,0:T(8,128)S(1)}, u32[]{:S(2)}, u32[]{:S(2)}) %collective-permute-start.3) | collective-permute-done | bytes 131104 | tf_op jit(solution)/shard_map/ppermute | solution.py:506
  21.9 0.0 collective-permute-done.4.refs_2_
  21.9 0.0 collective-permute-done.5.refs_3_
  22.0 1.3 %collective-permute-start.6 = (f32[16,64,128]{2,1,0:T(8,128)S(1)}, f32[16,64,128]{2,1,0:T(8,128)S(1)}, u32[]{:S(2)}, u32[]{:S(2)}) collective-permute-start(f32[16,64,128]{2,1,0:T(8,128)S(1)} %shard_map.60), channel_id=1, source_target_pairs={{128,0},{129,1},{130,2},{131,3},{132,4},{133,5},{134,6},{135,7},{1... | collective-permute-start | bytes 1572872 | tf_op jit(solution)/shard_map/ppermute | solution.py:512
  23.3 1.3 %collective-permute-start.7 = (f32[16,64,128]{2,1,0:T(8,128)S(1)}, f32[16,64,128]{2,1,0:T(8,128)S(1)}, u32[]{:S(2)}, u32[]{:S(2)}) collective-permute-start(f32[16,64,128]{2,1,0:T(8,128)S(1)} %shard_map.60), channel_id=1, source_target_pairs={{128,256},{384,512},{640,768},{896,769},{897,513},{641,257},{385,1... | collective-permute-start | bytes 1572872 | tf_op jit(solution)/shard_map/ppermute | solution.py:510
  24.6 1.3 %collective-permute-start.8 = (f32[16,64,128]{2,1,0:T(8,128)S(1)}, f32[16,64,128]{2,1,0:T(8,128)S(1)}, u32[]{:S(2)}, u32[]{:S(2)}) collective-permute-start(f32[16,64,128]{2,1,0:T(8,128)S(1)} %shard_map.60), channel_id=1, source_target_pairs={{384,0},{640,256},{896,512},{897,768},{641,769},{385,513},{129,257... | collective-permute-start | bytes 1572872 | tf_op jit(solution)/shard_map/ppermute | solution.py:511
  25.9 1.3 %collective-permute-start = (f32[16,16,128]{2,1,0:T(8,128)S(1)}, f32[16,16,128]{2,1,0:T(8,128)S(1)}, u32[]{:S(2)}, u32[]{:S(2)}) collective-permute-start(f32[16,16,128]{2,1,0:T(8,128)S(1)} %bitcast.6), channel_id=1, source_target_pairs={{128,256},{384,512},{640,768},{896,769},{897,513},{641,257},{385,1... | collective-permute-start | bytes 393224 | tf_op jit(solution)/shard_map/ppermute | solution.py:507
  27.2 1.3 %collective-permute-start.1 = (f32[16,16,128]{2,1,0:T(8,128)S(1)}, f32[16,16,128]{2,1,0:T(8,128)S(1)}, u32[]{:S(2)}, u32[]{:S(2)}) collective-permute-start(f32[16,16,128]{2,1,0:T(8,128)S(1)} %bitcast.7), channel_id=1, source_target_pairs={{384,0},{640,256},{896,512},{897,768},{641,769},{385,513},{129,257... | collective-permute-start | bytes 393224 | tf_op jit(solution)/shard_map/ppermute | solution.py:508
  28.5 12.8 %collective-permute-done.refs_1_ = f32[16,16,128]{2,1,0:T(8,128)S(1)} collective-permute-done((f32[16,16,128]{2,1,0:T(8,128)S(1)}, f32[16,16,128]{2,1,0:T(8,128)S(1)}, u32[]{:S(2)}, u32[]{:S(2)}) %collective-permute-start) | collective-permute-done | bytes 131104 | tf_op jit(solution)/shard_map/ppermute | solution.py:507
  41.3 2.3 %collective-permute-done.1.refs_2_ = f32[16,16,128]{2,1,0:T(8,128)S(1)} collective-permute-done((f32[16,16,128]{2,1,0:T(8,128)S(1)}, f32[16,16,128]{2,1,0:T(8,128)S(1)}, u32[]{:S(2)}, u32[]{:S(2)}) %collective-permute-start.1) | collective-permute-done | bytes 131104 | tf_op jit(solution)/shard_map/ppermute | solution.py:508
  43.6 0.0 collective-permute-done.6.refs_3_
  43.6 2.4 %shard_map.61.refs_0_ = f32[64,2,40,128]{3,2,1,0:T(8,128)S(1)} custom-call(f32[16,16,128]{2,1,0:T(8,128)S(1)} %bitcast.8, f32[16,16,128]{2,1,0:T(8,128)S(1)} %collective-permute-done.refs_1_, f32[16,16,128]{2,1,0:T(8,128)S(1)} %collective-permute-done.1.refs_2_, f32[16,64,128]{2,1,0:T(8,128)S(1)} %collective-permute-done.6.refs_3_), custom_call_target="tpu_custom_call" | custom-call | tf_op jit(solution)/shard_map/pallas_call | solution.py:154
  46.1 0.0 copy-start
  46.1 0.0 collective-permute-done.7.refs_1_
  46.1 0.0 collective-permute-done.8.refs_2_
  46.1 6.9 %shard_map.62 = (f32[4,136,128]{2,1,0:T(8,128)S(1)}, f32[4,136,128]{2,1,0:T(8,128)S(1)}) custom-call(f32[64,2,40,128]{3,2,1,0:T(8,128)S(1)} %shard_map.61.refs_0_, f32[16,64,128]{2,1,0:T(8,128)S(1)} %collective-permute-done.7.refs_1_, f32[16,64,128]{2,1,0:T(8,128)S(1)} %collective-permute-done.8.refs_2_), custom_call_target="tpu_custom_call" | custom-call | tf_op jit(solution)/shard_map/pallas_call | solution.py:435
  52.9 2.2 %all-gather = f32[8,136,128]{2,1,0:T(8,128)S(1)} all-gather(f32[4,136,128]{2,1,0:T(8,128)S(1)} %get-tuple-element.8), channel_id=2, replica_groups=mesh['gx_0'=4,'gx_1'=2,'gy'=16,'gz'=8] {'gx_1'}, dimensions={0}, use_global_device_ids=true | all-gather | bytes 835584 | tf_op jit(solution)/shard_map/all_gather | solution.py:515
  55.2 10.6 %all_to_all.16.fields = f32[4,136,128]{2,1,0:T(8,128)S(1)} all-to-all(f32[4,136,128]{2,1,0:T(8,128)S(1)} %slice_select_fusion), channel_id=1, replica_groups=mesh['gx_0'=4,'gx_1'=2,'gy'=16,'gz'=8] {'gx_0'}, dimensions={0} | all-to-all | bytes 557056 | tf_op jit(solution)/shard_map/all_to_all | solution.py:517
  65.9 36.7 %all_to_all.17 = f32[128,1,128]{2,1,0:T(1,128)S(1)} all-to-all(f32[128,1,128]{2,1,0:T(1,128)S(1)} %broadcast_in_dim.3), channel_id=1, replica_groups=mesh['gx_0'=4,'gx_1'=2,'gy'=16,'gz'=8] {'gy','gz'}, dimensions={0} | all-to-all | bytes 131072 | tf_op jit(solution)/shard_map/all_to_all | solution.py:519
  102.5 0.0 copy-done
  102.5 0.9 shard_map.63
  (4 shorter events, 0.1 us)
Async XLA Ops:
  12.7 8.0 %collective-permute-start.2 = (f32[16,16,128]{2,1,0:T(8,128)S(1)}, f32[16,16,128]{2,1,0:T(8,128)S(1)}, u32[]{:S(2)}, u32[]{:S(2)}) collective-permute-start(f32[16,16,128]{2,1,0:T(8,128)S(1)} %bitcast.2), channel_id=1, source_target_pairs={{0,144},{8,152},{16,160},{24,168},{32,176},{40,184},{48,192},{56,2... | collective-permute-start | bytes 393224 | tf_op jit(solution)/shard_map/ppermute | solution.py:506
  18.1 3.9 %collective-permute-start.3 = (f32[16,16,128]{2,1,0:T(8,128)S(1)}, f32[16,16,128]{2,1,0:T(8,128)S(1)}, u32[]{:S(2)}, u32[]{:S(2)}) collective-permute-start(f32[16,16,128]{2,1,0:T(8,128)S(1)} %bitcast.3), channel_id=1, source_target_pairs={{0,136},{8,144},{16,152},{24,160},{32,168},{40,176},{48,184},{56,1... | collective-permute-start | bytes 393224 | tf_op jit(solution)/shard_map/ppermute | solution.py:506
  19.4 2.6 %collective-permute-start.4 = (f32[16,16,128]{2,1,0:T(8,128)S(1)}, f32[16,16,128]{2,1,0:T(8,128)S(1)}, u32[]{:S(2)}, u32[]{:S(2)}) collective-permute-start(f32[16,16,128]{2,1,0:T(8,128)S(1)} %bitcast.4), channel_id=1, source_target_pairs={{8,128},{16,136},{24,144},{32,152},{40,160},{48,168},{56,176},{64,... | collective-permute-start | bytes 393224 | tf_op jit(solution)/shard_map/ppermute | solution.py:506
  20.0 1.9 %collective-permute-start.5 = (f32[16,16,128]{2,1,0:T(8,128)S(1)}, f32[16,16,128]{2,1,0:T(8,128)S(1)}, u32[]{:S(2)}, u32[]{:S(2)}) collective-permute-start(f32[16,16,128]{2,1,0:T(8,128)S(1)} %bitcast.5), channel_id=1, source_target_pairs={{16,128},{24,136},{32,144},{40,152},{48,160},{56,168},{64,176},{72... | collective-permute-start | bytes 393224 | tf_op jit(solution)/shard_map/ppermute | solution.py:506
  22.0 21.7 %collective-permute-start.6 = (f32[16,64,128]{2,1,0:T(8,128)S(1)}, f32[16,64,128]{2,1,0:T(8,128)S(1)}, u32[]{:S(2)}, u32[]{:S(2)}) collective-permute-start(f32[16,64,128]{2,1,0:T(8,128)S(1)} %shard_map.60), channel_id=1, source_target_pairs={{128,0},{129,1},{130,2},{131,3},{132,4},{133,5},{134,6},{135,7},{1... | collective-permute-start | bytes 1572872 | tf_op jit(solution)/shard_map/ppermute | solution.py:512
  23.3 22.8 %collective-permute-start.7 = (f32[16,64,128]{2,1,0:T(8,128)S(1)}, f32[16,64,128]{2,1,0:T(8,128)S(1)}, u32[]{:S(2)}, u32[]{:S(2)}) collective-permute-start(f32[16,64,128]{2,1,0:T(8,128)S(1)} %shard_map.60), channel_id=1, source_target_pairs={{128,256},{384,512},{640,768},{896,769},{897,513},{641,257},{385,1... | collective-permute-start | bytes 1572872 | tf_op jit(solution)/shard_map/ppermute | solution.py:510
  24.6 21.5 %collective-permute-start.8 = (f32[16,64,128]{2,1,0:T(8,128)S(1)}, f32[16,64,128]{2,1,0:T(8,128)S(1)}, u32[]{:S(2)}, u32[]{:S(2)}) collective-permute-start(f32[16,64,128]{2,1,0:T(8,128)S(1)} %shard_map.60), channel_id=1, source_target_pairs={{384,0},{640,256},{896,512},{897,768},{641,769},{385,513},{129,257... | collective-permute-start | bytes 1572872 | tf_op jit(solution)/shard_map/ppermute | solution.py:511
  25.9 15.4 %collective-permute-start = (f32[16,16,128]{2,1,0:T(8,128)S(1)}, f32[16,16,128]{2,1,0:T(8,128)S(1)}, u32[]{:S(2)}, u32[]{:S(2)}) collective-permute-start(f32[16,16,128]{2,1,0:T(8,128)S(1)} %bitcast.6), channel_id=1, source_target_pairs={{128,256},{384,512},{640,768},{896,769},{897,513},{641,257},{385,1... | collective-permute-start | bytes 393224 | tf_op jit(solution)/shard_map/ppermute | solution.py:507
  27.2 16.5 %collective-permute-start.1 = (f32[16,16,128]{2,1,0:T(8,128)S(1)}, f32[16,16,128]{2,1,0:T(8,128)S(1)}, u32[]{:S(2)}, u32[]{:S(2)}) collective-permute-start(f32[16,16,128]{2,1,0:T(8,128)S(1)} %bitcast.7), channel_id=1, source_target_pairs={{384,0},{640,256},{896,512},{897,768},{641,769},{385,513},{129,257... | collective-permute-start | bytes 393224 | tf_op jit(solution)/shard_map/ppermute | solution.py:508
  46.1 56.5 %copy-start = (f32[8,16,128]{2,1,0:T(8,128)S(1)}, f32[8,16,128]{2,1,0:T(8,128)}, u32[]{:S(2)}) copy-start(f32[8,16,128]{2,1,0:T(8,128)} %get-tuple-element.6.rhs) | copy-start | bytes 196612

commit v13 on v12

--- a/solution.py
+++ b/solution.py
@@ -280,6 +280,14 @@
                 e1[x, at(r)] = s * m
 
     chunks(NX // 2, nd, smooth1)
+    right, before, target = (ref.reshape((NX // 2 + 2) * 56, LANES) for ref in (f1, v1, e1))
+    for row in (last1[-1] + 8, last1[-1] + 9):
+        for x in range(1, NX // 2 + 1, 8):
+            here, under, over, prior, later = (pl.ds((x + i) * 56 + 8 + row + j, 8, stride=56) for i, j in ((0, 0), (0, -1), (0, 1), (-1, 0), (1, 0)))
+            v = before[here, :]
+            y = before[under, :] + before[over, :]
+            s = third(v) + relax * ((right[here, :] + (before[prior, :] + before[later, :])) + (y + sides(v, 2)))
+            target[here, :] = s * mask[8 + row : 9 + row]
 
     def correct0(first):
         for odd in range(2):
@@ -381,7 +389,7 @@
     middle = (8, 16, 24)
     cycle_down(r0, mask, mask2, fold, outer, v1, e1, f1, f2, (0, 8, 16, 24, 32), (0, 8, 12), 8, 8)
     cycle_coarse(mask2, f2, t2, e2, (0, 8, 12), (1, 9))
-    cycle_up(r0, mask, f1, e2, v1, e1, v0, z0, (6, 14, 22, 26), (7, 15, 23, 25), ((8, 16, 24, 25), (7, 15, 23, 24)), (middle, middle), 32, 64)
+    cycle_up(r0, mask, f1, e2, v1, e1, v0, z0, (6, 14, 22, 26), (7, 15, 23), ((8, 16, 24, 25), (7, 15, 23, 24)), (middle, middle), 32, 64)
 
     def image(first):
         for odd in range(2):
@@ -393,7 +401,7 @@
     chunks(NX, 64, image)
     cycle_down(q0, mask, mask2, fold, outer, v1, e1, f1, f2, middle, (5, 7), 8, 16)
     cycle_coarse(mask2, f2, t2, e2, (6,), (6,))
-    cycle_up(q0, mask, f1, e2, v1, e1, v0, w, (14, 18), (15, 17), ((15, 17), (15, 17)), ((16,), (16,)), 32, 64)
+    cycle_up(q0, mask, f1, e2, v1, e1, v0, w, (14, 18), (15,), ((15, 17), (15, 17)), ((16,), (16,)), 32, 64)
     smooth_row(q0, mask, v0, w, 0, 24)
     smooth_row(q0, mask, v0, w, 1, 15)
 

time: 104 us -> 104 us (level)
  no operation moved by 1% of the time
where the time goes in v13:
time: 104 us; the launch traced here: 103 us
  blocking collectives  59.9 us (58%)
  waiting for transfers between devices  16.4 us (16%)
  starting transfers between devices  14.4 us (14%)
  Pallas kernels  11.9 us (11%)
    all_to_all x1, blocking collectives, local(): lax.all_to_all(jnp.broadcast_to(sums, (128, 1, 128)), ('gy', 'gz'), 0, 0,...  36.7 us
    ppermute x1, waiting for transfers between devices, local(): left = lax.ppermute(own, Z_AXES, z_pairs(1))  12.8 us
    all_to_all x1, blocking collectives, local(): fields = lax.all_to_all(packed, 'gx_0', 0, 0, tiled=True)  10.6 us
    all_to_all x1, blocking collectives, local(): own = lax.all_to_all(packed, GX, 0, 0, tiled=True).reshape(16, BY, 128)  10.4 us
    ppermute x4, starting transfers between devices, local(): moved.append(lax.ppermute(own, ('gx_1', 'gy'), y_pairs(step)))  7.97 us
    pallas_call x1, Pallas kernels, cycles(): pl.pallas_call(cycles_kernel, out_shape=(jax.ShapeDtypeStruct((4, BX * BY...  6.81 us
    pallas_call x1, Pallas kernels, unpack(): pl.pallas_call(unpack_kernel, out_shape=jax.ShapeDtypeStruct((NX, 2, 40,...  2.43 us
    ppermute x1, waiting for transfers between devices, local(): right = lax.ppermute(own, Z_AXES, z_pairs(-1))  2.34 us
  transfers between devices with their start and end apart: 9, of which 3 were waited for; matrix products, arithmetic and copies ran while one was open for 0% of the time, Pallas kernels for 2%

profile of v13, /device:TPU:8, one launch (start us, length us, event | category | flops | bytes accessed | tf_op | source)
XLA Modules:
  0.0 103.4 jit_solution(17238543562216813723)
XLA Ops:
  0.6 1.7 %shard_map.59 = (f32[8,16,128]{2,1,0:T(8,128)}, f32[8,2,16,128]{3,2,1,0:T(8,128)}) custom-call(f32[8,16,128]{2,1,0:T(8,128)} %density_in.1, f32[2,16,128]{2,1,0:T(8,128)} %xf_in.1, f32[2,8,128]{2,1,0:T(8,128)} %yf_in.1, f32[2,8,16]{2,1,0:T(8,128)} %zf_in.1), custom_call_target="tpu_custom_call" | custom-call | tf_op jit(solution)/shard_map/pallas_call | solution.py:98
  2.3 10.4 %all_to_all.15 = f32[8,2,16,128]{3,2,1,0:T(8,128)S(1)} all-to-all(f32[8,2,16,128]{3,2,1,0:T(8,128)} %get-tuple-element.7), channel_id=1, replica_groups=mesh['gx_0'=4,'gx_1'=2,'gy'=16,'gz'=8] {'gx_0','gx_1'}, dimensions={0} | all-to-all | bytes 262144 | tf_op jit(solution)/shard_map/all_to_all | solution.py:511
  12.7 5.3 %collective-permute-start.2 = (f32[16,16,128]{2,1,0:T(8,128)S(1)}, f32[16,16,128]{2,1,0:T(8,128)S(1)}, u32[]{:S(2)}, u32[]{:S(2)}) collective-permute-start(f32[16,16,128]{2,1,0:T(8,128)S(1)} %bitcast.2), channel_id=1, source_target_pairs={{0,144},{8,152},{16,160},{24,168},{32,176},{40,184},{48,192},{56,2... | collective-permute-start | bytes 393224 | tf_op jit(solution)/shard_map/ppermute | solution.py:514
  18.1 1.3 %collective-permute-start.3 = (f32[16,16,128]{2,1,0:T(8,128)S(1)}, f32[16,16,128]{2,1,0:T(8,128)S(1)}, u32[]{:S(2)}, u32[]{:S(2)}) collective-permute-start(f32[16,16,128]{2,1,0:T(8,128)S(1)} %bitcast.3), channel_id=1, source_target_pairs={{0,136},{8,144},{16,152},{24,160},{32,168},{40,176},{48,184},{56,1... | collective-permute-start | bytes 393224 | tf_op jit(solution)/shard_map/ppermute | solution.py:514
  19.4 0.7 collective-permute-start.4
  20.0 0.7 collective-permute-start.5
  20.7 0.0 collective-permute-done.2.refs_0_
  20.7 1.2 %collective-permute-done.3.refs_1_ = f32[16,16,128]{2,1,0:T(8,128)S(1)} collective-permute-done((f32[16,16,128]{2,1,0:T(8,128)S(1)}, f32[16,16,128]{2,1,0:T(8,128)S(1)}, u32[]{:S(2)}, u32[]{:S(2)}) %collective-permute-start.3) | collective-permute-done | bytes 131104 | tf_op jit(solution)/shard_map/ppermute | solution.py:514
  21.9 0.0 collective-permute-done.4.refs_2_
  21.9 0.0 collective-permute-done.5.refs_3_
  22.0 1.3 %collective-permute-start.6 = (f32[16,64,128]{2,1,0:T(8,128)S(1)}, f32[16,64,128]{2,1,0:T(8,128)S(1)}, u32[]{:S(2)}, u32[]{:S(2)}) collective-permute-start(f32[16,64,128]{2,1,0:T(8,128)S(1)} %shard_map.60), channel_id=1, source_target_pairs={{128,0},{129,1},{130,2},{131,3},{132,4},{133,5},{134,6},{135,7},{1... | collective-permute-start | bytes 1572872 | tf_op jit(solution)/shard_map/ppermute | solution.py:520
  23.3 1.3 %collective-permute-start.7 = (f32[16,64,128]{2,1,0:T(8,128)S(1)}, f32[16,64,128]{2,1,0:T(8,128)S(1)}, u32[]{:S(2)}, u32[]{:S(2)}) collective-permute-start(f32[16,64,128]{2,1,0:T(8,128)S(1)} %shard_map.60), channel_id=1, source_target_pairs={{128,256},{384,512},{640,768},{896,769},{897,513},{641,257},{385,1... | collective-permute-start | bytes 1572872 | tf_op jit(solution)/shard_map/ppermute | solution.py:518
  24.6 1.3 %collective-permute-start.8 = (f32[16,64,128]{2,1,0:T(8,128)S(1)}, f32[16,64,128]{2,1,0:T(8,128)S(1)}, u32[]{:S(2)}, u32[]{:S(2)}) collective-permute-start(f32[16,64,128]{2,1,0:T(8,128)S(1)} %shard_map.60), channel_id=1, source_target_pairs={{384,0},{640,256},{896,512},{897,768},{641,769},{385,513},{129,257... | collective-permute-start | bytes 1572872 | tf_op jit(solution)/shard_map/ppermute | solution.py:519
  25.9 1.3 %collective-permute-start = (f32[16,16,128]{2,1,0:T(8,128)S(1)}, f32[16,16,128]{2,1,0:T(8,128)S(1)}, u32[]{:S(2)}, u32[]{:S(2)}) collective-permute-start(f32[16,16,128]{2,1,0:T(8,128)S(1)} %bitcast.6), channel_id=1, source_target_pairs={{128,256},{384,512},{640,768},{896,769},{897,513},{641,257},{385,1... | collective-permute-start | bytes 393224 | tf_op jit(solution)/shard_map/ppermute | solution.py:515
  27.2 1.3 %collective-permute-start.1 = (f32[16,16,128]{2,1,0:T(8,128)S(1)}, f32[16,16,128]{2,1,0:T(8,128)S(1)}, u32[]{:S(2)}, u32[]{:S(2)}) collective-permute-start(f32[16,16,128]{2,1,0:T(8,128)S(1)} %bitcast.7), channel_id=1, source_target_pairs={{384,0},{640,256},{896,512},{897,768},{641,769},{385,513},{129,257... | collective-permute-start | bytes 393224 | tf_op jit(solution)/shard_map/ppermute | solution.py:516
  28.5 12.8 %collective-permute-done.refs_1_ = f32[16,16,128]{2,1,0:T(8,128)S(1)} collective-permute-done((f32[16,16,128]{2,1,0:T(8,128)S(1)}, f32[16,16,128]{2,1,0:T(8,128)S(1)}, u32[]{:S(2)}, u32[]{:S(2)}) %collective-permute-start) | collective-permute-done | bytes 131104 | tf_op jit(solution)/shard_map/ppermute | solution.py:515
  41.3 2.3 %collective-permute-done.1.refs_2_ = f32[16,16,128]{2,1,0:T(8,128)S(1)} collective-permute-done((f32[16,16,128]{2,1,0:T(8,128)S(1)}, f32[16,16,128]{2,1,0:T(8,128)S(1)}, u32[]{:S(2)}, u32[]{:S(2)}) %collective-permute-start.1) | collective-permute-done | bytes 131104 | tf_op jit(solution)/shard_map/ppermute | solution.py:516
  43.6 0.0 collective-permute-done.6.refs_3_
  43.6 2.4 %shard_map.61.refs_0_ = f32[64,2,40,128]{3,2,1,0:T(8,128)S(1)} custom-call(f32[16,16,128]{2,1,0:T(8,128)S(1)} %bitcast.8, f32[16,16,128]{2,1,0:T(8,128)S(1)} %collective-permute-done.refs_1_, f32[16,16,128]{2,1,0:T(8,128)S(1)} %collective-permute-done.1.refs_2_, f32[16,64,128]{2,1,0:T(8,128)S(1)} %collective-permute-done.6.refs_3_), custom_call_target="tpu_custom_call" | custom-call | tf_op jit(solution)/shard_map/pallas_call | solution.py:154
  46.1 0.0 copy-start
  46.1 0.0 collective-permute-done.7.refs_1_
  46.1 0.0 collective-permute-done.8.refs_2_
  46.1 6.8 %shard_map.62 = (f32[4,136,128]{2,1,0:T(8,128)S(1)}, f32[4,136,128]{2,1,0:T(8,128)S(1)}) custom-call(f32[64,2,40,128]{3,2,1,0:T(8,128)S(1)} %shard_map.61.refs_0_, f32[16,64,128]{2,1,0:T(8,128)S(1)} %collective-permute-done.7.refs_1_, f32[16,64,128]{2,1,0:T(8,128)S(1)} %collective-permute-done.8.refs_2_), custom_call_target="tpu_custom_call" | custom-call | tf_op jit(solution)/shard_map/pallas_call | solution.py:443
  52.9 2.2 %all-gather = f32[8,136,128]{2,1,0:T(8,128)S(1)} all-gather(f32[4,136,128]{2,1,0:T(8,128)S(1)} %get-tuple-element.8), channel_id=2, replica_groups=mesh['gx_0'=4,'gx_1'=2,'gy'=16,'gz'=8] {'gx_1'}, dimensions={0}, use_global_device_ids=true | all-gather | bytes 835584 | tf_op jit(solution)/shard_map/all_gather | solution.py:523
  55.1 10.6 %all_to_all.16.fields = f32[4,136,128]{2,1,0:T(8,128)S(1)} all-to-all(f32[4,136,128]{2,1,0:T(8,128)S(1)} %slice_select_fusion), channel_id=1, replica_groups=mesh['gx_0'=4,'gx_1'=2,'gy'=16,'gz'=8] {'gx_0'}, dimensions={0} | all-to-all | bytes 557056 | tf_op jit(solution)/shard_map/all_to_all | solution.py:525
  65.8 36.7 %all_to_all.17 = f32[128,1,128]{2,1,0:T(1,128)S(1)} all-to-all(f32[128,1,128]{2,1,0:T(1,128)S(1)} %broadcast_in_dim.3), channel_id=1, replica_groups=mesh['gx_0'=4,'gx_1'=2,'gy'=16,'gz'=8] {'gy','gz'}, dimensions={0} | all-to-all | bytes 131072 | tf_op jit(solution)/shard_map/all_to_all | solution.py:527
  102.5 0.0 copy-done
  102.5 0.9 shard_map.63
  (4 shorter events, 0.1 us)
Async XLA Ops:
  12.7 8.0 %collective-permute-start.2 = (f32[16,16,128]{2,1,0:T(8,128)S(1)}, f32[16,16,128]{2,1,0:T(8,128)S(1)}, u32[]{:S(2)}, u32[]{:S(2)}) collective-permute-start(f32[16,16,128]{2,1,0:T(8,128)S(1)} %bitcast.2), channel_id=1, source_target_pairs={{0,144},{8,152},{16,160},{24,168},{32,176},{40,184},{48,192},{56,2... | collective-permute-start | bytes 393224 | tf_op jit(solution)/shard_map/ppermute | solution.py:514
  18.1 3.9 %collective-permute-start.3 = (f32[16,16,128]{2,1,0:T(8,128)S(1)}, f32[16,16,128]{2,1,0:T(8,128)S(1)}, u32[]{:S(2)}, u32[]{:S(2)}) collective-permute-start(f32[16,16,128]{2,1,0:T(8,128)S(1)} %bitcast.3), channel_id=1, source_target_pairs={{0,136},{8,144},{16,152},{24,160},{32,168},{40,176},{48,184},{56,1... | collective-permute-start | bytes 393224 | tf_op jit(solution)/shard_map/ppermute | solution.py:514
  19.4 2.6 %collective-permute-start.4 = (f32[16,16,128]{2,1,0:T(8,128)S(1)}, f32[16,16,128]{2,1,0:T(8,128)S(1)}, u32[]{:S(2)}, u32[]{:S(2)}) collective-permute-start(f32[16,16,128]{2,1,0:T(8,128)S(1)} %bitcast.4), channel_id=1, source_target_pairs={{8,128},{16,136},{24,144},{32,152},{40,160},{48,168},{56,176},{64,... | collective-permute-start | bytes 393224 | tf_op jit(solution)/shard_map/ppermute | solution.py:514
  20.0 1.9 %collective-permute-start.5 = (f32[16,16,128]{2,1,0:T(8,128)S(1)}, f32[16,16,128]{2,1,0:T(8,128)S(1)}, u32[]{:S(2)}, u32[]{:S(2)}) collective-permute-start(f32[16,16,128]{2,1,0:T(8,128)S(1)} %bitcast.5), channel_id=1, source_target_pairs={{16,128},{24,136},{32,144},{40,152},{48,160},{56,168},{64,176},{72... | collective-permute-start | bytes 393224 | tf_op jit(solution)/shard_map/ppermute | solution.py:514
  22.0 21.7 %collective-permute-start.6 = (f32[16,64,128]{2,1,0:T(8,128)S(1)}, f32[16,64,128]{2,1,0:T(8,128)S(1)}, u32[]{:S(2)}, u32[]{:S(2)}) collective-permute-start(f32[16,64,128]{2,1,0:T(8,128)S(1)} %shard_map.60), channel_id=1, source_target_pairs={{128,0},{129,1},{130,2},{131,3},{132,4},{133,5},{134,6},{135,7},{1... | collective-permute-start | bytes 1572872 | tf_op jit(solution)/shard_map/ppermute | solution.py:520
  23.3 22.8 %collective-permute-start.7 = (f32[16,64,128]{2,1,0:T(8,128)S(1)}, f32[16,64,128]{2,1,0:T(8,128)S(1)}, u32[]{:S(2)}, u32[]{:S(2)}) collective-permute-start(f32[16,64,128]{2,1,0:T(8,128)S(1)} %shard_map.60), channel_id=1, source_target_pairs={{128,256},{384,512},{640,768},{896,769},{897,513},{641,257},{385,1... | collective-permute-start | bytes 1572872 | tf_op jit(solution)/shard_map/ppermute | solution.py:518
  24.6 21.5 %collective-permute-start.8 = (f32[16,64,128]{2,1,0:T(8,128)S(1)}, f32[16,64,128]{2,1,0:T(8,128)S(1)}, u32[]{:S(2)}, u32[]{:S(2)}) collective-permute-start(f32[16,64,128]{2,1,0:T(8,128)S(1)} %shard_map.60), channel_id=1, source_target_pairs={{384,0},{640,256},{896,512},{897,768},{641,769},{385,513},{129,257... | collective-permute-start | bytes 1572872 | tf_op jit(solution)/shard_map/ppermute | solution.py:519
  25.9 15.4 %collective-permute-start = (f32[16,16,128]{2,1,0:T(8,128)S(1)}, f32[16,16,128]{2,1,0:T(8,128)S(1)}, u32[]{:S(2)}, u32[]{:S(2)}) collective-permute-start(f32[16,16,128]{2,1,0:T(8,128)S(1)} %bitcast.6), channel_id=1, source_target_pairs={{128,256},{384,512},{640,768},{896,769},{897,513},{641,257},{385,1... | collective-permute-start | bytes 393224 | tf_op jit(solution)/shard_map/ppermute | solution.py:515
  27.2 16.5 %collective-permute-start.1 = (f32[16,16,128]{2,1,0:T(8,128)S(1)}, f32[16,16,128]{2,1,0:T(8,128)S(1)}, u32[]{:S(2)}, u32[]{:S(2)}) collective-permute-start(f32[16,16,128]{2,1,0:T(8,128)S(1)} %bitcast.7), channel_id=1, source_target_pairs={{384,0},{640,256},{896,512},{897,768},{641,769},{385,513},{129,257... | collective-permute-start | bytes 393224 | tf_op jit(solution)/shard_map/ppermute | solution.py:516
  46.1 56.4 %copy-start = (f32[8,16,128]{2,1,0:T(8,128)S(1)}, f32[8,16,128]{2,1,0:T(8,128)}, u32[]{:S(2)}) copy-start(f32[8,16,128]{2,1,0:T(8,128)} %get-tuple-element.6.rhs) | copy-start | bytes 196612
